TPU v7x, 16 devices: a whole 2x2x2 slice. The times are simulated.
16 devices in a mesh: sp: 16 (over z, y, x, core).
Axes of the slice: x: 2, y: 2, z: 2, core: 2. Of those that a mesh axis runs over, the one named last changes fastest.
Arguments:
- x: bfloat16 [8, 2048, 2048], P(None, 'sp')
- d_y: bfloat16 [8, 2048, 2048], P(None, 'sp')
- ln_gamma: bfloat16 [2048], replicated
- ln_beta: bfloat16 [2048], replicated
- w_qkv: bfloat16 [2048, 6144], replicated
- b_qkv: bfloat16 [6144], replicated
- w_out: bfloat16 [2048, 2048], replicated
- b_out: bfloat16 [2048], replicated
- head_kind: int32 [16], replicated
Outputs:
- output 1: bfloat16 [8, 2048, 2048], P(None, 'sp')
- output 2: bfloat16 [8, 2048, 2048], P(None, 'sp')
- output 3: float32 [2048], replicated
- output 4: float32 [2048], replicated
- output 5: float32 [2048, 6144], replicated
- output 6: float32 [6144], replicated
- output 7: float32 [2048, 2048], replicated
- output 8: float32 [2048], replicated
All inputs are finite; a program needn't handle non-finite values.
Results may differ from a plain program's by a relative error of at most 0.0127672.
Values are sent between devices in bfloat16 or wider.
A program may use at most 1 GiB of HBM per device.

v0:
```python
import math
import jax
import jax.numpy as jnp
from jax import lax
from jax.sharding import PartitionSpec as P

LN_EPS = 1e-5
NEG_BIG = -1e30


def layer_norm(x_rows, gamma_f, beta_f):
    row_mean = jnp.mean(x_rows, axis=-1, keepdims=True)
    centred = x_rows - row_mean
    row_var = jnp.mean(centred * centred, axis=-1, keepdims=True)
    return centred * lax.rsqrt(row_var + LN_EPS) * gamma_f + beta_f


def score_probs(q_part, k_all, banded, q_first, band_width):
    q_len = q_part.shape[2]
    k_len = k_all.shape[2]
    score_scale = 1.0 / math.sqrt(q_part.shape[3])
    logits = jnp.einsum("bhqd,bhkd->bhqk", q_part, k_all, preferred_element_type=jnp.float32) * score_scale
    query_pos = q_first + lax.broadcasted_iota(jnp.int32, (1, 1, q_len, 1), 2)
    key_pos = lax.broadcasted_iota(jnp.int32, (1, 1, 1, k_len), 3)
    is_banded = (banded == 1)[None, :, None, None]
    allowed = (key_pos <= query_pos) & (jnp.logical_not(is_banded) | (key_pos > query_pos - band_width))
    return jax.nn.softmax(jnp.where(allowed, logits, NEG_BIG), axis=-1)


def attend_forward(q_all, k_all, v_all, banded, q_offset, band_width):
    q_len = q_all.shape[2]
    q_blk = min(128, q_len)

    def q_step(blk_index, out_buf):
        q_start = blk_index * q_blk
        q_part = lax.dynamic_slice_in_dim(q_all, q_start, q_blk, axis=2)
        attn_prob = score_probs(q_part, k_all, banded, q_offset + q_start, band_width)
        o_part = jnp.einsum("bhqk,bhkd->bhqd", attn_prob.astype(jnp.bfloat16), v_all, preferred_element_type=jnp.float32)
        return lax.dynamic_update_slice_in_dim(out_buf, o_part.astype(jnp.bfloat16), q_start, axis=2)

    return lax.fori_loop(0, q_len // q_blk, q_step, jnp.zeros_like(q_all))


def attend_backward(q_all, k_all, v_all, d_out, banded, q_offset, band_width):
    q_len = q_all.shape[2]
    q_blk = min(128, q_len)
    score_scale = 1.0 / math.sqrt(q_all.shape[3])

    def q_step(blk_index, grad_state):
        dq_buf, dk_acc, dv_acc = grad_state
        q_start = blk_index * q_blk
        q_part = lax.dynamic_slice_in_dim(q_all, q_start, q_blk, axis=2)
        do_part = lax.dynamic_slice_in_dim(d_out, q_start, q_blk, axis=2)
        attn_prob = score_probs(q_part, k_all, banded, q_offset + q_start, band_width)
        prob_bf = attn_prob.astype(jnp.bfloat16)
        d_prob = jnp.einsum("bhqd,bhkd->bhqk", do_part, v_all, preferred_element_type=jnp.float32).astype(jnp.bfloat16).astype(jnp.float32)
        d_logit = (attn_prob * (d_prob - jnp.sum(attn_prob * d_prob, axis=-1, keepdims=True)) * score_scale).astype(jnp.bfloat16)
        dq_part = jnp.einsum("bhqk,bhkd->bhqd", d_logit, k_all, preferred_element_type=jnp.float32)
        dk_acc = dk_acc + jnp.einsum("bhqk,bhqd->bhkd", d_logit, q_part, preferred_element_type=jnp.float32)
        dv_acc = dv_acc + jnp.einsum("bhqk,bhqd->bhkd", prob_bf, do_part, preferred_element_type=jnp.float32)
        dq_buf = lax.dynamic_update_slice_in_dim(dq_buf, dq_part.astype(jnp.bfloat16), q_start, axis=2)
        return dq_buf, dk_acc, dv_acc

    init_state = (jnp.zeros_like(q_all), jnp.zeros(k_all.shape, jnp.float32), jnp.zeros(v_all.shape, jnp.float32))
    return lax.fori_loop(0, q_len // q_blk, q_step, init_state)


def solution(mesh):
    seq_par = mesh.shape["sp"]
    tok_spec = P(None, "sp", None)

    def local_block(x, d_y, ln_gamma, ln_beta, w_qkv, b_qkv, w_out, b_out, head_kind):
        local_len = x.shape[1]
        d_model = x.shape[2]
        num_heads = head_kind.shape[0]
        head_dim = d_model // num_heads
        local_heads = num_heads // seq_par
        band_width = local_len * seq_par // 4
        my_kinds = lax.dynamic_slice_in_dim(head_kind, lax.axis_index("sp") * local_heads, local_heads)
        wqkv_r = w_qkv.reshape(d_model, 3, num_heads, head_dim)
        wout_r = w_out.reshape(num_heads, head_dim, d_model)
        x_f = x.astype(jnp.float32)
        h_f, ln_pull = jax.vjp(layer_norm, x_f, ln_gamma.astype(jnp.float32), ln_beta.astype(jnp.float32))
        h_norm = h_f.astype(jnp.bfloat16)
        qkv_bias = b_qkv.astype(jnp.float32).reshape(3, 1, num_heads, 1, head_dim)
        qkv_tok = (jnp.einsum("bsi,itnd->tbnsd", h_norm, wqkv_r, preferred_element_type=jnp.float32) + qkv_bias).astype(jnp.bfloat16)
        qkv_head = lax.all_to_all(qkv_tok, "sp", 2, 3, tiled=True)
        attn_head = attend_forward(qkv_head[0], qkv_head[1], qkv_head[2], my_kinds, 0, band_width)
        attn_tok = lax.all_to_all(attn_head, "sp", 2, 1, tiled=True)
        proj_out = jnp.einsum("bnsd,ndj->bsj", attn_tok, wout_r, preferred_element_type=jnp.float32)
        y_out = (x_f + proj_out + b_out.astype(jnp.float32)).astype(jnp.bfloat16)
        d_attn_tok = jnp.einsum("bsj,ndj->bnsd", d_y, wout_r, preferred_element_type=jnp.float32).astype(jnp.bfloat16)
        d_attn_head = lax.all_to_all(d_attn_tok, "sp", 1, 2, tiled=True)
        dq_head, dk_head, dv_head = attend_backward(qkv_head[0], qkv_head[1], qkv_head[2], d_attn_head, my_kinds, 0, band_width)
        d_qkv_head = jnp.stack([dq_head, dk_head.astype(jnp.bfloat16), dv_head.astype(jnp.bfloat16)])
        d_qkv_tok = lax.all_to_all(d_qkv_head, "sp", 3, 2, tiled=True)
        d_wqkv = jnp.einsum("bsi,tbnsd->itnd", h_norm, d_qkv_tok, preferred_element_type=jnp.float32).reshape(d_model, 3 * d_model)
        d_bqkv = jnp.sum(d_qkv_tok, axis=(1, 3), dtype=jnp.float32).reshape(3 * d_model)
        d_h = jnp.einsum("tbnsd,itnd->bsi", d_qkv_tok, wqkv_r, preferred_element_type=jnp.float32).astype(jnp.bfloat16).astype(jnp.float32)
        d_x_ln, d_gamma, d_beta = ln_pull(d_h)
        d_x = (d_y.astype(jnp.float32) + d_x_ln).astype(jnp.bfloat16)
        d_wout = jnp.einsum("bnsd,bsj->ndj", attn_tok, d_y, preferred_element_type=jnp.float32).reshape(d_model, d_model)
        d_bout = jnp.sum(d_y, axis=(0, 1), dtype=jnp.float32)
        grad_sums = lax.psum((d_gamma, d_beta, d_wqkv, d_bqkv, d_wout, d_bout), "sp")
        return (y_out, d_x) + tuple(grad_sums)

    return jax.shard_map(local_block, mesh=mesh, in_specs=(tok_spec, tok_spec, P(), P(), P(), P(), P(), P(), P()), out_specs=(tok_spec, tok_spec, P(), P(), P(), P(), P(), P()), check_vma=False)
```

profile of v0, /device:TPU:0, one launch (start us, length us, event | category | flops | bytes accessed | tf_op | source)
XLA Modules:
  0.0 2369.7 jit_solution(13967633339987168165)
XLA Ops:
  32.5 23.0 copy.152
  55.5 32.4 %fusion.73 = bf16[3,8,16,128,128]{4,3,2,0,1:T(8,128)(2,1)} fusion(f32[3,16,128]{2,1,0:T(8,128)S(1)} %convert.1, bf16[2048,3,16,128]{3,2,1,0:T(8,128)(2,1)} %bitcast.154, bf16[8,128,2048]{2,1,0:T(8,128)(2,1)S(1)} %copy-done.2, f32[2048]{0:T(1024)S(1)} %convert_element_type.137, f32[2048]{0:T(1024)S(1)} %convert_element_type.136, f32[8,128]{1,0:T(8,128)S(1)} %fusion.102, ...), kind=kOutput, calls=%fused_computation.86 | convolution fusion | flops 25794969600 | bytes 41992192 | tf_op jit(solution)/shard_map/bsi,itnd->tbnsd/dot_general | solution.py:86
  111.8 148.3 %all-to-all-done = bf16[3,8,16,128,128]{4,3,0,1,2:T(8,128)(2,1)} async-done(((bf16[3,8,16,128,128]{4,3,0,1,2:T(8,128)(2,1)}), bf16[3,8,16,128,128]{4,3,0,1,2:T(8,128)(2,1)}, u32[]{:S(2)}, u32[]{:S(2)}) %all-to-all-start) | async-done | bytes 12582944 | tf_op jit(solution)/shard_map/all_to_all | solution.py:87
  278.3 248.9 %while.35 = (s32[]{:T(128)}, bf16[8,1,2048,128]{3,0,1,2:T(8,128)(2,1)}, pred[1,1,1,1]{3,2,1,0:T(4,128)(4,1)}, bf16[8,1,2048,128]{3,2,0,1:T(8,128)(2,1)}, bf16[8,...) while((s32[]{:T(128)}, ...), condition=%wide.region_5.6_spmd, body=%wide.region_2.5_spmd.sunk | while | flops 1091700992 | bytes 60303548 | solution.py:41
  533.6 956.0 %while.36 = (s32[]{:T(128)}, bf16[8,1,2048,128]{3,0,2,1:T(8,128)(2,1)}, f32[8,1,2048,128]{3,2,0,1:T(8,128)}, f32[8,1,2048,128]{3,2,0,1:T(8,128)}, pred[1,1,1,1]{...) while((s32[]{:T(128)}, ...), condition=%wide.region_10.11_spmd.clone, body=%wide.region_6.10_spmd.clone.sunk | while | flops 2750554368 | bytes 140794096 | solution.py:65
  564.6 18.3 bitcast_add_fusion.4
  622.0 18.3 bitcast_add_fusion.4
  681.9 18.3 bitcast_add_fusion.4
  741.8 18.3 bitcast_add_fusion.4
  861.5 18.3 bitcast_add_fusion.4
  921.4 18.3 bitcast_add_fusion.4
  1041.1 18.3 bitcast_add_fusion.4
  1101.0 18.3 bitcast_add_fusion.4
  1160.8 18.3 bitcast_add_fusion.4
  1220.7 18.3 bitcast_add_fusion.4
  1280.6 18.3 bitcast_add_fusion.4
  1340.4 18.3 bitcast_add_fusion.4
  1400.3 18.3 bitcast_add_fusion.4
  1536.9 135.2 %all-to-all-done.3 = bf16[3,8,1,2048,128]{4,1,0,2,3:T(8,128)(2,1)} async-done(((bf16[3,8,1,2048,128]{4,1,0,2,3:T(8,128)(2,1)}), bf16[3,8,1,2048,128]{4,1,0,2,3:T(8,128)(2,1)}, u32[]{:S(2)}, u32[]{:S(2)}) %all-to-all-start.3) | async-done | bytes 12582944 | tf_op jit(solution)/shard_map/all_to_all | solution.py:96
  1689.3 36.8 %convolution_bitcast_fusion = f32[2048,6144]{1,0:T(8,128)} fusion(bf16[6144,8,128]{2,0,1:T(8,128)(2,1)} %bitcast.158, bf16[8,128,2048]{2,1,0:T(8,128)(2,1)} %param.13, f32[2048]{0:T(1024)S(1)} %copy-done.17, f32[2048]{0:T(1024)S(1)} %copy-done.8, f32[8,128]{1,0:T(8,128)S(1)} %copy-done.14, f32[8,128]{1,0:T(8,128)S(1)} %copy-done.10), kind=kOutput, calls=%fused_computation.78 | convolution fusion | flops 25782386688 | bytes 67133440 | tf_op jit(solution)/shard_map/bsi,tbnsd->itnd/dot_general | solution.py:97
  1765.7 35.1 %convert_reduce_fusion.1 = (f32[2048]{0:T(1024)S(1)}, f32[8,128]{1,0:T(8,128)S(1)}, bf16[8,128,2048]{2,1,0:T(8,128)(2,1)}) fusion(f32[2048]{0:T(1024)S(1)} %copy-done.8, f32[8,128]{1,0:T(8,128)S(1)} %copy-done.10, bf16[8,128,2048]{2,1,0:T(8,128)(2,1)S(1)} %copy-done.3, bf16[3,8,16,128,128]{4,3,2,1,0:T(8,128)(2,1)} %bitcast.157, ...), kind=kOutput, calls=%fused_computation.89 | convolution fusion | flops 25786576896 | bytes 46161920 | tf_op jit(solution)/shard_map/tbnsd,itnd->bsi/dot_general | solution.py:99
  1814.0 35.3 %all-reduce = (f32[2048]{0:T(1024)}, f32[2048]{0:T(1024)}, f32[6144]{0:T(1024)}, f32[2048]{0:T(1024)}) all-reduce(f32[2048]{0:T(1024)S(1)} %get-tuple-element.424, f32[2048]{0:T(1024)S(1)} %get-tuple-element.426, f32[6144]{0:T(1024)S(1)} %bitcast.163, f32[2048]{0:T(1024)S(1)} %get-tuple-element.475), channel_id=1, replica_groups=mesh['sp'=16] {'sp'}, use_global_device_ids=true, to_apply=%region_14.15 | all-reduce | flops 12288 | bytes 98304 | tf_op jit(solution)/shard_map/psum | solution.py:104
  1849.3 466.7 %all-reduce.4.cloned.1.call-done = (f32[2048,6144]{1,0:T(8,128)}, f32[2048,2048]{1,0:T(8,128)}) async-done(((f32[2048,6144]{1,0:T(8,128)}, f32[2048,2048]{1,0:T(8,128)}), (f32[2048,6144]{1,0:T(8,128)}, f32[2048,2048]{1,0:T(8,128)})) %all-reduce.4.cloned.1.call-update) | async-done | bytes 67108880 | tf_op jit(solution)/shard_map/psum | solution.py:104
  2316.0 34.5 %copy.199 = f32[2048,6144]{1,0:T(8,128)} copy(f32[2048,6144]{1,0:T(8,128)} %get-tuple-element.661) | data formatting | bytes 100663296
  (375 shorter events, 1167.2 us)
Async XLA Ops:
  20.5 11.9 copy-start.18
  20.5 11.9 copy-start.19
  20.5 11.9 copy-start.15
  20.5 79.3 %all-to-all-start.2 = ((bf16[8,16,128,128]{2,3,0,1:T(8,128)(2,1)}), bf16[8,16,128,128]{2,3,0,1:T(8,128)(2,1)}, u32[]{:S(2)}, u32[]{:S(2)}) async-start(bf16[8,16,128,128]{2,3,0,1:T(8,128)(2,1)} %convert_bitcast_fusion), calls=%async_computation.2 | async-start | bytes 8388608 | tf_op jit(solution)/shard_map/all_to_all | solution.py:93
  28.9 26.6 %copy-start.9 = (f32[8,128]{1,0:T(8,128)}, f32[8,128]{1,0:T(8,128)S(1)}, u32[]{:S(2)}) copy-start(f32[8,128]{1,0:T(8,128)S(1)} %broadcast_multiply_fusion) | copy-start | bytes 12292
  32.3 23.1 copy-start.11
  32.4 23.1 copy-start.13
  32.4 23.1 copy-start.7
  32.4 23.1 copy-start.16
  32.5 23.0 copy-start.2
  99.8 160.3 %all-to-all-start = ((bf16[3,8,16,128,128]{4,3,0,1,2:T(8,128)(2,1)}), bf16[3,8,16,128,128]{4,3,0,1,2:T(8,128)(2,1)}, u32[]{:S(2)}, u32[]{:S(2)}) async-start(bf16[3,8,16,128,128]{4,3,0,1,2:T(8,128)(2,1)} %copy.113), calls=%async_computation | async-start | bytes 25165824 | tf_op jit(solution)/shard_map/all_to_all | solution.py:87
  527.2 984.9 %all-to-all-start.1 = ((bf16[8,1,2048,128]{3,0,1,2:T(8,128)(2,1)}), bf16[8,1,2048,128]{3,0,1,2:T(8,128)(2,1)}, u32[]{:S(2)}, u32[]{:S(2)}) async-start(bf16[8,1,2048,128]{3,0,1,2:T(8,128)(2,1)} %get-tuple-element.390), calls=%async_computation.1 | async-start | bytes 8388608 | tf_op jit(solution)/shard_map/all_to_all | solution.py:89
  534.0 6.4 copy-start
  651.3 6.3 copy-start
  711.2 6.3 copy-start
  771.1 6.3 copy-start
  1489.6 16.6 copy-start.5
  1512.1 159.9 %all-to-all-start.3 = ((bf16[3,8,1,2048,128]{4,1,0,2,3:T(8,128)(2,1)}), bf16[3,8,1,2048,128]{4,1,0,2,3:T(8,128)(2,1)}, u32[]{:S(2)}, u32[]{:S(2)}) async-start(bf16[3,8,1,2048,128]{4,1,0,2,3:T(8,128)(2,1)} %pad_maximum_fusion), calls=%async_computation.3 | async-start | bytes 25165824 | tf_op jit(solution)/shard_map/all_to_all | solution.py:96
  1515.9 800.1 %all-reduce.4.cloned.1.call-start = ((), (), s32[]{:S(2)}) async-start(), calls=%async_computation.4 | async-start | bytes 134217728 | tf_op jit(solution)/shard_map/psum | solution.py:104
  1672.0 17.2 copy-start.8
  1672.0 17.2 copy-start.10
  1672.0 17.2 copy-start.14
  1672.0 17.2 copy-start.17
  1765.7 35.1 %copy-start.12 = (f32[8,128]{1,0:T(8,128)S(1)}, f32[8,128]{1,0:T(8,128)}, u32[]{:S(2)}) copy-start(f32[8,128]{1,0:T(8,128)} %copy-done.11) | copy-start | bytes 12292
  (33 other events, 189.7 us)
Sparse Core Ops, SparseCore 0:
  1726.2 589.7 all-reduce.3
where the time goes:
time: 2380 us; the launch traced here: 2370 us
  matrix products  1120 us (47%)
  waiting for transfers between devices  750 us (32%)
  other arithmetic  240 us (10%)
  local copies, waits for them, and re-layouts  193 us (8%)
  blocking collectives  35.3 us (1%)
    psum x1, waiting for transfers between devices, local_block(): lax.psum((d_gamma, d_beta, d_wqkv, d_bqkv, d_wout, d_bout), 'sp')  467 us
    dot_general x16, matrix products, q_step(): jnp.einsum('bhqk,bhqd->bhkd', d_logit, q_part, preferred_element_type=jnp...  293 us
    dot_general x16, matrix products, q_step(): jnp.einsum('bhqk,bhkd->bhqd', d_logit, k_all, preferred_element_type=jnp....  245 us
    sub x32, other arithmetic, score_probs(): return jax.nn.softmax(jnp.where(allowed, logits, NEG_BIG), axis=-1)  185 us
    dot_general x16, matrix products, q_step(): jnp.einsum('bhqk,bhqd->bhkd', prob_bf, do_part, preferred_element_type=jn...  173 us
    all_to_all x1, waiting for transfers between devices, local_block(): qkv_head = lax.all_to_all(qkv_tok, 'sp', 2, 3, tiled=True)  148 us
    all_to_all x1, waiting for transfers between devices, local_block(): d_qkv_tok = lax.all_to_all(d_qkv_head, 'sp', 3, 2, tiled=True)  135 us
    dot_general x16, matrix products, q_step(): jnp.einsum('bhqd,bhkd->bhqk', do_part, v_all, preferred_element_type=jnp....  92.5 us
  transfers between devices with their start and end apart: 5, of which 3 were waited for; matrix products, arithmetic and copies ran while one was open for 49% of the time, Pallas kernels for 0%

commit v1 on v0

v1 whole, which is shorter than its diff:
```python
import functools
import math
import jax
import jax.numpy as jnp
from jax import lax
from jax.experimental import pallas as pl
from jax.experimental.pallas import tpu as pltpu
from jax.sharding import Mesh, PartitionSpec as P

LN_EPS = 1e-5
NEG_BIG = -1e30
LOG2_E = 1.4426950408889634


def layer_norm(x_rows, gamma_f, beta_f):
    row_mean = jnp.mean(x_rows, axis=-1, keepdims=True)
    centred = x_rows - row_mean
    row_var = jnp.mean(centred * centred, axis=-1, keepdims=True)
    return centred * lax.rsqrt(row_var + LN_EPS) * gamma_f + beta_f


def dot_nn(a, b):
    return lax.dot_general(a, b, (((1,), (0,)), ((), ())), preferred_element_type=jnp.float32)


def dot_nt(a, b):
    return lax.dot_general(a, b, (((1,), (1,)), ((), ())), preferred_element_type=jnp.float32)


def fold(x, op):
    return op(x.reshape(x.shape[0] // 8, 8, x.shape[1]), axis=0)


def attention_kernel(n_blk, half, kind_ref, core_ref, qa, ka, va, ga, qb, kb, vb, gb, oa, ob, dg,
                     qs, ks, vs, gs, kt, vt, s_scr, dp_scr, dk_scr, dv_scr, out_scr):
    head = pl.program_id(0)
    qi = pl.program_id(1)
    core = core_ref[0]
    blk = 2 * half
    scale = 1.0 / math.sqrt(qs.shape[2])
    at_a = pl.multiple_of(core * half, half)
    at_b = pl.multiple_of((1 - core) * half, half)

    @pl.when(qi == 0)
    def _():
        for dst, src_a, src_b in ((qs, qa, qb), (ks, ka, kb), (vs, va, vb), (gs, ga, gb)):
            for c in range(n_blk):
                dst[c, pl.ds(at_a, half), :] = src_a[c]
                dst[c, pl.ds(at_b, half), :] = src_b[c]
        for c in range(n_blk):
            kt[c] = jnp.transpose(ks[c])
            vt[c] = jnp.transpose(vs[c])
        dk_scr[...] = jnp.zeros_like(dk_scr)
        dv_scr[...] = jnp.zeros_like(dv_scr)

    def process(chunks, band_first):
        q = qs[qi]
        g = gs[qi]
        n = len(chunks)
        row = lax.broadcasted_iota(jnp.int32, (blk, blk), 0)
        col = lax.broadcasted_iota(jnp.int32, (blk, blk), 1)
        top = None
        for idx, c in enumerate(chunks):
            s = dot_nt(ks[c], q) * (scale * LOG2_E)
            if idx == n - 1:
                s = jnp.where(row <= col, s, NEG_BIG)
            if band_first and idx == 0:
                s = jnp.where(row > col, s, NEG_BIG)
            s_scr[idx] = s
            part = fold(s, jnp.max)
            top = part if top is None else jnp.maximum(top, part)
            dp_scr[idx] = dot_nt(vs[c], g).astype(jnp.bfloat16)
        top = jnp.max(top, axis=0, keepdims=True)
        total = None
        for idx in range(n):
            e = jnp.exp2(s_scr[idx] - top)
            s_scr[idx] = e
            part = fold(e, jnp.sum)
            total = part if total is None else total + part
        inv = 1.0 / jnp.sum(total, axis=0, keepdims=True)
        delta = None
        o_t = None
        for idx, c in enumerate(chunks):
            p = s_scr[idx] * inv
            s_scr[idx] = p
            part = fold(p * dp_scr[idx].astype(jnp.float32), jnp.sum)
            delta = part if delta is None else delta + part
            p_bf = p.astype(jnp.bfloat16)
            o_part = dot_nn(vt[c], p_bf)
            o_t = o_part if o_t is None else o_t + o_part
            dv_scr[c] += dot_nn(p_bf, g)
        delta = jnp.sum(delta, axis=0, keepdims=True)
        dq_t = None
        for idx, c in enumerate(chunks):
            ds = (s_scr[idx] * (dp_scr[idx].astype(jnp.float32) - delta)).astype(jnp.bfloat16)
            dq_part = dot_nn(kt[c], ds)
            dq_t = dq_part if dq_t is None else dq_t + dq_part
            dk_scr[c] += dot_nn(ds, q)
        out_scr[0] = jnp.transpose(o_t).astype(jnp.bfloat16)
        out_scr[1] = jnp.transpose(dq_t * scale).astype(jnp.bfloat16)

    banded = kind_ref[head] == 1
    for i in range(n_blk):
        cond = qi == i
        if i >= 2:
            cond = cond & jnp.logical_not(banded)

        @pl.when(cond)
        def _():
            process(list(range(i + 1)), False)

    @pl.when(banded & (qi >= 2))
    def _():
        process([qi - 2, qi - 1, qi], True)

    oa[qi] = out_scr[0, pl.ds(at_a, half), :]
    ob[qi] = out_scr[0, pl.ds(at_b, half), :]
    dg[0, 0, qi] = out_scr[1, pl.ds(at_a, half), :]
    dg[0, 1, qi] = out_scr[1, pl.ds(at_b, half), :]

    @pl.when(qi == n_blk - 1)
    def _():
        for c in range(n_blk):
            out_scr[0] = (dk_scr[c] * scale).astype(jnp.bfloat16)
            out_scr[1] = dv_scr[c].astype(jnp.bfloat16)
            dg[1, 0, c] = out_scr[0, pl.ds(at_a, half), :]
            dg[1, 1, c] = out_scr[0, pl.ds(at_b, half), :]
            dg[2, 0, c] = out_scr[1, pl.ds(at_a, half), :]
            dg[2, 1, c] = out_scr[1, pl.ds(at_b, half), :]


def attention(kinds, core, qkv_own, do_own, qkv_oth, do_oth):
    n_blk, half, _ = qkv_own.shape
    heads = kinds.shape[0]
    dim = 128
    blk = 2 * half

    def own(part):
        return pl.BlockSpec((n_blk, half, dim), lambda h, i, kind, cr: (0, 0, part * 2 * heads + cr[0] * heads + h))

    out3 = pl.BlockSpec((n_blk, half, dim), lambda h, i, kind, cr: (0, 0, h))
    out5 = pl.BlockSpec((3, 2, n_blk, half, dim), lambda h, i, kind, cr: (0, 0, 0, 0, h))
    bf = jnp.bfloat16
    wide = heads * dim
    flops = 6 * 2 * heads * (n_blk * blk) ** 2 * dim // 2
    return pl.pallas_call(
        functools.partial(attention_kernel, n_blk, half),
        grid_spec=pltpu.PrefetchScalarGridSpec(
            num_scalar_prefetch=2,
            grid=(heads, n_blk),
            in_specs=[own(0), own(1), own(2), own(0), out3, out3, out3, out3],
            out_specs=[out3, out3, out5],
            scratch_shapes=[pltpu.VMEM((n_blk, blk, dim), bf)] * 4
            + [pltpu.VMEM((n_blk, dim, blk), bf)] * 2
            + [pltpu.VMEM((n_blk, blk, blk), jnp.float32), pltpu.VMEM((n_blk, blk, blk), bf)]
            + [pltpu.VMEM((n_blk, blk, dim), jnp.float32)] * 2
            + [pltpu.VMEM((2, blk, dim), bf)],
        ),
        out_shape=[jax.ShapeDtypeStruct((n_blk, half, wide), bf)] * 2
        + [jax.ShapeDtypeStruct((3, 2, n_blk, half, wide), bf)],
        compiler_params=pltpu.CompilerParams(
            dimension_semantics=("arbitrary", "arbitrary"), vmem_limit_bytes=48 * 1024 * 1024
        ),
        cost_estimate=pl.CostEstimate(flops=flops, bytes_accessed=40 * 2**20, transcendentals=heads * (n_blk * blk) ** 2 // 2),
        name="attention_fwd_bwd",
    )(kinds, core, qkv_own, qkv_own, qkv_own, do_own, *qkv_oth, do_oth)


def copy_kernel(*refs):
    refs[-1][...] = refs[-2][...]


def place(piece, total_rows, first_row, dst=None):
    rows, cols = piece.shape
    tile = 128 if cols > 4096 else 512
    skip = first_row // tile
    in_specs = [pl.BlockSpec((tile, cols), lambda r: (r, 0))]
    args = [piece]
    aliases = {}
    if dst is not None:
        in_specs = [pl.BlockSpec(memory_space=pl.ANY)] + in_specs
        args = [dst] + args
        aliases = {0: 0}
    return pl.pallas_call(
        copy_kernel,
        grid=(rows // tile,),
        in_specs=in_specs,
        out_specs=pl.BlockSpec((tile, cols), lambda r: (r + skip, 0)),
        out_shape=jax.ShapeDtypeStruct((total_rows, cols), piece.dtype),
        input_output_aliases=aliases,
        cost_estimate=pl.CostEstimate(flops=rows * cols * 8, bytes_accessed=2 * piece.nbytes, transcendentals=0),
        name="place_rows",
    )(*args)


def grad_sum_kernel(n_chip, rows, g0, g1, g2, small, out, small_out, acc, rc, rb, ra, slots, load_sem, loc_sem,
                    c_send, c_recv, b_send, b_recv, a_send, a_recv, g_send, g_recv, s_send, s_recv, v_send, v_recv):
    chip = lax.axis_index("chip")
    core = lax.axis_index("core")
    n_dev = 2 * n_chip
    me = chip * 2 + core
    bits = [chip % 2, (chip // 2) % 2, chip // 4]
    beside = [chip + (1 - 2 * bits[d]) * (1 << d) for d in range(3)]
    parts = (g0, g1, g2)
    chunk = rows // 8
    wide = acc.shape[2]
    mesh_id = pl.DeviceIdType.MESH

    barrier = pltpu.get_barrier_semaphore()
    for o in range(1, n_dev):
        to = (me + o) % n_dev
        pl.semaphore_signal(barrier, inc=1, device_id=(to // 2, to % 2), device_id_type=mesh_id)
    pl.semaphore_wait(barrier, n_dev - 1)

    def flip(b, f):
        return 1 - b if f else b

    def remote(src, dst, send, recv, to_chip, to_core):
        c = pltpu.make_async_remote_copy(src_ref=src, dst_ref=dst, send_sem=send, recv_sem=recv,
                                         device_id=(to_chip, to_core), device_id_type=mesh_id)
        c.start()
        return c

    bc = [bits[t % 3] for t in range(3)]
    bb = [bits[(t + 1) % 3] for t in range(3)]
    ba = [bits[(t + 2) % 3] for t in range(3)]
    to_c = [beside[t % 3] for t in range(3)]
    to_b = [beside[(t + 1) % 3] for t in range(3)]
    to_a = [beside[(t + 2) % 3] for t in range(3)]

    def near(t, fb, fa):
        return pl.multiple_of(flip(bb[t], fb) * (2 * chunk) + flip(ba[t], fa) * chunk, chunk)

    def full(t, fc, fb, fa):
        return pl.multiple_of(flip(bc[t], fc) * (4 * chunk) + flip(bb[t], fb) * (2 * chunk) + flip(ba[t], fa) * chunk, chunk)

    flips = ((1, 1), (1, 0), (0, 1), (0, 0))
    c_copy = {}
    for j, (fb, fa) in enumerate(flips):
        for t in range(3):
            c_copy[t, j] = remote(parts[t].at[pl.ds(full(t, 1, fb, fa), chunk), :], rc.at[t, j],
                                  c_send.at[t, j], c_recv.at[t, j], to_c[t], core)
    loads = []
    for t in range(3):
        half_row = pl.multiple_of(bc[t] * (4 * chunk), 4 * chunk)
        load = pltpu.make_async_copy(parts[t].at[pl.ds(half_row, 4 * chunk), :], acc.at[t], load_sem.at[t])
        load.start()
        loads.append(load)
    v_copy = []
    for o in range(1, n_dev):
        to = (me + o) % n_dev
        v_copy.append(remote(small, slots.at[o], v_send.at[o], v_recv.at[o], to // 2, to % 2))
    slots[0] = small[...]
    for load in loads:
        load.wait()

    tile = 64

    def add(t, fb, fa, got):
        first = near(t, fb, fa)

        def step(i, carry):
            at = pl.ds(pl.multiple_of(first + i * tile, tile), tile)
            acc[t, at, :] = acc[t, at, :] + got[pl.ds(pl.multiple_of(i * tile, tile), tile), :]
            return carry

        lax.fori_loop(0, chunk // tile, step, 0)

    def held(t, fb, fa):
        return acc.at[t, pl.ds(near(t, fb, fa), chunk), :]

    b_copy = {}
    for j in range(2):
        fb, fa = flips[j]
        for t in range(3):
            c_copy[t, j].wait_recv()
            add(t, fb, fa, rc.at[t, j])
        for t in range(3):
            b_copy[t, j] = remote(held(t, fb, fa), rb.at[t, j], b_send.at[t, j], b_recv.at[t, j], to_b[t], core)
    for j in range(2, 4):
        fb, fa = flips[j]
        for t in range(3):
            c_copy[t, j].wait_recv()
            add(t, fb, fa, rc.at[t, j])
    a_copy = {}
    for t in range(3):
        b_copy[t, 0].wait_recv()
        add(t, 0, 1, rb.at[t, 0])
    for t in range(3):
        a_copy[t] = remote(held(t, 0, 1), ra.at[t], a_send.at[t], a_recv.at[t], to_a[t], core)
    for t in range(3):
        b_copy[t, 1].wait_recv()
        add(t, 0, 0, rb.at[t, 1])
    for t in range(3):
        a_copy[t].wait_recv()
        add(t, 0, 0, ra.at[t])

    def place_at(t, fc, fb, fa):
        return out.at[pl.ds(full(t, fc, fb, fa), chunk), pl.ds(pl.multiple_of((2 * t + core) * wide, wide), wide)]

    g_copy, s_copy, stores = {}, {}, []

    def gather(t, idx, src, dst, to):
        g_copy[t, idx] = remote(src, dst, g_send.at[t, idx], g_recv.at[t, idx], to, core)

    def share(t, idx, src, dst):
        s_copy[t, idx] = remote(src, dst, s_send.at[t, idx], s_recv.at[t, idx], chip, 1 - core)

    for idx, to in ((0, to_a), (1, to_b), (3, to_c)):
        for t in range(3):
            gather(t, idx, held(t, 0, 0), place_at(t, 0, 0, 0), to[t])
    for t in range(3):
        share(t, 0, held(t, 0, 0), place_at(t, 0, 0, 0))
        store = pltpu.make_async_copy(held(t, 0, 0), place_at(t, 0, 0, 0), loc_sem.at[t])
        store.start()
        stores.append(store)
    got_flips = ((0, 0, 1), (0, 1, 0), (0, 1, 1), (1, 0, 0), (1, 0, 1), (1, 1, 0), (1, 1, 1))
    onward = {0: ((2, to_b), (4, to_c)), 1: ((5, to_c),), 2: ((6, to_c),)}
    for idx in (0, 1, 3, 2, 4, 5, 6):
        for t in range(3):
            g_copy[t, idx].wait_recv()
            where = place_at(t, *got_flips[idx])
            for nxt, to in onward.get(idx, ()):
                gather(t, nxt, where, where, to[t])
            share(t, idx + 1, where, where)

    for copy in v_copy:
        copy.wait_recv()
    total = slots[me % n_dev]
    for d in range(1, n_dev):
        total = total + slots[(me + n_dev - d) % n_dev]
    small_out[...] = total

    for group in (s_copy,):
        for copy in group.values():
            copy.wait_recv()
    for group in (c_copy, b_copy, a_copy, g_copy, s_copy):
        for copy in group.values():
            copy.wait_send()
    for copy in v_copy:
        copy.wait_send()
    for store in stores:
        store.wait()


def grad_sum(n_chip, g_parts, small):
    rows, wide = g_parts[0].shape
    chunk = rows // 8
    n_dev = 2 * n_chip
    f32 = jnp.float32
    dma = pltpu.SemaphoreType.DMA
    hbm = pl.BlockSpec(memory_space=pl.ANY)
    vmem = pl.BlockSpec(memory_space=pltpu.VMEM)
    return pl.pallas_call(
        functools.partial(grad_sum_kernel, n_chip, rows),
        in_specs=[hbm, hbm, hbm, vmem],
        out_specs=[hbm, vmem],
        out_shape=[jax.ShapeDtypeStruct((rows, 6 * wide), f32), jax.ShapeDtypeStruct(small.shape, f32)],
        scratch_shapes=[
            pltpu.VMEM((3, 4 * chunk, wide), f32), pltpu.VMEM((3, 4, chunk, wide), f32),
            pltpu.VMEM((3, 2, chunk, wide), f32), pltpu.VMEM((3, chunk, wide), f32),
            pltpu.VMEM((n_dev,) + small.shape, f32), dma((3,)), dma((3,)),
            dma((3, 4)), dma((3, 4)), dma((3, 2)), dma((3, 2)), dma((3,)), dma((3,)),
            dma((3, 7)), dma((3, 7)), dma((3, 8)), dma((3, 8)), dma((n_dev,)), dma((n_dev,)),
        ],
        compiler_params=pltpu.CompilerParams(collective_id=0, has_side_effects=True, vmem_limit_bytes=44 * 1024 * 1024),
        cost_estimate=pl.CostEstimate(flops=3 * 10**11, bytes_accessed=150 * 2**20, transcendentals=0),
        name="grad_sum",
    )(*g_parts, small)


def solution(mesh):
    n_dev = mesh.shape["sp"]
    n_chip = n_dev // 2
    grid_mesh = Mesh(mesh.devices.reshape(n_chip, 2), ("chip", "core"))
    tok_spec = P(None, ("chip", "core"), None)
    swap_pairs = [(0, 1), (1, 0)]

    def local_block(x, d_y, ln_gamma, ln_beta, w_qkv, b_qkv, w_out, b_out, head_kind):
        half = x.shape[1]
        d_model = x.shape[2]
        num_heads = head_kind.shape[0]
        own_heads = num_heads // 2
        wide = d_model // 2
        n_tok = n_chip * half
        f32, bf = jnp.float32, jnp.bfloat16
        core = lax.axis_index("core")
        core_arr = jnp.full((1,), core, jnp.int32)
        my_kinds = lax.dynamic_slice_in_dim(head_kind, core * own_heads, own_heads)

        def swap(v):
            return lax.ppermute(v, "core", swap_pairs)

        def other_half(v, part):
            lo = v[:, part * d_model:part * d_model + wide]
            hi = v[:, part * d_model + wide:(part + 1) * d_model]
            return jnp.where(core == 0, hi, lo).reshape(n_chip, half, wide)

        def by_core(mine, theirs):
            return jnp.where(core == 0, mine, theirs), jnp.where(core == 0, theirs, mine)

        x_b = lax.all_to_all(x, "chip", 0, 0, tiled=True).reshape(n_tok, d_model)
        g_b = lax.all_to_all(d_y, "chip", 0, 0, tiled=True).reshape(n_tok, d_model)

        x_f = x_b.astype(f32)
        h_f, ln_pull = jax.vjp(layer_norm, x_f, ln_gamma.astype(f32), ln_beta.astype(f32))
        h_norm = h_f.astype(bf)
        h_all = jnp.concatenate([h_norm, swap(h_norm)], axis=0)
        qkv = (dot_nn(h_norm, w_qkv) + b_qkv.astype(f32)).astype(bf)
        qkv_own = qkv.reshape(n_chip, half, 3 * d_model)
        qkv_oth = [swap(other_half(qkv, part)) for part in range(3)]
        d_attn = dot_nt(g_b, w_out).astype(bf)
        do_own = d_attn.reshape(n_chip, half, d_model)
        do_oth = swap(other_half(d_attn, 0))

        o_own, o_send, dg = attention(my_kinds, core_arr, qkv_own, do_own, qkv_oth, do_oth)
        o_recv = swap(o_send)
        dg_own = dg[:, 0]
        dg_recv = swap(dg[:, 1])

        o_lo, o_hi = by_core(o_own, o_recv)
        attn_tok = jnp.concatenate([o_lo.reshape(n_tok, wide), o_hi.reshape(n_tok, wide)], axis=1)
        d_wout = lax.dot_general(attn_tok, g_b, (((0,), (0,)), ((), ())), preferred_element_type=f32)
        d_wout, dg_own, dg_recv = lax.optimization_barrier((d_wout, dg_own, dg_recv))
        d_wout = lax.psum(d_wout, ("chip", "core"))
        y_b = (x_f + dot_nn(attn_tok, w_out) + b_out.astype(f32)).astype(bf)
        y_out = lax.all_to_all(y_b.reshape(n_chip, half, d_model), "chip", 0, 0, tiled=True)

        dg_lo, dg_hi = by_core(dg_own.reshape(3, n_tok, wide), dg_recv.reshape(3, n_tok, wide))
        d_qkv = jnp.concatenate([dg_lo[0], dg_hi[0], dg_lo[1], dg_hi[1], dg_lo[2], dg_hi[2]], axis=1)
        d_h = dot_nt(d_qkv, w_qkv).astype(bf).astype(f32)
        d_x_ln, d_gamma, d_beta = ln_pull(d_h)
        d_x_b = (g_b.astype(f32) + d_x_ln).astype(bf)
        d_x = lax.all_to_all(d_x_b.reshape(n_chip, half, d_model), "chip", 0, 0, tiled=True)
        d_bqkv = jnp.sum(d_qkv, axis=0, dtype=f32)
        d_bout = jnp.sum(g_b, axis=0, dtype=f32)

        dg_tok = dg.reshape(3, 2 * n_tok, wide)
        d_w = [lax.dot_general(h_all, dg_tok[t], (((0,), (0,)), ((), ())), preferred_element_type=f32) for t in range(3)]
        small = jnp.concatenate([d_gamma, d_beta, d_bqkv, d_bout]).reshape(-1, 128)
        d_wqkv, small = grad_sum(n_chip, d_w, small)
        d_wqkv = place(d_wqkv, d_model, 0)
        small = small.reshape(-1)
        d_gamma, d_beta, d_bqkv, d_bout = (small[:d_model], small[d_model:2 * d_model], small[2 * d_model:5 * d_model], small[5 * d_model:])
        d_wout = place(d_wout, d_model, 0)
        y_out = place(y_out.reshape(n_tok, d_model), n_tok, 0).reshape(n_chip, half, d_model)
        d_x = place(d_x.reshape(n_tok, d_model), n_tok, 0).reshape(n_chip, half, d_model)
        return y_out, d_x, d_gamma, d_beta, d_wqkv, d_bqkv, d_wout, d_bout

    return jax.shard_map(
        local_block, mesh=grid_mesh,
        in_specs=(tok_spec, tok_spec, P(), P(), P(), P(), P(), P(), P()),
        out_specs=(tok_spec, tok_spec, P(), P(), P(), P(), P(), P()), check_vma=False)
```

time: 2380 us -> 1000 us (0.42)
  matrix products: 1120 us -> 146 us
  waiting for transfers between devices: 750 us -> 54 us
  Pallas kernels: 0 us -> 610 us
  other arithmetic: 240 us -> 41.7 us
  local copies, waits for them, and re-layouts: 193 us -> 49 us
    dot_general x118 -> x8, matrix products: 1120 us -> 146 us  [the longest x2 47.3 us: dot_nt(): lax.dot_general(a, b, (((1,), (1,)), ((), ())), preferred_element_type=jn...]
    pallas_call x0 -> x6, Pallas kernels: none -> 610 us  [the longest x1 454 us: grad_sum(): pl.pallas_call(functools.partial(grad_sum_kernel, n_chip, rows), in_specs...]
    psum x1, waiting for transfers between devices: 467 us -> 0.01 us  [local_block(): d_wout = lax.psum(d_wout, ('chip', 'core'))]
    all_to_all x4 -> x3, waiting for transfers between devices: 283 us -> 44.5 us  [the longest x1 44.5 us: local_block(): g_b = lax.all_to_all(d_y, 'chip', 0, 0, tiled=True).reshape(n_tok, d_model)]
    sub x32 -> x0, other arithmetic: 185 us -> none  [score_probs(): return jax.nn.softmax(jnp.where(allowed, logits, NEG_BIG), axis=-1)]
    all_to_all x0 -> x1, blocking collectives: none -> 59 us  [local_block(): x_b = lax.all_to_all(x, 'chip', 0, 0, tiled=True).reshape(n_tok, d_model)]
    unnamed x46 -> x57, local copies, waits for them, and re-layouts: 78.3 us -> 21.4 us
    psum x1 -> x0, blocking collectives: 35.3 us -> none  [local_block(): lax.psum((d_gamma, d_beta, d_wqkv, d_bqkv, d_wout, d_bout), 'sp')]
  transfers between devices with their start and end apart: 5 -> 11, of which waited for: 3 -> 4; matrix products, arithmetic and copies ran while one was open for 49% -> 21% of each run, Pallas kernels for 0% -> 50%
where the time goes in v1:
time: 1000 us; the launch traced here: 991 us
  Pallas kernels  610 us (61%)
  matrix products  146 us (15%)
  blocking collectives  59 us (6%)
  waiting for transfers between devices  54 us (5%)
  local copies, waits for them, and re-layouts  49 us (5%)
  other arithmetic  41.7 us (4%)
  starting transfers between devices  16.5 us (2%)
  between operations  14.9 us (1%)
    pallas_call x1, Pallas kernels, grad_sum(): pl.pallas_call(functools.partial(grad_sum_kernel, n_chip, rows), in_specs...  454 us
    pallas_call x1, Pallas kernels, attention(): pl.pallas_call(functools.partial(attention_kernel, n_blk, half), grid_spe...  100 us
    all_to_all x1, blocking collectives, local_block(): x_b = lax.all_to_all(x, 'chip', 0, 0, tiled=True).reshape(n_tok, d_model)  59 us
    pallas_call x4, Pallas kernels, place(): pl.pallas_call(copy_kernel, grid=(rows // tile,), in_specs=in_specs, out_...  55.2 us
    dot_general x2, matrix products, dot_nt(): lax.dot_general(a, b, (((1,), (1,)), ((), ())), preferred_element_type=jn...  47.3 us
    all_to_all x1, waiting for transfers between devices, local_block(): g_b = lax.all_to_all(d_y, 'chip', 0, 0, tiled=True).reshape(n_tok, d_model)  44.5 us
    dot_general x3, matrix products, local_block(): lax.dot_general(h_all, dg_tok[t], (((0,), (0,)), ((), ())), preferred_ele...  43.1 us
    dot_general x2, matrix products, dot_nn(): lax.dot_general(a, b, (((1,), (0,)), ((), ())), preferred_element_type=jn...  40.9 us
  transfers between devices with their start and end apart: 11, of which 4 were waited for; matrix products, arithmetic and copies ran while one was open for 21% of the time, Pallas kernels for 50%

profile of v1, /device:TPU:0, one launch (start us, length us, event | category | flops | bytes accessed | tf_op | source)
XLA Modules:
  0.0 990.8 jit_solution(13360888759228475938)
XLA Ops:
  7.2 59.0 %all_to_all.20 = bf16[8,128,2048]{2,1,0:T(8,128)(2,1)} all-to-all(bf16[8,128,2048]{2,1,0:T(8,128)(2,1)} %param.9), channel_id=1, replica_groups=mesh['chip'=8,'core'=2] {'chip'}, dimensions={0} | all-to-all | bytes 8388608 | tf_op jit(solution)/shard_map/all_to_all | solution.py:402
  66.2 4.6 all-to-all-start.1
  77.7 44.5 %all-to-all-done.1 = bf16[8,128,2048]{2,1,0:T(8,128)(2,1)} async-done(((bf16[8,128,2048]{2,1,0:T(8,128)(2,1)}), bf16[8,128,2048]{2,1,0:T(8,128)(2,1)}, u32[]{:S(2)}, u32[]{:S(2)}) %all-to-all-start.1) | async-done | bytes 4194336 | tf_op jit(solution)/shard_map/all_to_all | solution.py:403
  122.1 12.6 %convolution_convert_fusion.1 = bf16[1024,2048]{1,0:T(8,128)(2,1)S(1)} fusion(bf16[1024,2048]{1,0:T(8,128)(2,1)} %bitcast.5, bf16[2048,2048]{1,0:T(8,128)(2,1)} %param.15), kind=kOutput, calls=%fused_computation.33 | convolution fusion | flops 8592031744 | bytes 16777216 | tf_op jit(solution)/shard_map/dot_general | solution.py:27
  141.5 30.5 %add_convert_fusion = bf16[1024,6144]{1,0:T(8,128)(2,1)S(1)} fusion(f32[6144]{0:T(1024)S(1)} %convert_element_type.59, bf16[1024,2048]{1,0:T(8,128)(2,1)} %fusion.8, bf16[2048,6144]{1,0:T(8,128)(2,1)} %param.13), kind=kOutput, calls=%fused_computation.1 | convolution fusion | flops 25782386688 | bytes 41967616 | tf_op jit(solution)/shard_map/dot_general | solution.py:23
  188.8 100.4 %attention_fwd_bwd.1 = (bf16[8,128,1024]{2,1,0:T(8,128)(2,1)S(1)}, bf16[8,128,1024]{2,1,0:T(8,128)(2,1)S(1)}, bf16[3,2,8,128,1024]{4,3,2,1,0:T(8,128)(2,1)}) custom-call(s32[8]{0:T(128)S(1)} %dynamic_slice.3.kind_ref, s32[1]{0:T(128)} %bitcast.1.core_ref, bf16[8,128,6144]{2,1,0:T(8,128)(2,1)} %bitcast.92, bf16[8,128,6144]{2,1,0:T(8,128)(2,1)} %bitcast.93, ...), custom_call_target="tpu_custom_call" | custom-call | flops 25769803776 | bytes 41943040 | tf_op jit(solution)/shard_map/attention_fwd_bwd/pallas_call | solution.py:146
  293.2 6.5 slice_bitcast_fusion.1
  299.9 6.6 slice_bitcast_fusion
  306.5 9.3 fusion.27
  318.8 10.4 %fusion.12 = bf16[1024,2048]{1,0:T(8,128)(2,1)} fusion(bf16[8,128,2048]{2,1,0:T(8,128)(2,1)S(1)} %copy-done.2, f32[2048]{0:T(1024)S(1)} %convert_element_type.62, bf16[2048,2048]{1,0:T(8,128)(2,1)S(1)} %bitcast.114, bf16[1024,1024]{1,0:T(8,128)(2,1)S(1)} %bitcast.111, bf16[1024,1024]{1,0:T(8,128)(2,1)S(1)} %bitcast.109), kind=kOutput, calls=%fused_computation.23 | convolution fusion | flops 8606711808 | bytes 20979712 | tf_op jit(solution)/shard_map/dot_general | solution.py:23
  329.1 5.5 all-to-all-start.2
  334.7 14.9 %fusion.16.g1 = f32[2048,1024]{1,0:T(8,128)} fusion(bf16[2048,1024]{1,0:T(8,128)(2,1)} %bitcast.107, bf16[1024,2048]{1,0:T(8,128)(2,1)} %collective-permute-done.6, bf16[1024,2048]{1,0:T(8,128)(2,1)} %fusion.8), kind=kOutput, calls=%fused_computation.36 | convolution fusion | flops 8606711808 | bytes 20971520 | tf_op jit(solution)/shard_map/dot_general | solution.py:439
  349.7 13.5 %fusion.15.g2 = f32[2048,1024]{1,0:T(8,128)} fusion(bf16[2048,1024]{1,0:T(8,128)(2,1)S(1)} %bitcast.106, bf16[1024,2048]{1,0:T(8,128)(2,1)} %collective-permute-done.6, bf16[1024,2048]{1,0:T(8,128)(2,1)} %fusion.8), kind=kOutput, calls=%fused_computation.35 | convolution fusion | flops 8606711808 | bytes 20971520 | tf_op jit(solution)/shard_map/dot_general | solution.py:439
  363.2 14.4 %fusion.14 = f32[2048,2048]{1,0:T(8,128)} fusion(bf16[1024,2048]{1,0:T(8,128)(2,1)} %bitcast.5, bf16[1024,1024]{1,0:T(8,128)(2,1)S(1)} %bitcast.112, bf16[1024,1024]{1,0:T(8,128)(2,1)S(1)} %bitcast.110), kind=kOutput, calls=%fused_computation.34 | convolution fusion | flops 8598323200 | bytes 25165824 | tf_op jit(solution)/shard_map/dot_general | solution.py:423
  377.5 14.6 %fusion.17.g0 = f32[2048,1024]{1,0:T(8,128)} fusion(bf16[2048,1024]{1,0:T(8,128)(2,1)} %bitcast.105, bf16[1024,2048]{1,0:T(8,128)(2,1)} %collective-permute-done.6, bf16[1024,2048]{1,0:T(8,128)(2,1)} %fusion.8), kind=kOutput, calls=%fused_computation.37 | convolution fusion | flops 8606711808 | bytes 20971520 | tf_op jit(solution)/shard_map/dot_general | solution.py:439
  396.0 5.2 broadcast_select_fusion
  412.6 6.9 convert_reduce_fusion
  419.6 34.7 %fusion.2 = (f32[1024]{0:T(1024)S(1)}, bf16[1024,2048]{1,0:T(8,128)(2,1)}) fusion(bf16[8,128,2048]{2,1,0:T(8,128)(2,1)S(1)} %copy-done.3, f32[2048]{0:T(1024)S(1)} %copy-done.11, f32[1024]{0:T(1024)S(1)} %copy-done.13, bf16[1024,6144]{1,0:T(8,128)(2,1)} %constant_dynamic-update-slice_fusion, bf16[2048,6144]{1,0:T(8,128)(2,1)} %param.13), kind=kOutput, calls=%fused_computation.8 | convolution fusion | flops 25784483840 | bytes 46153728 | tf_op jit(solution)/shard_map/dot_general | solution.py:27
  454.3 6.3 fusion.3
  460.7 7.1 add_convert_fusion.1
  467.7 5.2 all-to-all-start.3
  476.3 454.5 %grad_sum.1 = (f32[2048,6144]{1,0:T(8,128)}, f32[96,128]{1,0:T(8,128)S(1)}) custom-call(f32[2048,1024]{1,0:T(8,128)S(1)} %copy-done, f32[2048,1024]{1,0:T(8,128)} %fusion.16.g1, f32[2048,1024]{1,0:T(8,128)} %fusion.15.g2, f32[96,128]{1,0:T(8,128)S(1)} %maximum_bitcast_fusion.small), custom_call_target="tpu_custom_call" | custom-call | flops 299999985664 | bytes 157286400 | tf_op jit(solution)/shard_map/grad_sum/pallas_call | solution.py:354
  930.8 36.3 %place_rows.6 = f32[2048,6144]{1,0:T(8,128)} custom-call(f32[2048,6144]{1,0:T(8,128)} %get-tuple-element.22.refs_0_), custom_call_target="tpu_custom_call" | custom-call | flops 100663296 | bytes 100663296 | tf_op jit(solution)/shard_map/place_rows/pallas_call | solution.py:184
  972.0 11.4 %place_rows.7 = f32[2048,2048]{1,0:T(8,128)} custom-call(f32[2048,2048]{1,0:T(8,128)} %all-reduce.2.cloned.1.call-done.refs_0_), custom_call_target="tpu_custom_call" | custom-call | flops 33554432 | bytes 33554432 | tf_op jit(solution)/shard_map/place_rows/pallas_call | solution.py:184
  (100 shorter events, 61.1 us)
Async XLA Ops:
  7.2 63.6 %copy-start.20 = (bf16[2048]{0:T(1024)(128)(2,1)S(1)}, bf16[2048]{0:T(1024)(128)(2,1)}, u32[]{:S(2)}) copy-start(bf16[2048]{0:T(1024)(128)(2,1)} %param.11) | copy-start | bytes 12292
  7.2 63.6 %copy-start.21 = (bf16[2048]{0:T(1024)(128)(2,1)S(1)}, bf16[2048]{0:T(1024)(128)(2,1)}, u32[]{:S(2)}) copy-start(bf16[2048]{0:T(1024)(128)(2,1)} %param.12) | copy-start | bytes 12292
  7.2 63.6 %copy-start.19 = (bf16[6144]{0:T(1024)(128)(2,1)S(1)}, bf16[6144]{0:T(1024)(128)(2,1)}, u32[]{:S(2)}) copy-start(bf16[6144]{0:T(1024)(128)(2,1)} %param.14) | copy-start | bytes 36868
  66.2 56.0 %all-to-all-start.1 = ((bf16[8,128,2048]{2,1,0:T(8,128)(2,1)}), bf16[8,128,2048]{2,1,0:T(8,128)(2,1)}, u32[]{:S(2)}, u32[]{:S(2)}) async-start(bf16[8,128,2048]{2,1,0:T(8,128)(2,1)} %param.10), calls=%async_computation.1 | async-start | bytes 8388608 | tf_op jit(solution)/shard_map/all_to_all | solution.py:403
  70.8 64.2 %copy-start.10 = (f32[2048]{0:T(1024)}, f32[2048]{0:T(1024)S(1)}, u32[]{:S(2)}) copy-start(f32[2048]{0:T(1024)S(1)} %convert_element_type.56) | copy-start | bytes 24580
  73.6 61.4 %copy-start.12 = (f32[1024]{0:T(1024)}, f32[1024]{0:T(1024)S(1)}, u32[]{:S(2)}) copy-start(f32[1024]{0:T(1024)S(1)} %get-tuple-element.46) | copy-start | bytes 12292
  77.7 57.3 %copy-start.14 = (f32[1024]{0:T(1024)}, f32[1024]{0:T(1024)S(1)}, u32[]{:S(2)}) copy-start(f32[1024]{0:T(1024)S(1)} %bitcast_rsqrt_fusion) | copy-start | bytes 12292
  134.9 44.4 %collective-permute-start.3 = (bf16[8,128,1024]{2,1,0:T(8,128)(2,1)S(1)}, bf16[8,128,1024]{2,1,0:T(8,128)(2,1)}, u32[]{:S(2)}, u32[]{:S(2)}) collective-permute-start(bf16[8,128,1024]{2,1,0:T(8,128)(2,1)S(1)} %bitcast.108), channel_id=1, source_target_pairs={{0,1},{1,0},{2,3},{3,2},{4,5},{5,4},{6,7},{7,6},{8,9},{9,8},{10,11... | collective-permute-start | bytes 6291464 | tf_op jit(solution)/shard_map/ppermute | solution.py:392
  178.7 4.1 collective-permute-start
  178.7 7.1 collective-permute-start.2
  179.2 9.6 collective-permute-start.1
  188.8 100.6 %copy-start.22 = (bf16[2048]{0:T(1024)(128)(2,1)S(1)}, bf16[2048]{0:T(1024)(128)(2,1)}, u32[]{:S(2)}) copy-start(bf16[2048]{0:T(1024)(128)(2,1)} %param.16) | copy-start | bytes 12292
  289.2 26.6 %collective-permute-start.4 = (bf16[8,128,1024]{2,1,0:T(8,128)(2,1)S(1)}, bf16[8,128,1024]{2,1,0:T(8,128)(2,1)S(1)}, u32[]{:S(2)}, u32[]{:S(2)}) collective-permute-start(bf16[8,128,1024]{2,1,0:T(8,128)(2,1)S(1)} %get-tuple-element.17), channel_id=1, source_target_pairs={{0,1},{1,0},{2,3},{3,2},{4,5},{5,4},{6,7},{7,6},{8,9},{9,8},{10,11... | collective-permute-start | bytes 6291464 | tf_op jit(solution)/shard_map/ppermute | solution.py:392
  289.4 45.3 %collective-permute-start.6 = (bf16[1024,2048]{1,0:T(8,128)(2,1)}, bf16[1024,2048]{1,0:T(8,128)(2,1)}, u32[]{:S(2)}, u32[]{:S(2)}) collective-permute-start(bf16[1024,2048]{1,0:T(8,128)(2,1)} %fusion.8), channel_id=1, source_target_pairs={{0,1},{1,0},{2,3},{3,2},{4,5},{5,4},{6,7},{7,6},{8,9},{9,8},{10,11... | collective-permute-start | bytes 12582920 | tf_op jit(solution)/shard_map/ppermute | solution.py:392
  299.7 96.2 %collective-permute-start.5 = (bf16[3,8,128,1024]{3,2,1,0:T(8,128)(2,1)}, bf16[3,8,128,1024]{3,2,1,0:T(8,128)(2,1)}, u32[]{:S(2)}, u32[]{:S(2)}) collective-permute-start(bf16[3,8,128,1024]{3,2,1,0:T(8,128)(2,1)} %slice_bitcast_fusion.1), channel_id=1, source_target_pairs={{0,1},{1,0},{2,3},{3,2},{4,5},{5,4},{6,7},{7,6},{8,9},{9,8},{10,11... | collective-permute-start | bytes 18874376 | tf_op jit(solution)/shard_map/ppermute | solution.py:392
  299.9 16.2 %slice-start = ((s8[8388608]{0:T(1024)(128)(4,1)}), s8[4194304]{0:T(1024)(128)(4,1)S(1)}, s32[]{:S(2)}) async-start(s8[8388608]{0:T(1024)(128)(4,1)} %bitcast.113), calls=%async_computation.5 | async-start | bytes 8388608
  316.0 13.1 %copy-start.8 = (bf16[8,128,1024]{2,1,0:T(8,128)(2,1)}, bf16[8,128,1024]{2,1,0:T(8,128)(2,1)S(1)}, u32[]{:S(2)}) copy-start(bf16[8,128,1024]{2,1,0:T(8,128)(2,1)S(1)} %get-tuple-element.42) | copy-start | bytes 6291460
  329.1 63.0 %all-to-all-start.2 = ((bf16[8,128,2048]{2,1,0:T(8,128)(2,1)}), bf16[8,128,2048]{2,1,0:T(8,128)(2,1)}, u32[]{:S(2)}, u32[]{:S(2)}) async-start(bf16[8,128,2048]{2,1,0:T(8,128)(2,1)} %bitcast.103), calls=%async_computation.2 | async-start | bytes 8388608 | tf_op jit(solution)/shard_map/all_to_all | solution.py:427
  334.7 637.4 %all-reduce.2.cloned.1.call-start = ((), (), s32[]{:S(2)}) async-start(), calls=%async_computation.4 | async-start | bytes 33554432 | tf_op jit(solution)/shard_map/psum | solution.py:425
  334.7 14.9 %copy-start.7 = (bf16[1,2,8,128,1024]{4,3,2,1,0:T(8,128)(2,1)S(1)}, bf16[1,2,8,128,1024]{4,3,2,1,0:T(8,128)(2,1)}, u32[]{:S(2)}) copy-start(bf16[1,2,8,128,1024]{4,3,2,1,0:T(8,128)(2,1)} %get-tuple-element.27) | copy-start | bytes 12582916
  349.7 13.5 %copy-start.9 = (bf16[8,128,1024]{2,1,0:T(8,128)(2,1)S(1)}, bf16[8,128,1024]{2,1,0:T(8,128)(2,1)}, u32[]{:S(2)}) copy-start(bf16[8,128,1024]{2,1,0:T(8,128)(2,1)} %copy-done.8) | copy-start | bytes 6291460
  419.5 34.8 %copy-start.17 = (f32[8,128]{1,0:T(8,128)S(1)}, f32[8,128]{1,0:T(8,128)}, u32[]{:S(2)}) copy-start(f32[8,128]{1,0:T(8,128)} %copy-done.16) | copy-start | bytes 12292
  419.6 34.8 %copy-start.15 = (f32[1024]{0:T(1024)S(1)}, f32[1024]{0:T(1024)}, u32[]{:S(2)}) copy-start(f32[1024]{0:T(1024)} %copy-done.14) | copy-start | bytes 12292
  467.7 500.6 %all-to-all-start.3 = ((bf16[8,128,2048]{2,1,0:T(8,128)(2,1)}), bf16[8,128,2048]{2,1,0:T(8,128)(2,1)}, u32[]{:S(2)}, u32[]{:S(2)}) async-start(bf16[8,128,2048]{2,1,0:T(8,128)(2,1)} %bitcast.91), calls=%async_computation.3 | async-start | bytes 8388608 | tf_op jit(solution)/shard_map/all_to_all | solution.py:434
  (13 other events, 73.2 us)
Sparse Core Ops, SparseCore 0:
  396.1 288.3 all-reduce.1

commit v2 on v1

--- a/solution.py
+++ b/solution.py
@@ -31,7 +31,7 @@
     return op(x.reshape(x.shape[0] // 8, 8, x.shape[1]), axis=0)
 
 
-def attention_kernel(n_blk, half, kind_ref, core_ref, qa, ka, va, ga, qb, kb, vb, gb, oa, ob, dg,
+def attention_kernel(n_blk, half, kind_ref, core_ref, qa, ka, va, ga, qb, kb, vb, gb, oa, ob, da, db, bias,
                      qs, ks, vs, gs, kt, vt, s_scr, dp_scr, dk_scr, dv_scr, out_scr):
     head = pl.program_id(0)
     qi = pl.program_id(1)
@@ -51,6 +51,7 @@
             kt[c] = jnp.transpose(ks[c])
             vt[c] = jnp.transpose(vs[c])
         dk_scr[...] = jnp.zeros_like(dk_scr)
+        bias[...] = jnp.zeros_like(bias)
         dv_scr[...] = jnp.zeros_like(dv_scr)
 
     def process(chunks, band_first):
@@ -113,43 +114,49 @@
     def _():
         process([qi - 2, qi - 1, qi], True)
 
+    def add_bias(part, v):
+        bias[part] += fold(v.astype(jnp.float32), jnp.sum)
+
+    add_bias(0, out_scr[1])
     oa[qi] = out_scr[0, pl.ds(at_a, half), :]
     ob[qi] = out_scr[0, pl.ds(at_b, half), :]
-    dg[0, 0, qi] = out_scr[1, pl.ds(at_a, half), :]
-    dg[0, 1, qi] = out_scr[1, pl.ds(at_b, half), :]
+    da[0, qi] = out_scr[1, pl.ds(at_a, half), :]
+    db[0, qi] = out_scr[1, pl.ds(at_b, half), :]
 
     @pl.when(qi == n_blk - 1)
     def _():
         for c in range(n_blk):
             out_scr[0] = (dk_scr[c] * scale).astype(jnp.bfloat16)
             out_scr[1] = dv_scr[c].astype(jnp.bfloat16)
-            dg[1, 0, c] = out_scr[0, pl.ds(at_a, half), :]
-            dg[1, 1, c] = out_scr[0, pl.ds(at_b, half), :]
-            dg[2, 0, c] = out_scr[1, pl.ds(at_a, half), :]
-            dg[2, 1, c] = out_scr[1, pl.ds(at_b, half), :]
+            add_bias(1, out_scr[0])
+            add_bias(2, out_scr[1])
+            da[1, c] = out_scr[0, pl.ds(at_a, half), :]
+            db[1, c] = out_scr[0, pl.ds(at_b, half), :]
+            da[2, c] = out_scr[1, pl.ds(at_a, half), :]
+            db[2, c] = out_scr[1, pl.ds(at_b, half), :]
 
 
 def attention(kinds, core, qkv_own, do_own, qkv_oth, do_oth):
-    n_blk, half, _ = qkv_own.shape
+    _, n_blk, half, wide = qkv_own.shape
     heads = kinds.shape[0]
-    dim = 128
+    dim = wide // heads
     blk = 2 * half
 
-    def own(part):
-        return pl.BlockSpec((n_blk, half, dim), lambda h, i, kind, cr: (0, 0, part * 2 * heads + cr[0] * heads + h))
-
-    out3 = pl.BlockSpec((n_blk, half, dim), lambda h, i, kind, cr: (0, 0, h))
-    out5 = pl.BlockSpec((3, 2, n_blk, half, dim), lambda h, i, kind, cr: (0, 0, 0, 0, h))
+    def part(t):
+        return pl.BlockSpec((None, n_blk, half, dim), lambda h, i, kind, cr: (t, 0, 0, h))
+
+    one = pl.BlockSpec((n_blk, half, dim), lambda h, i, kind, cr: (0, 0, h))
+    three = pl.BlockSpec((3, n_blk, half, dim), lambda h, i, kind, cr: (0, 0, 0, h))
+    sums = pl.BlockSpec((None, 3, 8, dim), lambda h, i, kind, cr: (h, 0, 0, 0))
     bf = jnp.bfloat16
-    wide = heads * dim
     flops = 6 * 2 * heads * (n_blk * blk) ** 2 * dim // 2
     return pl.pallas_call(
         functools.partial(attention_kernel, n_blk, half),
         grid_spec=pltpu.PrefetchScalarGridSpec(
             num_scalar_prefetch=2,
             grid=(heads, n_blk),
-            in_specs=[own(0), own(1), own(2), own(0), out3, out3, out3, out3],
-            out_specs=[out3, out3, out5],
+            in_specs=[part(0), part(1), part(2), one, part(0), part(1), part(2), one],
+            out_specs=[one, one, three, three, sums],
             scratch_shapes=[pltpu.VMEM((n_blk, blk, dim), bf)] * 4
             + [pltpu.VMEM((n_blk, dim, blk), bf)] * 2
             + [pltpu.VMEM((n_blk, blk, blk), jnp.float32), pltpu.VMEM((n_blk, blk, blk), bf)]
@@ -157,13 +164,148 @@
             + [pltpu.VMEM((2, blk, dim), bf)],
         ),
         out_shape=[jax.ShapeDtypeStruct((n_blk, half, wide), bf)] * 2
-        + [jax.ShapeDtypeStruct((3, 2, n_blk, half, wide), bf)],
+        + [jax.ShapeDtypeStruct((3, n_blk, half, wide), bf)] * 2
+        + [jax.ShapeDtypeStruct((heads, 3, 8, dim), jnp.float32)],
         compiler_params=pltpu.CompilerParams(
             dimension_semantics=("arbitrary", "arbitrary"), vmem_limit_bytes=48 * 1024 * 1024
         ),
         cost_estimate=pl.CostEstimate(flops=flops, bytes_accessed=40 * 2**20, transcendentals=heads * (n_blk * blk) ** 2 // 2),
         name="attention_fwd_bwd",
-    )(kinds, core, qkv_own, qkv_own, qkv_own, do_own, *qkv_oth, do_oth)
+    )(kinds, core, qkv_own, qkv_own, qkv_own, do_own, qkv_oth, qkv_oth, qkv_oth, do_oth)
+
+
+def matmul_call(body, scalars, grid, ins, outs, out_shape, flops):
+    args = [a for a, _ in ins]
+    moved = sum(a.size * a.dtype.itemsize for a in args)
+    return pl.pallas_call(
+        body,
+        grid_spec=pltpu.PrefetchScalarGridSpec(
+            num_scalar_prefetch=len(scalars), grid=grid, in_specs=[spec for _, spec in ins], out_specs=outs),
+        out_shape=out_shape,
+        compiler_params=pltpu.CompilerParams(
+            dimension_semantics=("arbitrary",) * len(grid), vmem_limit_bytes=56 * 1024 * 1024),
+        cost_estimate=pl.CostEstimate(flops=flops, bytes_accessed=moved, transcendentals=0),
+    )(*scalars, *args)
+
+
+def project_qkv(h, w, bias, group):
+    n_tok, d_model = h.shape
+    wide = d_model // 2
+    tile = wide // 2
+
+    def body(g, h_ref, w_ref, b_ref, out):
+        out[...] = (dot_nn(h_ref[...], w_ref[...]) + b_ref[...].astype(jnp.float32)).astype(jnp.bfloat16)
+
+    def cols(t, j, g):
+        return (0, t * 4 + g[0] * 2 + j)
+
+    return matmul_call(
+        body, [group], (3, 2),
+        [(h, pl.BlockSpec((n_tok, d_model), lambda t, j, g: (0, 0))),
+         (w, pl.BlockSpec((d_model, tile), cols)), (bias, pl.BlockSpec((1, tile), cols))],
+        pl.BlockSpec((None, n_tok, tile), lambda t, j, g: (t, 0, j)),
+        jax.ShapeDtypeStruct((3, n_tok, wide), jnp.bfloat16), 6 * n_tok * d_model * wide)
+
+
+def project_do(dy, w, group):
+    n_tok, d_model = dy.shape
+    wide = d_model // 2
+    tile = wide // 2
+
+    def body(g, dy_ref, w_ref, out):
+        out[...] = dot_nt(dy_ref[...], w_ref[...]).astype(jnp.bfloat16)
+
+    return matmul_call(
+        body, [group], (2,),
+        [(dy, pl.BlockSpec((n_tok, d_model), lambda j, g: (0, 0))),
+         (w, pl.BlockSpec((tile, d_model), lambda j, g: (g[0] * 2 + j, 0)))],
+        pl.BlockSpec((n_tok, tile), lambda j, g: (0, j)),
+        jax.ShapeDtypeStruct((n_tok, wide), jnp.bfloat16), 2 * n_tok * d_model * wide)
+
+
+def out_weight_grad(o_own, o_oth, dy, core):
+    n_tok, d_model = dy.shape
+    wide = d_model // 2
+    tile = wide // 2
+
+    def body(c, own, oth, dy_ref, out):
+        @pl.when(pl.program_id(0) == 0)
+        def _():
+            out[...] = dot_nn(jnp.transpose(own[...]), dy_ref[...])
+
+        @pl.when(pl.program_id(0) == 1)
+        def _():
+            out[...] = dot_nn(jnp.transpose(oth[...]), dy_ref[...])
+
+    return matmul_call(
+        body, [core], (2, 2),
+        [(o_own, pl.BlockSpec((n_tok, tile), lambda s, j, c: (0, j * (1 - s) + s))),
+         (o_oth, pl.BlockSpec((n_tok, tile), lambda s, j, c: (0, j * s))),
+         (dy, pl.BlockSpec((n_tok, d_model), lambda s, j, c: (0, 0)))],
+        pl.BlockSpec((tile, d_model), lambda s, j, c: (((1 - s) * c[0] + s * (1 - c[0])) * 2 + j, 0)),
+        jax.ShapeDtypeStruct((d_model, d_model), jnp.float32), 2 * n_tok * d_model * d_model)
+
+
+def project_out(x, o_own, o_oth, w, bias, core):
+    n_tok, d_model = x.shape
+    wide = d_model // 2
+    tile = d_model // 4
+
+    def body(c, x_ref, own, oth, w_own, w_oth, b_ref, out):
+        y = dot_nn(own[...], w_own[...]) + dot_nn(oth[...], w_oth[...])
+        out[...] = (x_ref[...].astype(jnp.float32) + y + b_ref[...].astype(jnp.float32)).astype(jnp.bfloat16)
+
+    whole = pl.BlockSpec((n_tok, wide), lambda j, c: (0, 0))
+    return matmul_call(
+        body, [core], (4,),
+        [(x, pl.BlockSpec((n_tok, tile), lambda j, c: (0, j))), (o_own, whole), (o_oth, whole),
+         (w, pl.BlockSpec((wide, tile), lambda j, c: (c[0], j))), (w, pl.BlockSpec((wide, tile), lambda j, c: (1 - c[0], j))),
+         (bias, pl.BlockSpec((1, tile), lambda j, c: (0, j)))],
+        pl.BlockSpec((n_tok, tile), lambda j, c: (0, j)),
+        jax.ShapeDtypeStruct((n_tok, d_model), jnp.bfloat16), 2 * n_tok * d_model * d_model)
+
+
+def hidden_grad(dg_own, dg_oth, w, core):
+    _, n_tok, wide = dg_own.shape
+    d_model = 2 * wide
+    tile = d_model // 8
+
+    def body(c, own, oth, *refs):
+        out = refs[-1]
+        total = None
+        for t in range(3):
+            for src, w_ref in ((own, refs[t]), (oth, refs[3 + t])):
+                one = dot_nt(src[t], w_ref[...])
+                total = one if total is None else total + one
+        out[...] = total.astype(jnp.bfloat16)
+
+    whole = pl.BlockSpec((3, n_tok, wide), lambda j, c: (0, 0, 0))
+
+    def col(t, mine):
+        return pl.BlockSpec((tile, wide), lambda j, c: (j, 2 * t + (c[0] if mine else 1 - c[0])))
+
+    return matmul_call(
+        body, [core], (8,),
+        [(dg_own, whole), (dg_oth, whole)] + [(w, col(t, True)) for t in range(3)] + [(w, col(t, False)) for t in range(3)],
+        pl.BlockSpec((n_tok, tile), lambda j, c: (0, j)),
+        jax.ShapeDtypeStruct((n_tok, d_model), jnp.bfloat16), 12 * n_tok * wide * d_model)
+
+
+def qkv_weight_grad(h_own, h_oth, dg_own, dg_oth):
+    n_tok, d_model = h_own.shape
+    wide = d_model // 2
+    tile = d_model // 4
+
+    def body(ha, hb, da, db, out):
+        out[...] = dot_nn(jnp.transpose(ha[...]), da[...]) + dot_nn(jnp.transpose(hb[...]), db[...])
+
+    h_spec = pl.BlockSpec((n_tok, tile), lambda t, i: (0, i))
+    d_spec = pl.BlockSpec((None, n_tok, wide), lambda t, i: (t, 0, 0))
+    return matmul_call(
+        body, [], (3, 4),
+        [(h_own, h_spec), (h_oth, h_spec), (dg_own, d_spec), (dg_oth, d_spec)],
+        pl.BlockSpec((None, tile, wide), lambda t, i: (t, i, 0)),
+        jax.ShapeDtypeStruct((3, d_model, wide), jnp.float32), 12 * n_tok * d_model * wide)
 
 
 def copy_kernel(*refs):
@@ -193,7 +335,7 @@
     )(*args)
 
 
-def grad_sum_kernel(n_chip, rows, g0, g1, g2, small, out, small_out, acc, rc, rb, ra, slots, load_sem, loc_sem,
+def grad_sum_kernel(n_chip, rows, g_all, small, out, small_out, acc, rc, rb, ra, slots, load_sem, loc_sem,
                     c_send, c_recv, b_send, b_recv, a_send, a_recv, g_send, g_recv, s_send, s_recv, v_send, v_recv):
     chip = lax.axis_index("chip")
     core = lax.axis_index("core")
@@ -201,7 +343,7 @@
     me = chip * 2 + core
     bits = [chip % 2, (chip // 2) % 2, chip // 4]
     beside = [chip + (1 - 2 * bits[d]) * (1 << d) for d in range(3)]
-    parts = (g0, g1, g2)
+    parts = [g_all.at[t] for t in range(3)]
     chunk = rows // 8
     wide = acc.shape[2]
     mesh_id = pl.DeviceIdType.MESH
@@ -343,8 +485,8 @@
         store.wait()
 
 
-def grad_sum(n_chip, g_parts, small):
-    rows, wide = g_parts[0].shape
+def grad_sum(n_chip, g_all, small):
+    _, rows, wide = g_all.shape
     chunk = rows // 8
     n_dev = 2 * n_chip
     f32 = jnp.float32
@@ -353,7 +495,7 @@
     vmem = pl.BlockSpec(memory_space=pltpu.VMEM)
     return pl.pallas_call(
         functools.partial(grad_sum_kernel, n_chip, rows),
-        in_specs=[hbm, hbm, hbm, vmem],
+        in_specs=[hbm, vmem],
         out_specs=[hbm, vmem],
         out_shape=[jax.ShapeDtypeStruct((rows, 6 * wide), f32), jax.ShapeDtypeStruct(small.shape, f32)],
         scratch_shapes=[
@@ -366,7 +508,7 @@
         compiler_params=pltpu.CompilerParams(collective_id=0, has_side_effects=True, vmem_limit_bytes=44 * 1024 * 1024),
         cost_estimate=pl.CostEstimate(flops=3 * 10**11, bytes_accessed=150 * 2**20, transcendentals=0),
         name="grad_sum",
-    )(*g_parts, small)
+    )(g_all, small)
 
 
 def solution(mesh):
@@ -391,52 +533,49 @@
         def swap(v):
             return lax.ppermute(v, "core", swap_pairs)
 
-        def other_half(v, part):
-            lo = v[:, part * d_model:part * d_model + wide]
-            hi = v[:, part * d_model + wide:(part + 1) * d_model]
-            return jnp.where(core == 0, hi, lo).reshape(n_chip, half, wide)
-
-        def by_core(mine, theirs):
-            return jnp.where(core == 0, mine, theirs), jnp.where(core == 0, theirs, mine)
-
         x_b = lax.all_to_all(x, "chip", 0, 0, tiled=True).reshape(n_tok, d_model)
         g_b = lax.all_to_all(d_y, "chip", 0, 0, tiled=True).reshape(n_tok, d_model)
+
+        other_arr = 1 - core_arr
+        blocks = (3, n_chip, half, wide)
 
         x_f = x_b.astype(f32)
         h_f, ln_pull = jax.vjp(layer_norm, x_f, ln_gamma.astype(f32), ln_beta.astype(f32))
         h_norm = h_f.astype(bf)
-        h_all = jnp.concatenate([h_norm, swap(h_norm)], axis=0)
-        qkv = (dot_nn(h_norm, w_qkv) + b_qkv.astype(f32)).astype(bf)
-        qkv_own = qkv.reshape(n_chip, half, 3 * d_model)
-        qkv_oth = [swap(other_half(qkv, part)) for part in range(3)]
-        d_attn = dot_nt(g_b, w_out).astype(bf)
-        do_own = d_attn.reshape(n_chip, half, d_model)
-        do_oth = swap(other_half(d_attn, 0))
-
-        o_own, o_send, dg = attention(my_kinds, core_arr, qkv_own, do_own, qkv_oth, do_oth)
-        o_recv = swap(o_send)
-        dg_own = dg[:, 0]
-        dg_recv = swap(dg[:, 1])
-
-        o_lo, o_hi = by_core(o_own, o_recv)
-        attn_tok = jnp.concatenate([o_lo.reshape(n_tok, wide), o_hi.reshape(n_tok, wide)], axis=1)
-        d_wout = lax.dot_general(attn_tok, g_b, (((0,), (0,)), ((), ())), preferred_element_type=f32)
-        d_wout, dg_own, dg_recv = lax.optimization_barrier((d_wout, dg_own, dg_recv))
+        bias_row = b_qkv.reshape(1, 3 * d_model)
+        qkv_send = project_qkv(h_norm, w_qkv, bias_row, other_arr)
+        qkv_oth = swap(qkv_send)
+        qkv_own = project_qkv(h_norm, w_qkv, bias_row, core_arr)
+        g_b, qkv_own = lax.optimization_barrier((g_b, qkv_own))
+        do_oth = swap(project_do(g_b, w_out, other_arr))
+        do_own = project_do(g_b, w_out, core_arr)
+        h_oth = swap(h_norm)
+
+        o_own, o_send, dg_own, dg_send, bias_sums = attention(
+            my_kinds, core_arr, qkv_own.reshape(blocks), do_own.reshape(blocks[1:]),
+            qkv_oth.reshape(blocks), do_oth.reshape(blocks[1:]))
+        o_oth = swap(o_send).reshape(n_tok, wide)
+        dg_oth = swap(dg_send).reshape(3, n_tok, wide)
+        o_own = o_own.reshape(n_tok, wide)
+        dg_own = dg_own.reshape(3, n_tok, wide)
+        dg_send = dg_send.reshape(3, n_tok, wide)
+
+        d_wout = out_weight_grad(o_own, o_oth, g_b, core_arr)
+        d_wout, dg_own, dg_oth = lax.optimization_barrier((d_wout, dg_own, dg_oth))
         d_wout = lax.psum(d_wout, ("chip", "core"))
-        y_b = (x_f + dot_nn(attn_tok, w_out) + b_out.astype(f32)).astype(bf)
+        y_b = project_out(x_b, o_own, o_oth, w_out, b_out.reshape(1, d_model), core_arr)
         y_out = lax.all_to_all(y_b.reshape(n_chip, half, d_model), "chip", 0, 0, tiled=True)
 
-        dg_lo, dg_hi = by_core(dg_own.reshape(3, n_tok, wide), dg_recv.reshape(3, n_tok, wide))
-        d_qkv = jnp.concatenate([dg_lo[0], dg_hi[0], dg_lo[1], dg_hi[1], dg_lo[2], dg_hi[2]], axis=1)
-        d_h = dot_nt(d_qkv, w_qkv).astype(bf).astype(f32)
+        d_h = hidden_grad(dg_own, dg_oth, w_qkv, core_arr)
+        d_h = d_h.astype(f32)
         d_x_ln, d_gamma, d_beta = ln_pull(d_h)
         d_x_b = (g_b.astype(f32) + d_x_ln).astype(bf)
         d_x = lax.all_to_all(d_x_b.reshape(n_chip, half, d_model), "chip", 0, 0, tiled=True)
-        d_bqkv = jnp.sum(d_qkv, axis=0, dtype=f32)
+        bias_mine = jnp.sum(bias_sums, axis=2).transpose(1, 0, 2).reshape(3, 1, wide)
+        d_bqkv = jnp.where(lax.broadcasted_iota(jnp.int32, (3, 2, wide), 1) == core, bias_mine, 0.0).reshape(3 * d_model)
         d_bout = jnp.sum(g_b, axis=0, dtype=f32)
 
-        dg_tok = dg.reshape(3, 2 * n_tok, wide)
-        d_w = [lax.dot_general(h_all, dg_tok[t], (((0,), (0,)), ((), ())), preferred_element_type=f32) for t in range(3)]
+        d_w = qkv_weight_grad(h_norm, h_oth, dg_own, dg_send)
         small = jnp.concatenate([d_gamma, d_beta, d_bqkv, d_bout]).reshape(-1, 128)
         d_wqkv, small = grad_sum(n_chip, d_w, small)
         d_wqkv = place(d_wqkv, d_model, 0)

time: 1000 us -> 965 us (0.965)
  matrix products: 146 us -> 0 us
  Pallas kernels: 610 us -> 745 us
  waiting for transfers between devices: 54 us -> 129 us
  blocking collectives: 59 us -> 0 us
  local copies, waits for them, and re-layouts: 49 us -> 7.1 us
  starting transfers between devices: 16.5 us -> 30.6 us
  other arithmetic: 41.7 us -> 31.3 us
    pallas_call x0 -> x8, Pallas kernels: none -> 154 us  [matmul_call(): pl.pallas_call(body, grid_spec=pltpu.PrefetchScalarGridSpec(num_scalar_pr...]
    dot_general x8 -> x0, matrix products: 146 us -> none  [the longest x2 47.3 us: dot_nt(): lax.dot_general(a, b, (((1,), (1,)), ((), ())), preferred_element_type=jn...]
    all_to_all x1 -> x0, blocking collectives: 59 us -> none  [local_block(): x_b = lax.all_to_all(x, 'chip', 0, 0, tiled=True).reshape(n_tok, d_model)]
    all_to_all x0 -> x1, waiting for transfers between devices: none -> 51.8 us  [local_block(): x_b = lax.all_to_all(x, 'chip', 0, 0, tiled=True).reshape(n_tok, d_model)]
    all_to_all x1, waiting for transfers between devices: 0.01 us -> 38.3 us  [local_block(): lax.all_to_all(y_b.reshape(n_chip, half, d_model), 'chip', 0, 0, tiled=True)]
    pallas_call x1, Pallas kernels: 454 us -> 433 us  [grad_sum(): pl.pallas_call(functools.partial(grad_sum_kernel, n_chip, rows), in_specs...]
    unnamed x57 -> x19, local copies, waits for them, and re-layouts: 21.4 us -> 4.58 us
    squeeze x2 -> x0, local copies, waits for them, and re-layouts: 13.1 us -> none  [the longest x1 6.58 us: local_block(): dg_own = dg[:, 0]]
  transfers between devices with their start and end apart: 11 -> 10, of which waited for: 4 -> 4; matrix products, arithmetic and copies ran while one was open for 21% -> 2% of each run, Pallas kernels for 50% -> 64%
where the time goes in v2:
time: 965 us; the launch traced here: 958 us
  Pallas kernels  745 us (77%)
  waiting for transfers between devices  129 us (13%)
  other arithmetic  31.3 us (3%)
  starting transfers between devices  30.6 us (3%)
  between operations  14.4 us (1%)
    pallas_call x1, Pallas kernels, grad_sum(): pl.pallas_call(functools.partial(grad_sum_kernel, n_chip, rows), in_specs...  433 us
    pallas_call x8, Pallas kernels, matmul_call(): pl.pallas_call(body, grid_spec=pltpu.PrefetchScalarGridSpec(num_scalar_pr...  154 us
    pallas_call x1, Pallas kernels, attention(): pl.pallas_call(functools.partial(attention_kernel, n_blk, half), grid_spe...  103 us
    pallas_call x4, Pallas kernels, place(): pl.pallas_call(copy_kernel, grid=(rows // tile,), in_specs=in_specs, out_...  55.2 us
    all_to_all x1, waiting for transfers between devices, local_block(): x_b = lax.all_to_all(x, 'chip', 0, 0, tiled=True).reshape(n_tok, d_model)  51.8 us
    all_to_all x1, waiting for transfers between devices, local_block(): lax.all_to_all(y_b.reshape(n_chip, half, d_model), 'chip', 0, 0, tiled=True)  38.3 us
    all_to_all x1, waiting for transfers between devices, local_block(): g_b = lax.all_to_all(d_y, 'chip', 0, 0, tiled=True).reshape(n_tok, d_model)  35.8 us
  transfers between devices with their start and end apart: 10, of which 4 were waited for; matrix products, arithmetic and copies ran while one was open for 2% of the time, Pallas kernels for 64%

profile of v2, /device:TPU:0, one launch (start us, length us, event | category | flops | bytes accessed | tf_op | source)
XLA Modules:
  0.0 957.5 jit_solution(5054667570847085865)
XLA Ops:
  7.2 6.6 all-to-all-start
  14.5 51.8 %all-to-all-done = bf16[8,128,2048]{2,1,0:T(8,128)(2,1)} async-done(((bf16[8,128,2048]{2,1,0:T(8,128)(2,1)}), bf16[8,128,2048]{2,1,0:T(8,128)(2,1)}, u32[]{:S(2)}, u32[]{:S(2)}) %all-to-all-start) | async-done | bytes 4194336 | tf_op jit(solution)/shard_map/all_to_all | solution.py:536
  72.5 4.6 add_convert_fusion.h_ref.ha
  77.1 18.0 %shard_map.154 = bf16[3,1024,1024]{2,1,0:T(8,128)(2,1)} custom-call(s32[1]{0:T(128)S(6)} %sub.20.g, bf16[1024,2048]{1,0:T(8,128)(2,1)} %add_convert_fusion.h_ref.ha, bf16[2048,6144]{1,0:T(8,128)(2,1)} %refs_5_.1, bf16[1,6144]{1,0:T(2,128)(2,1)} %reshape.141.b_ref), custom_call_target="tpu_custom_call" | custom-call | flops 12884901888 | bytes 29372416 | tf_op jit(solution)/shard_map/pallas_call | solution.py:180
  95.1 7.4 all-to-all-start.1
  102.5 18.0 %shard_map.152 = bf16[3,1024,1024]{2,1,0:T(8,128)(2,1)} custom-call(s32[1]{0:T(128)} %bitcast.g.core_ref.c, bf16[1024,2048]{1,0:T(8,128)(2,1)} %add_convert_fusion.h_ref.ha, bf16[2048,6144]{1,0:T(8,128)(2,1)} %refs_5_.1, bf16[1,6144]{1,0:T(2,128)(2,1)} %reshape.141.b_ref), custom_call_target="tpu_custom_call" | custom-call | flops 12884901888 | bytes 29372416 | tf_op jit(solution)/shard_map/pallas_call | solution.py:180
  120.5 35.8 %all-to-all-done.1 = bf16[8,128,2048]{2,1,0:T(8,128)(2,1)} async-done(((bf16[8,128,2048]{2,1,0:T(8,128)(2,1)}), bf16[8,128,2048]{2,1,0:T(8,128)(2,1)}, u32[]{:S(2)}, u32[]{:S(2)}) %all-to-all-start.1) | async-done | bytes 4194336 | tf_op jit(solution)/shard_map/all_to_all | solution.py:537
  156.3 8.6 shard_map.155
  165.0 8.5 shard_map.153
  174.8 103.0 %attention_fwd_bwd.1 = (bf16[8,128,1024]{2,1,0:T(8,128)(2,1)S(1)}, bf16[8,128,1024]{2,1,0:T(8,128)(2,1)S(1)}, bf16[3,8,128,1024]{3,2,1,0:T(8,128)(2,1)}, bf16[3,...) custom-call(s32[8]{0:T(128)S(1)} %dynamic_slice.3.kind_ref, s32[1]{0:T(128)} %bitcast.g.core_ref.c, ...), custom_call_target="tpu_custom_call" | custom-call | flops 25769803776 | bytes 41943040 | tf_op jit(solution)/shard_map/attention_fwd_bwd/pallas_call | solution.py:153
  284.7 14.0 %shard_map.156 = bf16[1024,2048]{1,0:T(8,128)(2,1)} custom-call(s32[1]{0:T(128)} %bitcast.g.core_ref.c, bf16[1024,2048]{1,0:T(8,128)(2,1)} %bitcast.1.x_ref, bf16[1024,1024]{1,0:T(8,128)(2,1)} %bitcast.52, bf16[1024,1024]{1,0:T(8,128)(2,1)} %bitcast.63, bf16[2048,2048]{1,0:T(8,128)(2,1)} %w_oth.1, bf16[2048,2048]{1,0:T(8,128)(2,1)} %w_oth.1, ...), custom_call_target="tpu_custom_call" | custom-call | flops 8589934592 | bytes 25169920 | tf_op jit(solution)/shard_map/pallas_call | solution.py:180
  298.7 7.5 all-to-all-start.2
  306.4 14.5 %shard_map.157 = f32[2048,2048]{1,0:T(8,128)} custom-call(s32[1]{0:T(128)} %bitcast.g.core_ref.c, bf16[1024,1024]{1,0:T(8,128)(2,1)} %bitcast.53, bf16[1024,1024]{1,0:T(8,128)(2,1)} %bitcast.64, bf16[1024,2048]{1,0:T(8,128)(2,1)} %bitcast.2.dy_ref), custom_call_target="tpu_custom_call" | custom-call | flops 8589934592 | bytes 8388608 | tf_op jit(solution)/shard_map/pallas_call | solution.py:180
  321.0 38.3 %all-to-all-done.2 = bf16[8,128,2048]{2,1,0:T(8,128)(2,1)} async-done(((bf16[8,128,2048]{2,1,0:T(8,128)(2,1)}), bf16[8,128,2048]{2,1,0:T(8,128)(2,1)}, u32[]{:S(2)}, u32[]{:S(2)}) %all-to-all-start.2) | async-done | bytes 4194336 | tf_op jit(solution)/shard_map/all_to_all | solution.py:567
  363.1 34.9 %shard_map.158 = bf16[1024,2048]{1,0:T(8,128)(2,1)} custom-call(s32[1]{0:T(128)} %bitcast.g.core_ref.c, bf16[3,1024,1024]{2,1,0:T(8,128)(2,1)} %bitcast.55, bf16[3,1024,1024]{2,1,0:T(8,128)(2,1)} %bitcast.15.oth, bf16[2048,6144]{1,0:T(8,128)(2,1)} %refs_5_.1, bf16[2048,6144]{1,0:T(8,128)(2,1)} %refs_5_.1, bf16[2048,6144]{1,0:T(8,128)(2,1)} %refs_5_.1, ...), custom_call_target="tpu_custom_call" | custom-call | flops 25769803776 | bytes 163577856 | tf_op jit(solution)/shard_map/pallas_call | solution.py:180
  398.0 4.8 fusion.2
  403.4 6.3 fusion.6
  409.7 9.2 convert_reduce_fusion.1
  418.9 8.6 all-to-all-start.3
  427.5 37.3 %shard_map.159.g_all = f32[3,2048,1024]{2,1,0:T(8,128)} custom-call(bf16[1024,2048]{1,0:T(8,128)(2,1)} %add_convert_fusion.h_ref.ha, bf16[1024,2048]{1,0:T(8,128)(2,1)} %collective-permute-done.4.hb, bf16[3,1024,1024]{2,1,0:T(8,128)(2,1)} %bitcast.56, bf16[3,1024,1024]{2,1,0:T(8,128)(2,1)} %bitcast.62), custom_call_target="tpu_custom_call" | custom-call | flops 25769803776 | bytes 20971520 | tf_op jit(solution)/shard_map/pallas_call | solution.py:180
  464.8 433.0 %grad_sum.1 = (f32[2048,6144]{1,0:T(8,128)}, f32[96,128]{1,0:T(8,128)S(1)}) custom-call(f32[3,2048,1024]{2,1,0:T(8,128)} %shard_map.159.g_all, f32[96,128]{1,0:T(8,128)S(1)} %maximum_bitcast_fusion.small), custom_call_target="tpu_custom_call" | custom-call | flops 299999985664 | bytes 157286400 | tf_op jit(solution)/shard_map/grad_sum/pallas_call | solution.py:496
  897.8 36.3 %place_rows.6 = f32[2048,6144]{1,0:T(8,128)} custom-call(f32[2048,6144]{1,0:T(8,128)} %get-tuple-element.30.refs_0_), custom_call_target="tpu_custom_call" | custom-call | flops 100663296 | bytes 100663296 | tf_op jit(solution)/shard_map/place_rows/pallas_call | solution.py:326
  935.3 3.7 place_rows.5
  939.0 11.4 %place_rows.7 = f32[2048,2048]{1,0:T(8,128)} custom-call(f32[2048,2048]{1,0:T(8,128)} %all-reduce.2.cloned.1.call-done.refs_0_), custom_call_target="tpu_custom_call" | custom-call | flops 33554432 | bytes 33554432 | tf_op jit(solution)/shard_map/place_rows/pallas_call | solution.py:326
  (51 shorter events, 20.9 us)
Async XLA Ops:
  7.2 6.6 copy-start.3
  7.2 6.6 copy-start.4
  7.2 6.6 copy-start.2
  7.2 59.1 %all-to-all-start = ((bf16[8,128,2048]{2,1,0:T(8,128)(2,1)}), bf16[8,128,2048]{2,1,0:T(8,128)(2,1)}, u32[]{:S(2)}, u32[]{:S(2)}) async-start(bf16[8,128,2048]{2,1,0:T(8,128)(2,1)} %param.9), calls=%async_computation | async-start | bytes 8388608 | tf_op jit(solution)/shard_map/all_to_all | solution.py:536
  95.1 78.4 %collective-permute-start = (bf16[3,1024,1024]{2,1,0:T(8,128)(2,1)}, bf16[3,1024,1024]{2,1,0:T(8,128)(2,1)}, u32[]{:S(2)}, u32[]{:S(2)}) collective-permute-start(bf16[3,1024,1024]{2,1,0:T(8,128)(2,1)} %shard_map.154), channel_id=1, source_target_pairs={{0,1},{1,0},{2,3},{3,2},{4,5},{5,4},{6,7},{7,6},{8,9},{9,8},{10,11... | collective-permute-start | bytes 18874376 | tf_op jit(solution)/shard_map/ppermute | solution.py:534
  95.1 61.1 %all-to-all-start.1 = ((bf16[8,128,2048]{2,1,0:T(8,128)(2,1)}), bf16[8,128,2048]{2,1,0:T(8,128)(2,1)}, u32[]{:S(2)}, u32[]{:S(2)}) async-start(bf16[8,128,2048]{2,1,0:T(8,128)(2,1)} %param.10), calls=%async_computation.1 | async-start | bytes 8388608 | tf_op jit(solution)/shard_map/all_to_all | solution.py:537
  120.5 44.4 %copy-start.8 = (s32[16]{0:T(128)S(1)}, s32[16]{0:T(128)}, u32[]{:S(2)}) copy-start(s32[16]{0:T(128)} %param.17) | copy-start | bytes 196
  164.9 8.6 collective-permute-start.1
  173.5 1.3 copy-start.7
  174.8 104.9 %copy-start.5 = (bf16[2048]{0:T(1024)(128)(2,1)S(1)}, bf16[2048]{0:T(1024)(128)(2,1)}, u32[]{:S(2)}) copy-start(bf16[2048]{0:T(1024)(128)(2,1)} %param.16) | copy-start | bytes 12292
  277.9 1.3 copy-start
  279.2 4.2 collective-permute-start.2
  279.2 83.8 %collective-permute-start.3 = (bf16[3,8,128,1024]{3,2,1,0:T(8,128)(2,1)}, bf16[3,8,128,1024]{3,2,1,0:T(8,128)(2,1)}, u32[]{:S(2)}, u32[]{:S(2)}) collective-permute-start(bf16[3,8,128,1024]{3,2,1,0:T(8,128)(2,1)} %get-tuple-element.25), channel_id=1, source_target_pairs={{0,1},{1,0},{2,3},{3,2},{4,5},{5,4},{6,7},{7,6},{8,9},{9,8},{10,11... | collective-permute-start | bytes 18874376 | tf_op jit(solution)/shard_map/ppermute | solution.py:534
  283.4 1.4 copy-start.6
  298.7 60.6 %all-to-all-start.2 = ((bf16[8,128,2048]{2,1,0:T(8,128)(2,1)}), bf16[8,128,2048]{2,1,0:T(8,128)(2,1)}, u32[]{:S(2)}, u32[]{:S(2)}) async-start(bf16[8,128,2048]{2,1,0:T(8,128)(2,1)} %bitcast.58), calls=%async_computation.2 | async-start | bytes 8388608 | tf_op jit(solution)/shard_map/all_to_all | solution.py:567
  306.2 632.8 %all-reduce.2.cloned.1.call-start = ((), (), s32[]{:S(2)}) async-start(), calls=%async_computation.4 | async-start | bytes 33554432 | tf_op jit(solution)/shard_map/psum | solution.py:565
  306.3 121.2 %collective-permute-start.4 = (bf16[1024,2048]{1,0:T(8,128)(2,1)}, bf16[1024,2048]{1,0:T(8,128)(2,1)}, u32[]{:S(2)}, u32[]{:S(2)}) collective-permute-start(bf16[1024,2048]{1,0:T(8,128)(2,1)} %add_convert_fusion.h_ref.ha), channel_id=1, source_target_pairs={{0,1},{1,0},{2,3},{3,2},{4,5},{5,4},{6,7},{7,6},{8,9},{9,8},{10,11... | collective-permute-start | bytes 12582920 | tf_op jit(solution)/shard_map/ppermute | solution.py:534
  398.0 5.4 copy-start.1
  418.9 516.4 %all-to-all-start.3 = ((bf16[8,128,2048]{2,1,0:T(8,128)(2,1)}), bf16[8,128,2048]{2,1,0:T(8,128)(2,1)}, u32[]{:S(2)}, u32[]{:S(2)}) async-start(bf16[8,128,2048]{2,1,0:T(8,128)(2,1)} %bitcast.54), calls=%async_computation.3 | async-start | bytes 8388608 | tf_op jit(solution)/shard_map/all_to_all | solution.py:573
Sparse Core Ops, SparseCore 0:
  363.2 309.3 all-reduce.1

commit v3 on v2

--- a/solution.py
+++ b/solution.py
@@ -31,147 +31,197 @@
     return op(x.reshape(x.shape[0] // 8, 8, x.shape[1]), axis=0)
 
 
-def attention_kernel(n_blk, half, kind_ref, core_ref, qa, ka, va, ga, qb, kb, vb, gb, oa, ob, da, db, bias,
-                     qs, ks, vs, gs, kt, vt, s_scr, dp_scr, dk_scr, dv_scr, out_scr):
-    head = pl.program_id(0)
+def merge_halves(n_blk, half, at_a, at_b, triples):
+    for dst, src_a, src_b in triples:
+        for c in range(n_blk):
+            dst[c, pl.ds(at_a, half), :] = src_a[c]
+            dst[c, pl.ds(at_b, half), :] = src_b[c]
+
+
+def block_cases(n_blk, qi, banded, process):
+    for i in range(n_blk):
+        cond = qi == i
+        if i >= 2:
+            cond = cond & jnp.logical_not(banded)
+
+        @pl.when(cond)
+        def _():
+            process(list(range(i + 1)), False)
+
+    @pl.when(banded & (qi >= 2))
+    def _():
+        process([qi - 2, qi - 1, qi], True)
+
+
+def masked_scores(k, q, factor, last, band_first):
+    s = dot_nt(k, q) * factor
+    if last or band_first:
+        row = lax.broadcasted_iota(jnp.int32, s.shape, 0)
+        col = lax.broadcasted_iota(jnp.int32, s.shape, 1)
+        s = jnp.where(row <= col if last else row > col, s, NEG_BIG)
+    return s
+
+
+def plus(total, part):
+    return part if total is None else total + part
+
+
+def forward_kernel(n_blk, half, kind_ref, core_ref, qa, ka, va, qb, kb, vb, oa, ob, lse, qs, ks, vs, vt, s_scr, out_scr):
     qi = pl.program_id(1)
     core = core_ref[0]
-    blk = 2 * half
-    scale = 1.0 / math.sqrt(qs.shape[2])
+    factor = LOG2_E / math.sqrt(qs.shape[2])
     at_a = pl.multiple_of(core * half, half)
     at_b = pl.multiple_of((1 - core) * half, half)
 
     @pl.when(qi == 0)
     def _():
-        for dst, src_a, src_b in ((qs, qa, qb), (ks, ka, kb), (vs, va, vb), (gs, ga, gb)):
-            for c in range(n_blk):
-                dst[c, pl.ds(at_a, half), :] = src_a[c]
-                dst[c, pl.ds(at_b, half), :] = src_b[c]
+        merge_halves(n_blk, half, at_a, at_b, ((qs, qa, qb), (ks, ka, kb), (vs, va, vb)))
         for c in range(n_blk):
-            kt[c] = jnp.transpose(ks[c])
             vt[c] = jnp.transpose(vs[c])
-        dk_scr[...] = jnp.zeros_like(dk_scr)
-        bias[...] = jnp.zeros_like(bias)
-        dv_scr[...] = jnp.zeros_like(dv_scr)
 
     def process(chunks, band_first):
         q = qs[qi]
-        g = gs[qi]
         n = len(chunks)
-        row = lax.broadcasted_iota(jnp.int32, (blk, blk), 0)
-        col = lax.broadcasted_iota(jnp.int32, (blk, blk), 1)
         top = None
         for idx, c in enumerate(chunks):
-            s = dot_nt(ks[c], q) * (scale * LOG2_E)
-            if idx == n - 1:
-                s = jnp.where(row <= col, s, NEG_BIG)
-            if band_first and idx == 0:
-                s = jnp.where(row > col, s, NEG_BIG)
+            s = masked_scores(ks[c], q, factor, idx == n - 1, band_first and idx == 0)
             s_scr[idx] = s
             part = fold(s, jnp.max)
             top = part if top is None else jnp.maximum(top, part)
-            dp_scr[idx] = dot_nt(vs[c], g).astype(jnp.bfloat16)
         top = jnp.max(top, axis=0, keepdims=True)
         total = None
         for idx in range(n):
             e = jnp.exp2(s_scr[idx] - top)
             s_scr[idx] = e
-            part = fold(e, jnp.sum)
-            total = part if total is None else total + part
-        inv = 1.0 / jnp.sum(total, axis=0, keepdims=True)
-        delta = None
+            total = plus(total, fold(e, jnp.sum))
+        total = jnp.sum(total, axis=0, keepdims=True)
+        inv = 1.0 / total
         o_t = None
         for idx, c in enumerate(chunks):
-            p = s_scr[idx] * inv
-            s_scr[idx] = p
-            part = fold(p * dp_scr[idx].astype(jnp.float32), jnp.sum)
-            delta = part if delta is None else delta + part
-            p_bf = p.astype(jnp.bfloat16)
-            o_part = dot_nn(vt[c], p_bf)
-            o_t = o_part if o_t is None else o_t + o_part
-            dv_scr[c] += dot_nn(p_bf, g)
+            p_bf = (s_scr[idx] * inv).astype(jnp.bfloat16)
+            o_t = plus(o_t, dot_nn(vt[c], p_bf))
+        out_scr[...] = jnp.transpose(o_t).astype(jnp.bfloat16)
+        lse[qi] = jnp.broadcast_to(top + jnp.log2(total), lse.shape[1:])
+
+    block_cases(n_blk, qi, kind_ref[pl.program_id(0)] == 1, process)
+    oa[qi] = out_scr[pl.ds(at_a, half), :]
+    ob[qi] = out_scr[pl.ds(at_b, half), :]
+
+
+def backward_kernel(n_blk, half, kind_ref, core_ref, qa, ka, va, ga, qb, kb, vb, gb, lse, da, db, bias,
+                    qs, ks, vs, gs, kt, p_scr, dp_scr, dk_scr, dv_scr, out_scr):
+    qi = pl.program_id(1)
+    core = core_ref[0]
+    scale = 1.0 / math.sqrt(qs.shape[2])
+    at_a = pl.multiple_of(core * half, half)
+    at_b = pl.multiple_of((1 - core) * half, half)
+
+    @pl.when(qi == 0)
+    def _():
+        merge_halves(n_blk, half, at_a, at_b, ((qs, qa, qb), (ks, ka, kb), (vs, va, vb), (gs, ga, gb)))
+        for c in range(n_blk):
+            kt[c] = jnp.transpose(ks[c])
+        dk_scr[...] = jnp.zeros_like(dk_scr)
+        dv_scr[...] = jnp.zeros_like(dv_scr)
+        bias[...] = jnp.zeros_like(bias)
+
+    def process(chunks, band_first):
+        q = qs[qi]
+        g = gs[qi]
+        n = len(chunks)
+        shift = lse[qi][0:1]
+        delta = None
+        for idx, c in enumerate(chunks):
+            p = jnp.exp2(masked_scores(ks[c], q, scale * LOG2_E, idx == n - 1, band_first and idx == 0) - shift)
+            p_scr[idx] = p
+            dp = dot_nt(vs[c], g).astype(jnp.bfloat16)
+            dp_scr[idx] = dp
+            delta = plus(delta, fold(p * dp.astype(jnp.float32), jnp.sum))
+            dv_scr[c] += dot_nn(p.astype(jnp.bfloat16), g)
         delta = jnp.sum(delta, axis=0, keepdims=True)
         dq_t = None
         for idx, c in enumerate(chunks):
-            ds = (s_scr[idx] * (dp_scr[idx].astype(jnp.float32) - delta)).astype(jnp.bfloat16)
-            dq_part = dot_nn(kt[c], ds)
-            dq_t = dq_part if dq_t is None else dq_t + dq_part
+            ds = (p_scr[idx] * (dp_scr[idx].astype(jnp.float32) - delta)).astype(jnp.bfloat16)
+            dq_t = plus(dq_t, dot_nn(kt[c], ds))
             dk_scr[c] += dot_nn(ds, q)
-        out_scr[0] = jnp.transpose(o_t).astype(jnp.bfloat16)
-        out_scr[1] = jnp.transpose(dq_t * scale).astype(jnp.bfloat16)
-
-    banded = kind_ref[head] == 1
-    for i in range(n_blk):
-        cond = qi == i
-        if i >= 2:
-            cond = cond & jnp.logical_not(banded)
-
-        @pl.when(cond)
-        def _():
-            process(list(range(i + 1)), False)
-
-    @pl.when(banded & (qi >= 2))
-    def _():
-        process([qi - 2, qi - 1, qi], True)
-
-    def add_bias(part, v):
-        bias[part] += fold(v.astype(jnp.float32), jnp.sum)
-
-    add_bias(0, out_scr[1])
-    oa[qi] = out_scr[0, pl.ds(at_a, half), :]
-    ob[qi] = out_scr[0, pl.ds(at_b, half), :]
-    da[0, qi] = out_scr[1, pl.ds(at_a, half), :]
-    db[0, qi] = out_scr[1, pl.ds(at_b, half), :]
+        out_scr[0] = jnp.transpose(dq_t * scale).astype(jnp.bfloat16)
+
+    block_cases(n_blk, qi, kind_ref[pl.program_id(0)] == 1, process)
+
+    def give(part, c, slot):
+        bias[part] += fold(out_scr[slot].astype(jnp.float32), jnp.sum)
+        da[part, c] = out_scr[slot, pl.ds(at_a, half), :]
+        db[part, c] = out_scr[slot, pl.ds(at_b, half), :]
+
+    give(0, qi, 0)
 
     @pl.when(qi == n_blk - 1)
     def _():
         for c in range(n_blk):
             out_scr[0] = (dk_scr[c] * scale).astype(jnp.bfloat16)
             out_scr[1] = dv_scr[c].astype(jnp.bfloat16)
-            add_bias(1, out_scr[0])
-            add_bias(2, out_scr[1])
-            da[1, c] = out_scr[0, pl.ds(at_a, half), :]
-            db[1, c] = out_scr[0, pl.ds(at_b, half), :]
-            da[2, c] = out_scr[1, pl.ds(at_a, half), :]
-            db[2, c] = out_scr[1, pl.ds(at_b, half), :]
-
-
-def attention(kinds, core, qkv_own, do_own, qkv_oth, do_oth):
+            give(1, c, 0)
+            give(2, c, 1)
+
+
+def head_specs(n_blk, half, dim):
+    def part(t):
+        return pl.BlockSpec((None, n_blk, half, dim), lambda h, i, kind, cr: (t, 0, 0, h))
+
+    one = pl.BlockSpec((n_blk, half, dim), lambda h, i, kind, cr: (0, 0, h))
+    three = pl.BlockSpec((3, n_blk, half, dim), lambda h, i, kind, cr: (0, 0, 0, h))
+    lse = pl.BlockSpec((None, n_blk, 8, 2 * half), lambda h, i, kind, cr: (h, 0, 0, 0))
+    sums = pl.BlockSpec((None, 3, 8, dim), lambda h, i, kind, cr: (h, 0, 0, 0))
+    return part, one, three, lse, sums
+
+
+def attention_call(body, kinds, core, args, in_specs, out_specs, out_shape, scratch, n_tok, products):
+    heads = kinds.shape[0]
+    return pl.pallas_call(
+        body,
+        grid_spec=pltpu.PrefetchScalarGridSpec(
+            num_scalar_prefetch=2, grid=(heads, n_tok[0]), in_specs=in_specs, out_specs=out_specs, scratch_shapes=scratch),
+        out_shape=out_shape,
+        compiler_params=pltpu.CompilerParams(
+            dimension_semantics=("arbitrary", "arbitrary"), vmem_limit_bytes=48 * 1024 * 1024),
+        cost_estimate=pl.CostEstimate(
+            flops=products * heads * (n_tok[0] * n_tok[1]) ** 2 * 128, bytes_accessed=24 * 2**20,
+            transcendentals=heads * (n_tok[0] * n_tok[1]) ** 2 // 2),
+    )(kinds, core, *args)
+
+
+def attention_forward(kinds, core, qkv_own, qkv_oth):
     _, n_blk, half, wide = qkv_own.shape
     heads = kinds.shape[0]
     dim = wide // heads
     blk = 2 * half
-
-    def part(t):
-        return pl.BlockSpec((None, n_blk, half, dim), lambda h, i, kind, cr: (t, 0, 0, h))
-
-    one = pl.BlockSpec((n_blk, half, dim), lambda h, i, kind, cr: (0, 0, h))
-    three = pl.BlockSpec((3, n_blk, half, dim), lambda h, i, kind, cr: (0, 0, 0, h))
-    sums = pl.BlockSpec((None, 3, 8, dim), lambda h, i, kind, cr: (h, 0, 0, 0))
     bf = jnp.bfloat16
-    flops = 6 * 2 * heads * (n_blk * blk) ** 2 * dim // 2
-    return pl.pallas_call(
-        functools.partial(attention_kernel, n_blk, half),
-        grid_spec=pltpu.PrefetchScalarGridSpec(
-            num_scalar_prefetch=2,
-            grid=(heads, n_blk),
-            in_specs=[part(0), part(1), part(2), one, part(0), part(1), part(2), one],
-            out_specs=[one, one, three, three, sums],
-            scratch_shapes=[pltpu.VMEM((n_blk, blk, dim), bf)] * 4
-            + [pltpu.VMEM((n_blk, dim, blk), bf)] * 2
-            + [pltpu.VMEM((n_blk, blk, blk), jnp.float32), pltpu.VMEM((n_blk, blk, blk), bf)]
-            + [pltpu.VMEM((n_blk, blk, dim), jnp.float32)] * 2
-            + [pltpu.VMEM((2, blk, dim), bf)],
-        ),
-        out_shape=[jax.ShapeDtypeStruct((n_blk, half, wide), bf)] * 2
-        + [jax.ShapeDtypeStruct((3, n_blk, half, wide), bf)] * 2
-        + [jax.ShapeDtypeStruct((heads, 3, 8, dim), jnp.float32)],
-        compiler_params=pltpu.CompilerParams(
-            dimension_semantics=("arbitrary", "arbitrary"), vmem_limit_bytes=48 * 1024 * 1024
-        ),
-        cost_estimate=pl.CostEstimate(flops=flops, bytes_accessed=40 * 2**20, transcendentals=heads * (n_blk * blk) ** 2 // 2),
-        name="attention_fwd_bwd",
-    )(kinds, core, qkv_own, qkv_own, qkv_own, do_own, qkv_oth, qkv_oth, qkv_oth, do_oth)
+    part, one, _, lse, _ = head_specs(n_blk, half, dim)
+    return attention_call(
+        functools.partial(forward_kernel, n_blk, half), kinds, core, [qkv_own] * 3 + [qkv_oth] * 3,
+        [part(0), part(1), part(2)] * 2, [one, one, lse],
+        [jax.ShapeDtypeStruct((n_blk, half, wide), bf)] * 2 + [jax.ShapeDtypeStruct((heads, n_blk, 8, blk), jnp.float32)],
+        [pltpu.VMEM((n_blk, blk, dim), bf)] * 3 + [pltpu.VMEM((n_blk, dim, blk), bf)]
+        + [pltpu.VMEM((n_blk, blk, blk), jnp.float32), pltpu.VMEM((blk, dim), bf)],
+        (n_blk, blk), 2)
+
+
+def attention_backward(kinds, core, qkv_own, do_own, qkv_oth, do_oth, lse_arr):
+    _, n_blk, half, wide = qkv_own.shape
+    heads = kinds.shape[0]
+    dim = wide // heads
+    blk = 2 * half
+    bf = jnp.bfloat16
+    part, one, three, lse, sums = head_specs(n_blk, half, dim)
+    return attention_call(
+        functools.partial(backward_kernel, n_blk, half), kinds, core,
+        [qkv_own] * 3 + [do_own] + [qkv_oth] * 3 + [do_oth, lse_arr],
+        [part(0), part(1), part(2), one] * 2 + [lse], [three, three, sums],
+        [jax.ShapeDtypeStruct((3, n_blk, half, wide), bf)] * 2 + [jax.ShapeDtypeStruct((heads, 3, 8, dim), jnp.float32)],
+        [pltpu.VMEM((n_blk, blk, dim), bf)] * 4 + [pltpu.VMEM((n_blk, dim, blk), bf)]
+        + [pltpu.VMEM((n_blk, blk, blk), jnp.float32), pltpu.VMEM((n_blk, blk, blk), bf)]
+        + [pltpu.VMEM((n_blk, blk, dim), jnp.float32)] * 2 + [pltpu.VMEM((2, blk, dim), bf)],
+        (n_blk, blk), 5)
 
 
 def matmul_call(body, scalars, grid, ins, outs, out_shape, flops):
@@ -544,30 +594,28 @@
         h_norm = h_f.astype(bf)
         bias_row = b_qkv.reshape(1, 3 * d_model)
         qkv_send = project_qkv(h_norm, w_qkv, bias_row, other_arr)
-        qkv_oth = swap(qkv_send)
-        qkv_own = project_qkv(h_norm, w_qkv, bias_row, core_arr)
+        qkv_oth = swap(qkv_send).reshape(blocks)
+        qkv_own = project_qkv(h_norm, w_qkv, bias_row, core_arr).reshape(blocks)
         g_b, qkv_own = lax.optimization_barrier((g_b, qkv_own))
-        do_oth = swap(project_do(g_b, w_out, other_arr))
-        do_own = project_do(g_b, w_out, core_arr)
+        o_own, o_send, lse = attention_forward(my_kinds, core_arr, qkv_own, qkv_oth)
+        o_oth = swap(o_send).reshape(n_tok, wide)
+        o_own = o_own.reshape(n_tok, wide)
+        do_oth = swap(project_do(g_b, w_out, other_arr)).reshape(blocks[1:])
+        do_own = project_do(g_b, w_out, core_arr).reshape(blocks[1:])
         h_oth = swap(h_norm)
 
-        o_own, o_send, dg_own, dg_send, bias_sums = attention(
-            my_kinds, core_arr, qkv_own.reshape(blocks), do_own.reshape(blocks[1:]),
-            qkv_oth.reshape(blocks), do_oth.reshape(blocks[1:]))
-        o_oth = swap(o_send).reshape(n_tok, wide)
+        d_wout = out_weight_grad(o_own, o_oth, g_b, core_arr)
+        y_b = project_out(x_b, o_own, o_oth, w_out, b_out.reshape(1, d_model), core_arr)
+        d_wout, y_b, do_own, do_oth = lax.optimization_barrier((d_wout, y_b, do_own, do_oth))
+        d_wout = lax.psum(d_wout, ("chip", "core"))
+        y_out = lax.all_to_all(y_b.reshape(n_chip, half, d_model), "chip", 0, 0, tiled=True)
+
+        dg_own, dg_send, bias_sums = attention_backward(my_kinds, core_arr, qkv_own, do_own, qkv_oth, do_oth, lse)
         dg_oth = swap(dg_send).reshape(3, n_tok, wide)
-        o_own = o_own.reshape(n_tok, wide)
         dg_own = dg_own.reshape(3, n_tok, wide)
         dg_send = dg_send.reshape(3, n_tok, wide)
 
-        d_wout = out_weight_grad(o_own, o_oth, g_b, core_arr)
-        d_wout, dg_own, dg_oth = lax.optimization_barrier((d_wout, dg_own, dg_oth))
-        d_wout = lax.psum(d_wout, ("chip", "core"))
-        y_b = project_out(x_b, o_own, o_oth, w_out, b_out.reshape(1, d_model), core_arr)
-        y_out = lax.all_to_all(y_b.reshape(n_chip, half, d_model), "chip", 0, 0, tiled=True)
-
-        d_h = hidden_grad(dg_own, dg_oth, w_qkv, core_arr)
-        d_h = d_h.astype(f32)
+        d_h = hidden_grad(dg_own, dg_oth, w_qkv, core_arr).astype(f32)
         d_x_ln, d_gamma, d_beta = ln_pull(d_h)
         d_x_b = (g_b.astype(f32) + d_x_ln).astype(bf)
         d_x = lax.all_to_all(d_x_b.reshape(n_chip, half, d_model), "chip", 0, 0, tiled=True)

time: 965 us -> 1020 us (1.057)
  Pallas kernels: 745 us -> 812 us
  waiting for transfers between devices: 129 us -> 117 us
    pallas_call x1 -> x2, Pallas kernels: 103 us -> 155 us  [attention_call(): pl.pallas_call(body, grid_spec=pltpu.PrefetchScalarGridSpec(num_scalar_pr...]
    pallas_call x1, Pallas kernels: 433 us -> 447 us  [grad_sum(): pl.pallas_call(functools.partial(grad_sum_kernel, n_chip, rows), in_specs...]
  transfers between devices with their start and end apart: 10 -> 10, of which waited for: 4 -> 3; matrix products, arithmetic and copies ran while one was open for 2% -> 2% of each run, Pallas kernels for 64% -> 71%
where the time goes in v3:
time: 1020 us; the launch traced here: 1010 us
  Pallas kernels  812 us (80%)
  waiting for transfers between devices  117 us (11%)
  starting transfers between devices  33.3 us (3%)
  other arithmetic  31.3 us (3%)
  between operations  14.6 us (1%)
    pallas_call x1, Pallas kernels, grad_sum(): pl.pallas_call(functools.partial(grad_sum_kernel, n_chip, rows), in_specs...  447 us
    pallas_call x2, Pallas kernels, attention_call(): pl.pallas_call(body, grid_spec=pltpu.PrefetchScalarGridSpec(num_scalar_pr...  155 us
    pallas_call x8, Pallas kernels, matmul_call(): pl.pallas_call(body, grid_spec=pltpu.PrefetchScalarGridSpec(num_scalar_pr...  154 us
    pallas_call x4, Pallas kernels, place(): pl.pallas_call(copy_kernel, grid=(rows // tile,), in_specs=in_specs, out_...  55.6 us
    all_to_all x1, waiting for transfers between devices, local_block(): x_b = lax.all_to_all(x, 'chip', 0, 0, tiled=True).reshape(n_tok, d_model)  51.8 us
    all_to_all x1, waiting for transfers between devices, local_block(): g_b = lax.all_to_all(d_y, 'chip', 0, 0, tiled=True).reshape(n_tok, d_model)  35.6 us
    all_to_all x1, waiting for transfers between devices, local_block(): lax.all_to_all(y_b.reshape(n_chip, half, d_model), 'chip', 0, 0, tiled=True)  28.7 us
  transfers between devices with their start and end apart: 10, of which 3 were waited for; matrix products, arithmetic and copies ran while one was open for 2% of the time, Pallas kernels for 71%

profile of v3, /device:TPU:0, one launch (start us, length us, event | category | flops | bytes accessed | tf_op | source)
XLA Modules:
  0.0 1014.7 jit_solution(15476521329356564621)
XLA Ops:
  7.2 6.6 all-to-all-start.1
  14.5 51.8 %all-to-all-done.1 = bf16[8,128,2048]{2,1,0:T(8,128)(2,1)} async-done(((bf16[8,128,2048]{2,1,0:T(8,128)(2,1)}), bf16[8,128,2048]{2,1,0:T(8,128)(2,1)}, u32[]{:S(2)}, u32[]{:S(2)}) %all-to-all-start.1) | async-done | bytes 4194336 | tf_op jit(solution)/shard_map/all_to_all | solution.py:586
  73.7 4.6 add_convert_fusion.h_ref.ha
  78.3 18.0 %shard_map.153 = bf16[3,1024,1024]{2,1,0:T(8,128)(2,1)} custom-call(s32[1]{0:T(128)S(6)} %sub.20.g, bf16[1024,2048]{1,0:T(8,128)(2,1)} %add_convert_fusion.h_ref.ha, bf16[2048,6144]{1,0:T(8,128)(2,1)} %refs_5_.1, bf16[1,6144]{1,0:T(2,128)(2,1)} %reshape.141.b_ref), custom_call_target="tpu_custom_call" | custom-call | flops 12884901888 | bytes 29372416 | tf_op jit(solution)/shard_map/pallas_call | solution.py:230
  96.4 8.0 all-to-all-start
  104.4 18.0 %shard_map.152 = bf16[3,1024,1024]{2,1,0:T(8,128)(2,1)} custom-call(s32[1]{0:T(128)} %bitcast.g.core_ref.c, bf16[1024,2048]{1,0:T(8,128)(2,1)} %add_convert_fusion.h_ref.ha, bf16[2048,6144]{1,0:T(8,128)(2,1)} %refs_5_.1, bf16[1,6144]{1,0:T(2,128)(2,1)} %reshape.141.b_ref), custom_call_target="tpu_custom_call" | custom-call | flops 12884901888 | bytes 29372416 | tf_op jit(solution)/shard_map/pallas_call | solution.py:230
  122.4 35.6 %all-to-all-done = bf16[8,128,2048]{2,1,0:T(8,128)(2,1)} async-done(((bf16[8,128,2048]{2,1,0:T(8,128)(2,1)}), bf16[8,128,2048]{2,1,0:T(8,128)(2,1)}, u32[]{:S(2)}, u32[]{:S(2)}) %all-to-all-start) | async-done | bytes 4194336 | tf_op jit(solution)/shard_map/all_to_all | solution.py:587
  158.0 66.8 %shard_map.154 = (bf16[8,128,1024]{2,1,0:T(8,128)(2,1)S(1)}, bf16[8,128,1024]{2,1,0:T(8,128)(2,1)S(1)}, f32[8,8,8,256]{3,2,1,0:T(8,128)S(1)}) custom-call(s32[8]{0:T(128)S(1)} %dynamic_slice.3.kind_ref, s32[1]{0:T(128)} %bitcast.g.core_ref.c, bf16[3,8,128,1024]{3,2,1,0:T(8,128)(2,1)} %bitcast.56, bf16[3,8,128,1024]{3,2,1,0:T(8,128)(2,1)} %bitcast.57, ...), custom_call_target="tpu_custom_call" | custom-call | flops 8589934592 | bytes 25165824 | tf_op jit(solution)/shard_map/pallas_call | solution.py:180
  226.2 8.6 shard_map.158
  235.9 8.5 shard_map.157
  245.8 14.7 %shard_map.155 = f32[2048,2048]{1,0:T(8,128)} custom-call(s32[1]{0:T(128)} %bitcast.g.core_ref.c, bf16[1024,1024]{1,0:T(8,128)(2,1)} %bitcast.53, bf16[1024,1024]{1,0:T(8,128)(2,1)} %bitcast.71, bf16[1024,2048]{1,0:T(8,128)(2,1)} %bitcast.1.dy_ref), custom_call_target="tpu_custom_call" | custom-call | flops 8589934592 | bytes 8388608 | tf_op jit(solution)/shard_map/pallas_call | solution.py:230
  260.5 14.1 %shard_map.156 = bf16[1024,2048]{1,0:T(8,128)(2,1)} custom-call(s32[1]{0:T(128)} %bitcast.g.core_ref.c, bf16[1024,2048]{1,0:T(8,128)(2,1)} %bitcast.2.x_ref, bf16[1024,1024]{1,0:T(8,128)(2,1)} %bitcast.54, bf16[1024,1024]{1,0:T(8,128)(2,1)} %bitcast.72, bf16[2048,2048]{1,0:T(8,128)(2,1)} %w_ref.7, bf16[2048,2048]{1,0:T(8,128)(2,1)} %w_ref.7, ...), custom_call_target="tpu_custom_call" | custom-call | flops 8589934592 | bytes 25169920 | tf_op jit(solution)/shard_map/pallas_call | solution.py:230
  274.6 88.2 %shard_map.159 = (bf16[3,8,128,1024]{3,2,1,0:T(8,128)(2,1)}, bf16[3,8,128,1024]{3,2,1,0:T(8,128)(2,1)}, f32[8,3,8,128]{3,2,1,0:T(8,128)S(1)}) custom-call(s32[8]{0:T(128)S(1)} %dynamic_slice.3.kind_ref, s32[1]{0:T(128)} %bitcast.g.core_ref.c, bf16[3,8,128,1024]{3,2,1,0:T(8,128)(2,1)} %bitcast.59, bf16[3,8,128,1024]{3,2,1,0:T(8,128)(2,1)} %bitcast.60, ...), custom_call_target="tpu_custom_call" | custom-call | flops 21474836480 | bytes 25165824 | tf_op jit(solution)/shard_map/pallas_call | solution.py:180
  362.8 7.4 all-to-all-start.2
  371.1 37.2 %shard_map.161.g_all = f32[3,2048,1024]{2,1,0:T(8,128)} custom-call(bf16[1024,2048]{1,0:T(8,128)(2,1)} %add_convert_fusion.h_ref.ha, bf16[1024,2048]{1,0:T(8,128)(2,1)} %collective-permute-done.4.hb, bf16[3,1024,1024]{2,1,0:T(8,128)(2,1)} %bitcast.63, bf16[3,1024,1024]{2,1,0:T(8,128)(2,1)} %bitcast.70), custom_call_target="tpu_custom_call" | custom-call | flops 25769803776 | bytes 20971520 | tf_op jit(solution)/shard_map/pallas_call | solution.py:230
  408.3 28.7 %all-to-all-done.2 = bf16[8,128,2048]{2,1,0:T(8,128)(2,1)} async-done(((bf16[8,128,2048]{2,1,0:T(8,128)(2,1)}), bf16[8,128,2048]{2,1,0:T(8,128)(2,1)}, u32[]{:S(2)}, u32[]{:S(2)}) %all-to-all-start.2) | async-done | bytes 4194336 | tf_op jit(solution)/shard_map/all_to_all | solution.py:611
  441.1 35.3 %shard_map.160 = bf16[1024,2048]{1,0:T(8,128)(2,1)} custom-call(s32[1]{0:T(128)} %bitcast.g.core_ref.c, bf16[3,1024,1024]{2,1,0:T(8,128)(2,1)} %bitcast.64, bf16[3,1024,1024]{2,1,0:T(8,128)(2,1)} %bitcast.15.oth, bf16[2048,6144]{1,0:T(8,128)(2,1)} %refs_5_.1, bf16[2048,6144]{1,0:T(8,128)(2,1)} %refs_5_.1, bf16[2048,6144]{1,0:T(8,128)(2,1)} %refs_5_.1, ...), custom_call_target="tpu_custom_call" | custom-call | flops 25769803776 | bytes 163577856 | tf_op jit(solution)/shard_map/pallas_call | solution.py:230
  476.5 4.9 fusion.2
  481.6 6.3 fusion.6
  487.9 9.1 convert_reduce_fusion.1
  497.1 10.8 %all-to-all-start.3 = ((bf16[8,128,2048]{2,1,0:T(8,128)(2,1)}), bf16[8,128,2048]{2,1,0:T(8,128)(2,1)}, u32[]{:S(2)}, u32[]{:S(2)}) async-start(bf16[8,128,2048]{2,1,0:T(8,128)(2,1)} %bitcast.62), calls=%async_computation.3 | async-start | bytes 8388608 | tf_op jit(solution)/shard_map/all_to_all | solution.py:621
  507.9 447.0 %grad_sum.1 = (f32[2048,6144]{1,0:T(8,128)}, f32[96,128]{1,0:T(8,128)S(1)}) custom-call(f32[3,2048,1024]{2,1,0:T(8,128)} %shard_map.161.g_all, f32[96,128]{1,0:T(8,128)S(1)} %maximum_bitcast_fusion.small), custom_call_target="tpu_custom_call" | custom-call | flops 299999985664 | bytes 157286400 | tf_op jit(solution)/shard_map/grad_sum/pallas_call | solution.py:546
  954.9 36.3 %place_rows.6 = f32[2048,6144]{1,0:T(8,128)} custom-call(f32[2048,6144]{1,0:T(8,128)} %get-tuple-element.34.refs_0_), custom_call_target="tpu_custom_call" | custom-call | flops 100663296 | bytes 100663296 | tf_op jit(solution)/shard_map/place_rows/pallas_call | solution.py:376
  992.4 11.4 %place_rows.7 = f32[2048,2048]{1,0:T(8,128)} custom-call(f32[2048,2048]{1,0:T(8,128)} %all-reduce.2.cloned.1.call-done.refs_0_), custom_call_target="tpu_custom_call" | custom-call | flops 33554432 | bytes 33554432 | tf_op jit(solution)/shard_map/place_rows/pallas_call | solution.py:376
  (68 shorter events, 22.2 us)
Async XLA Ops:
  7.2 6.6 copy-start.12
  7.2 6.6 copy-start.13
  7.2 6.6 copy-start.11
  7.2 59.1 %all-to-all-start.1 = ((bf16[8,128,2048]{2,1,0:T(8,128)(2,1)}), bf16[8,128,2048]{2,1,0:T(8,128)(2,1)}, u32[]{:S(2)}, u32[]{:S(2)}) async-start(bf16[8,128,2048]{2,1,0:T(8,128)(2,1)} %param.9), calls=%async_computation.1 | async-start | bytes 8388608 | tf_op jit(solution)/shard_map/all_to_all | solution.py:586
  13.8 64.5 %copy-start.3 = (f32[2048]{0:T(1024)}, f32[2048]{0:T(1024)S(1)}, u32[]{:S(2)}) copy-start(f32[2048]{0:T(1024)S(1)} %convert_element_type.28) | copy-start | bytes 24580
  69.1 4.0 copy-start.5
  96.3 8.0 copy-start.16
  96.4 61.7 %collective-permute-start = (bf16[3,1024,1024]{2,1,0:T(8,128)(2,1)}, bf16[3,1024,1024]{2,1,0:T(8,128)(2,1)}, u32[]{:S(2)}, u32[]{:S(2)}) collective-permute-start(bf16[3,1024,1024]{2,1,0:T(8,128)(2,1)} %shard_map.153), channel_id=1, source_target_pairs={{0,1},{1,0},{2,3},{3,2},{4,5},{5,4},{6,7},{7,6},{8,9},{9,8},{10,11... | collective-permute-start | bytes 18874376 | tf_op jit(solution)/shard_map/ppermute | solution.py:584
  96.4 61.7 %all-to-all-start = ((bf16[8,128,2048]{2,1,0:T(8,128)(2,1)}), bf16[8,128,2048]{2,1,0:T(8,128)(2,1)}, u32[]{:S(2)}, u32[]{:S(2)}) async-start(bf16[8,128,2048]{2,1,0:T(8,128)(2,1)} %param.10), calls=%async_computation | async-start | bytes 8388608 | tf_op jit(solution)/shard_map/all_to_all | solution.py:587
  224.8 1.4 copy-start
  226.2 9.1 copy-start.14
  226.2 18.3 %collective-permute-start.1 = (bf16[8,128,1024]{2,1,0:T(8,128)(2,1)S(1)}, bf16[8,128,1024]{2,1,0:T(8,128)(2,1)S(1)}, u32[]{:S(2)}, u32[]{:S(2)}) collective-permute-start(bf16[8,128,1024]{2,1,0:T(8,128)(2,1)S(1)} %get-tuple-element.24), channel_id=1, source_target_pairs={{0,1},{1,0},{2,3},{3,2},{4,5},{5,4},{6,7},{7,6},{8,9},{9,8},{10,11... | collective-permute-start | bytes 6291464 | tf_op jit(solution)/shard_map/ppermute | solution.py:584
  234.8 39.8 %collective-permute-start.2 = (bf16[1024,1024]{1,0:T(8,128)(2,1)}, bf16[1024,1024]{1,0:T(8,128)(2,1)S(1)}, u32[]{:S(2)}, u32[]{:S(2)}) collective-permute-start(bf16[1024,1024]{1,0:T(8,128)(2,1)} %shard_map.158), channel_id=1, source_target_pairs={{0,1},{1,0},{2,3},{3,2},{4,5},{5,4},{6,7},{7,6},{8,9},{9,8},{10,11... | collective-permute-start | bytes 6291464 | tf_op jit(solution)/shard_map/ppermute | solution.py:584
  235.9 135.2 %collective-permute-start.4 = (bf16[1024,2048]{1,0:T(8,128)(2,1)}, bf16[1024,2048]{1,0:T(8,128)(2,1)}, u32[]{:S(2)}, u32[]{:S(2)}) collective-permute-start(bf16[1024,2048]{1,0:T(8,128)(2,1)} %add_convert_fusion.h_ref.ha), channel_id=1, source_target_pairs={{0,1},{1,0},{2,3},{3,2},{4,5},{5,4},{6,7},{7,6},{8,9},{9,8},{10,11... | collective-permute-start | bytes 12582920 | tf_op jit(solution)/shard_map/ppermute | solution.py:584
  260.5 14.1 %copy-start.1 = (bf16[1024,1024]{1,0:T(8,128)(2,1)S(1)}, bf16[1024,1024]{1,0:T(8,128)(2,1)}, u32[]{:S(2)}) copy-start(bf16[1024,1024]{1,0:T(8,128)(2,1)} %shard_map.157) | copy-start | bytes 6291460
  362.8 78.3 %collective-permute-start.3 = (bf16[3,8,128,1024]{3,2,1,0:T(8,128)(2,1)}, bf16[3,8,128,1024]{3,2,1,0:T(8,128)(2,1)}, u32[]{:S(2)}, u32[]{:S(2)}) collective-permute-start(bf16[3,8,128,1024]{3,2,1,0:T(8,128)(2,1)} %get-tuple-element.31), channel_id=1, source_target_pairs={{0,1},{1,0},{2,3},{3,2},{4,5},{5,4},{6,7},{7,6},{8,9},{9,8},{10,11... | collective-permute-start | bytes 18874376 | tf_op jit(solution)/shard_map/ppermute | solution.py:584
  362.8 74.2 %all-to-all-start.2 = ((bf16[8,128,2048]{2,1,0:T(8,128)(2,1)}), bf16[8,128,2048]{2,1,0:T(8,128)(2,1)}, u32[]{:S(2)}, u32[]{:S(2)}) async-start(bf16[8,128,2048]{2,1,0:T(8,128)(2,1)} %bitcast.66), calls=%async_computation.2 | async-start | bytes 8388608 | tf_op jit(solution)/shard_map/all_to_all | solution.py:611
  370.3 622.1 %all-reduce.2.cloned.1.call-start = ((), (), s32[]{:S(2)}) async-start(), calls=%async_computation.4 | async-start | bytes 33554432 | tf_op jit(solution)/shard_map/psum | solution.py:610
  441.1 35.3 %copy-start.4 = (f32[2048]{0:T(1024)S(1)}, f32[2048]{0:T(1024)}, u32[]{:S(2)}) copy-start(f32[2048]{0:T(1024)} %copy-done.3) | copy-start | bytes 24580
  441.1 35.3 %copy-start.6 = (f32[1024]{0:T(1024)S(1)}, f32[1024]{0:T(1024)}, u32[]{:S(2)}) copy-start(f32[1024]{0:T(1024)} %copy-done.5) | copy-start | bytes 12292
  476.4 4.9 copy-start.10
  476.4 5.2 copy-start.2
  476.4 5.2 copy-start.8
  497.1 506.7 %all-to-all-start.3 = ((bf16[8,128,2048]{2,1,0:T(8,128)(2,1)}), bf16[8,128,2048]{2,1,0:T(8,128)(2,1)}, u32[]{:S(2)}, u32[]{:S(2)}) async-start(bf16[8,128,2048]{2,1,0:T(8,128)(2,1)} %bitcast.62), calls=%async_computation.3 | async-start | bytes 8388608 | tf_op jit(solution)/shard_map/all_to_all | solution.py:621
  (3 other events, 2.5 us)
Sparse Core Ops, SparseCore 0:
  377.1 316.2 all-reduce.1

commit v4 on v3

--- a/solution.py
+++ b/solution.py
@@ -38,19 +38,19 @@
             dst[c, pl.ds(at_b, half), :] = src_b[c]
 
 
-def block_cases(n_blk, qi, banded, process):
-    for i in range(n_blk):
-        cond = qi == i
-        if i >= 2:
+def block_cases(n_blk, pair, banded, process):
+    for i in range(n_blk // 2):
+        cond = pair == i
+        if i >= 1:
             cond = cond & jnp.logical_not(banded)
 
         @pl.when(cond)
         def _():
-            process(list(range(i + 1)), False)
-
-    @pl.when(banded & (qi >= 2))
+            process(list(range(2 * i + 2)), ((0, 2 * i + 1), (0, 2 * i + 2)), False)
+
+    @pl.when(banded & (pair >= 1))
     def _():
-        process([qi - 2, qi - 1, qi], True)
+        process([2 * pair - 2 + i for i in range(4)], ((0, 3), (1, 4)), True)
 
 
 def masked_scores(k, q, factor, last, band_first):
@@ -67,56 +67,57 @@
 
 
 def forward_kernel(n_blk, half, kind_ref, core_ref, qa, ka, va, qb, kb, vb, oa, ob, lse, qs, ks, vs, vt, s_scr, out_scr):
-    qi = pl.program_id(1)
+    pair = pl.program_id(1)
     core = core_ref[0]
     factor = LOG2_E / math.sqrt(qs.shape[2])
     at_a = pl.multiple_of(core * half, half)
     at_b = pl.multiple_of((1 - core) * half, half)
 
-    @pl.when(qi == 0)
+    @pl.when(pair == 0)
     def _():
         merge_halves(n_blk, half, at_a, at_b, ((qs, qa, qb), (ks, ka, kb), (vs, va, vb)))
         for c in range(n_blk):
             vt[c] = jnp.transpose(vs[c])
 
-    def process(chunks, band_first):
-        q = qs[qi]
-        n = len(chunks)
-        top = None
+    def process(chunks, ranges, banded):
+        tops, sums = [None, None], [None, None]
         for idx, c in enumerate(chunks):
-            s = masked_scores(ks[c], q, factor, idx == n - 1, band_first and idx == 0)
-            s_scr[idx] = s
-            part = fold(s, jnp.max)
-            top = part if top is None else jnp.maximum(top, part)
-        top = jnp.max(top, axis=0, keepdims=True)
-        total = None
-        for idx in range(n):
-            e = jnp.exp2(s_scr[idx] - top)
-            s_scr[idx] = e
-            total = plus(total, fold(e, jnp.sum))
-        total = jnp.sum(total, axis=0, keepdims=True)
-        inv = 1.0 / total
-        o_t = None
-        for idx, c in enumerate(chunks):
-            p_bf = (s_scr[idx] * inv).astype(jnp.bfloat16)
-            o_t = plus(o_t, dot_nn(vt[c], p_bf))
-        out_scr[...] = jnp.transpose(o_t).astype(jnp.bfloat16)
-        lse[qi] = jnp.broadcast_to(top + jnp.log2(total), lse.shape[1:])
-
-    block_cases(n_blk, qi, kind_ref[pl.program_id(0)] == 1, process)
-    oa[qi] = out_scr[pl.ds(at_a, half), :]
-    ob[qi] = out_scr[pl.ds(at_b, half), :]
+            for r, (lo, hi) in enumerate(ranges):
+                if lo <= idx < hi:
+                    s = masked_scores(ks[c], qs[2 * pair + r], factor, idx == hi - 1, banded and idx == lo)
+                    s_scr[r, idx] = s
+                    part = fold(s, jnp.max)
+                    tops[r] = part if tops[r] is None else jnp.maximum(tops[r], part)
+        for r, (lo, hi) in enumerate(ranges):
+            tops[r] = jnp.max(tops[r], axis=0, keepdims=True)
+            for idx in range(lo, hi):
+                e = jnp.exp2(s_scr[r, idx] - tops[r])
+                s_scr[r, idx] = e
+                sums[r] = plus(sums[r], fold(e, jnp.sum))
+        for r, (lo, hi) in enumerate(ranges):
+            total = jnp.sum(sums[r], axis=0, keepdims=True)
+            inv = 1.0 / total
+            o_t = None
+            for idx in range(lo, hi):
+                o_t = plus(o_t, dot_nn(vt[chunks[idx]], (s_scr[r, idx] * inv).astype(jnp.bfloat16)))
+            out_scr[r] = jnp.transpose(o_t).astype(jnp.bfloat16)
+            lse[2 * pair + r] = jnp.broadcast_to(tops[r] + jnp.log2(total), lse.shape[1:])
+
+    block_cases(n_blk, pair, kind_ref[pl.program_id(0)] == 1, process)
+    for r in range(2):
+        oa[2 * pair + r] = out_scr[r, pl.ds(at_a, half), :]
+        ob[2 * pair + r] = out_scr[r, pl.ds(at_b, half), :]
 
 
 def backward_kernel(n_blk, half, kind_ref, core_ref, qa, ka, va, ga, qb, kb, vb, gb, lse, da, db, bias,
                     qs, ks, vs, gs, kt, p_scr, dp_scr, dk_scr, dv_scr, out_scr):
-    qi = pl.program_id(1)
+    pair = pl.program_id(1)
     core = core_ref[0]
     scale = 1.0 / math.sqrt(qs.shape[2])
     at_a = pl.multiple_of(core * half, half)
     at_b = pl.multiple_of((1 - core) * half, half)
 
-    @pl.when(qi == 0)
+    @pl.when(pair == 0)
     def _():
         merge_halves(n_blk, half, at_a, at_b, ((qs, qa, qb), (ks, ka, kb), (vs, va, vb), (gs, ga, gb)))
         for c in range(n_blk):
@@ -125,37 +126,44 @@
         dv_scr[...] = jnp.zeros_like(dv_scr)
         bias[...] = jnp.zeros_like(bias)
 
-    def process(chunks, band_first):
-        q = qs[qi]
-        g = gs[qi]
-        n = len(chunks)
-        shift = lse[qi][0:1]
-        delta = None
+    def process(chunks, ranges, banded):
+        deltas, dq_t = [None, None], [None, None]
         for idx, c in enumerate(chunks):
-            p = jnp.exp2(masked_scores(ks[c], q, scale * LOG2_E, idx == n - 1, band_first and idx == 0) - shift)
-            p_scr[idx] = p
-            dp = dot_nt(vs[c], g).astype(jnp.bfloat16)
-            dp_scr[idx] = dp
-            delta = plus(delta, fold(p * dp.astype(jnp.float32), jnp.sum))
-            dv_scr[c] += dot_nn(p.astype(jnp.bfloat16), g)
-        delta = jnp.sum(delta, axis=0, keepdims=True)
-        dq_t = None
+            dv = None
+            for r, (lo, hi) in enumerate(ranges):
+                if lo <= idx < hi:
+                    qi = 2 * pair + r
+                    s = masked_scores(ks[c], qs[qi], scale * LOG2_E, idx == hi - 1, banded and idx == lo)
+                    p = jnp.exp2(s - lse[qi][0:1])
+                    p_scr[r, idx] = p
+                    dp = dot_nt(vs[c], gs[qi]).astype(jnp.bfloat16)
+                    dp_scr[r, idx] = dp
+                    deltas[r] = plus(deltas[r], fold(p * dp.astype(jnp.float32), jnp.sum))
+                    dv = plus(dv, dot_nn(p.astype(jnp.bfloat16), gs[qi]))
+            dv_scr[c] += dv
+        deltas = [jnp.sum(d, axis=0, keepdims=True) for d in deltas]
         for idx, c in enumerate(chunks):
-            ds = (p_scr[idx] * (dp_scr[idx].astype(jnp.float32) - delta)).astype(jnp.bfloat16)
-            dq_t = plus(dq_t, dot_nn(kt[c], ds))
-            dk_scr[c] += dot_nn(ds, q)
-        out_scr[0] = jnp.transpose(dq_t * scale).astype(jnp.bfloat16)
-
-    block_cases(n_blk, qi, kind_ref[pl.program_id(0)] == 1, process)
+            dk = None
+            for r, (lo, hi) in enumerate(ranges):
+                if lo <= idx < hi:
+                    ds = (p_scr[r, idx] * (dp_scr[r, idx].astype(jnp.float32) - deltas[r])).astype(jnp.bfloat16)
+                    dq_t[r] = plus(dq_t[r], dot_nn(kt[c], ds))
+                    dk = plus(dk, dot_nn(ds, qs[2 * pair + r]))
+            dk_scr[c] += dk
+        for r in range(2):
+            out_scr[r] = jnp.transpose(dq_t[r] * scale).astype(jnp.bfloat16)
+
+    block_cases(n_blk, pair, kind_ref[pl.program_id(0)] == 1, process)
 
     def give(part, c, slot):
         bias[part] += fold(out_scr[slot].astype(jnp.float32), jnp.sum)
         da[part, c] = out_scr[slot, pl.ds(at_a, half), :]
         db[part, c] = out_scr[slot, pl.ds(at_b, half), :]
 
-    give(0, qi, 0)
-
-    @pl.when(qi == n_blk - 1)
+    for r in range(2):
+        give(0, 2 * pair + r, r)
+
+    @pl.when(pair == n_blk // 2 - 1)
     def _():
         for c in range(n_blk):
             out_scr[0] = (dk_scr[c] * scale).astype(jnp.bfloat16)
@@ -180,7 +188,7 @@
     return pl.pallas_call(
         body,
         grid_spec=pltpu.PrefetchScalarGridSpec(
-            num_scalar_prefetch=2, grid=(heads, n_tok[0]), in_specs=in_specs, out_specs=out_specs, scratch_shapes=scratch),
+            num_scalar_prefetch=2, grid=(heads, n_tok[0] // 2), in_specs=in_specs, out_specs=out_specs, scratch_shapes=scratch),
         out_shape=out_shape,
         compiler_params=pltpu.CompilerParams(
             dimension_semantics=("arbitrary", "arbitrary"), vmem_limit_bytes=48 * 1024 * 1024),
@@ -202,7 +210,7 @@
         [part(0), part(1), part(2)] * 2, [one, one, lse],
         [jax.ShapeDtypeStruct((n_blk, half, wide), bf)] * 2 + [jax.ShapeDtypeStruct((heads, n_blk, 8, blk), jnp.float32)],
         [pltpu.VMEM((n_blk, blk, dim), bf)] * 3 + [pltpu.VMEM((n_blk, dim, blk), bf)]
-        + [pltpu.VMEM((n_blk, blk, blk), jnp.float32), pltpu.VMEM((blk, dim), bf)],
+        + [pltpu.VMEM((2, n_blk, blk, blk), jnp.float32), pltpu.VMEM((2, blk, dim), bf)],
         (n_blk, blk), 2)
 
 
@@ -219,7 +227,7 @@
         [part(0), part(1), part(2), one] * 2 + [lse], [three, three, sums],
         [jax.ShapeDtypeStruct((3, n_blk, half, wide), bf)] * 2 + [jax.ShapeDtypeStruct((heads, 3, 8, dim), jnp.float32)],
         [pltpu.VMEM((n_blk, blk, dim), bf)] * 4 + [pltpu.VMEM((n_blk, dim, blk), bf)]
-        + [pltpu.VMEM((n_blk, blk, blk), jnp.float32), pltpu.VMEM((n_blk, blk, blk), bf)]
+        + [pltpu.VMEM((2, n_blk, blk, blk), jnp.float32), pltpu.VMEM((2, n_blk, blk, blk), bf)]
         + [pltpu.VMEM((n_blk, blk, dim), jnp.float32)] * 2 + [pltpu.VMEM((2, blk, dim), bf)],
         (n_blk, blk), 5)
 
@@ -606,7 +614,7 @@
 
         d_wout = out_weight_grad(o_own, o_oth, g_b, core_arr)
         y_b = project_out(x_b, o_own, o_oth, w_out, b_out.reshape(1, d_model), core_arr)
-        d_wout, y_b, do_own, do_oth = lax.optimization_barrier((d_wout, y_b, do_own, do_oth))
+        y_b, do_own, do_oth = lax.optimization_barrier((y_b, do_own, do_oth))
         d_wout = lax.psum(d_wout, ("chip", "core"))
         y_out = lax.all_to_all(y_b.reshape(n_chip, half, d_model), "chip", 0, 0, tiled=True)
 

time: 1020 us -> 964 us (0.945)
  Pallas kernels: 812 us -> 777 us
  waiting for transfers between devices: 117 us -> 95.6 us
    pallas_call x2, Pallas kernels: 155 us -> 114 us  [attention_call(): pl.pallas_call(body, grid_spec=pltpu.PrefetchScalarGridSpec(num_scalar_pr...]
    all_to_all x1, waiting for transfers between devices: 28.7 us -> 8.11 us  [local_block(): lax.all_to_all(y_b.reshape(n_chip, half, d_model), 'chip', 0, 0, tiled=True)]
  transfers between devices with their start and end apart: 10 -> 10, of which waited for: 3 -> 3; matrix products, arithmetic and copies ran while one was open for 2% -> 2% of each run, Pallas kernels for 71% -> 74%
where the time goes in v4:
time: 964 us; the launch traced here: 959 us
  Pallas kernels  777 us (81%)
  waiting for transfers between devices  95.6 us (10%)
  starting transfers between devices  33.7 us (3%)
  other arithmetic  31.3 us (3%)
  between operations  14.6 us (2%)
    pallas_call x1, Pallas kernels, grad_sum(): pl.pallas_call(functools.partial(grad_sum_kernel, n_chip, rows), in_specs...  453 us
    pallas_call x8, Pallas kernels, matmul_call(): pl.pallas_call(body, grid_spec=pltpu.PrefetchScalarGridSpec(num_scalar_pr...  155 us
    pallas_call x2, Pallas kernels, attention_call(): pl.pallas_call(body, grid_spec=pltpu.PrefetchScalarGridSpec(num_scalar_pr...  114 us
    pallas_call x4, Pallas kernels, place(): pl.pallas_call(copy_kernel, grid=(rows // tile,), in_specs=in_specs, out_...  55.3 us
    all_to_all x1, waiting for transfers between devices, local_block(): x_b = lax.all_to_all(x, 'chip', 0, 0, tiled=True).reshape(n_tok, d_model)  51.8 us
    all_to_all x1, waiting for transfers between devices, local_block(): g_b = lax.all_to_all(d_y, 'chip', 0, 0, tiled=True).reshape(n_tok, d_model)  35.6 us
  transfers between devices with their start and end apart: 10, of which 3 were waited for; matrix products, arithmetic and copies ran while one was open for 2% of the time, Pallas kernels for 74%

profile of v4, /device:TPU:0, one launch (start us, length us, event | category | flops | bytes accessed | tf_op | source)
XLA Modules:
  0.0 959.0 jit_solution(6690875977803322855)
XLA Ops:
  7.2 6.6 all-to-all-start
  14.5 51.8 %all-to-all-done = bf16[8,128,2048]{2,1,0:T(8,128)(2,1)} async-done(((bf16[8,128,2048]{2,1,0:T(8,128)(2,1)}), bf16[8,128,2048]{2,1,0:T(8,128)(2,1)}, u32[]{:S(2)}, u32[]{:S(2)}) %all-to-all-start) | async-done | bytes 4194336 | tf_op jit(solution)/shard_map/all_to_all | solution.py:594
  73.7 4.6 add_convert_fusion.h_ref.ha
  78.3 18.0 %shard_map.153 = bf16[3,1024,1024]{2,1,0:T(8,128)(2,1)} custom-call(s32[1]{0:T(128)S(6)} %sub.20.g, bf16[1024,2048]{1,0:T(8,128)(2,1)} %add_convert_fusion.h_ref.ha, bf16[2048,6144]{1,0:T(8,128)(2,1)} %refs_5_.1, bf16[1,6144]{1,0:T(2,128)(2,1)} %reshape.141.b_ref), custom_call_target="tpu_custom_call" | custom-call | flops 12884901888 | bytes 29372416 | tf_op jit(solution)/shard_map/pallas_call | solution.py:238
  96.4 8.0 all-to-all-start.1
  104.4 18.0 %shard_map.152 = bf16[3,1024,1024]{2,1,0:T(8,128)(2,1)} custom-call(s32[1]{0:T(128)} %bitcast.g.core_ref.c, bf16[1024,2048]{1,0:T(8,128)(2,1)} %add_convert_fusion.h_ref.ha, bf16[2048,6144]{1,0:T(8,128)(2,1)} %refs_5_.1, bf16[1,6144]{1,0:T(2,128)(2,1)} %reshape.141.b_ref), custom_call_target="tpu_custom_call" | custom-call | flops 12884901888 | bytes 29372416 | tf_op jit(solution)/shard_map/pallas_call | solution.py:238
  122.4 35.6 %all-to-all-done.1 = bf16[8,128,2048]{2,1,0:T(8,128)(2,1)} async-done(((bf16[8,128,2048]{2,1,0:T(8,128)(2,1)}), bf16[8,128,2048]{2,1,0:T(8,128)(2,1)}, u32[]{:S(2)}, u32[]{:S(2)}) %all-to-all-start.1) | async-done | bytes 4194336 | tf_op jit(solution)/shard_map/all_to_all | solution.py:595
  158.0 44.1 %shard_map.154 = (bf16[8,128,1024]{2,1,0:T(8,128)(2,1)S(1)}, bf16[8,128,1024]{2,1,0:T(8,128)(2,1)S(1)}, f32[8,8,8,256]{3,2,1,0:T(8,128)S(1)}) custom-call(s32[8]{0:T(128)S(1)} %dynamic_slice.3.kind_ref, s32[1]{0:T(128)} %bitcast.g.core_ref.c, bf16[3,8,128,1024]{3,2,1,0:T(8,128)(2,1)} %bitcast.56, bf16[3,8,128,1024]{3,2,1,0:T(8,128)(2,1)} %bitcast.57, ...), custom_call_target="tpu_custom_call" | custom-call | flops 8589934592 | bytes 25165824 | tf_op jit(solution)/shard_map/pallas_call | solution.py:188
  203.5 8.6 shard_map.157
  213.2 8.6 shard_map.156
  223.2 14.1 %shard_map.155 = bf16[1024,2048]{1,0:T(8,128)(2,1)} custom-call(s32[1]{0:T(128)} %bitcast.g.core_ref.c, bf16[1024,2048]{1,0:T(8,128)(2,1)} %bitcast.1.x_ref, bf16[1024,1024]{1,0:T(8,128)(2,1)} %bitcast.52, bf16[1024,1024]{1,0:T(8,128)(2,1)} %bitcast.71, bf16[2048,2048]{1,0:T(8,128)(2,1)} %w_ref.7, bf16[2048,2048]{1,0:T(8,128)(2,1)} %w_ref.7, ...), custom_call_target="tpu_custom_call" | custom-call | flops 8589934592 | bytes 25169920 | tf_op jit(solution)/shard_map/pallas_call | solution.py:238
  237.3 69.5 %shard_map.158 = (bf16[3,8,128,1024]{3,2,1,0:T(8,128)(2,1)}, bf16[3,8,128,1024]{3,2,1,0:T(8,128)(2,1)}, f32[8,3,8,128]{3,2,1,0:T(8,128)S(1)}) custom-call(s32[8]{0:T(128)S(1)} %dynamic_slice.3.kind_ref, s32[1]{0:T(128)} %bitcast.g.core_ref.c, bf16[3,8,128,1024]{3,2,1,0:T(8,128)(2,1)} %bitcast.59, bf16[3,8,128,1024]{3,2,1,0:T(8,128)(2,1)} %bitcast.60, ...), custom_call_target="tpu_custom_call" | custom-call | flops 21474836480 | bytes 25165824 | tf_op jit(solution)/shard_map/pallas_call | solution.py:188
  306.8 7.5 all-to-all-start.2
  314.4 14.8 %shard_map.161 = f32[2048,2048]{1,0:T(8,128)} custom-call(s32[1]{0:T(128)} %bitcast.g.core_ref.c, bf16[1024,1024]{1,0:T(8,128)(2,1)} %bitcast.53, bf16[1024,1024]{1,0:T(8,128)(2,1)} %bitcast.72, bf16[1024,2048]{1,0:T(8,128)(2,1)} %bitcast.2.dy_ref), custom_call_target="tpu_custom_call" | custom-call | flops 8589934592 | bytes 8388608 | tf_op jit(solution)/shard_map/pallas_call | solution.py:238
  329.2 36.8 %shard_map.160.g_all = f32[3,2048,1024]{2,1,0:T(8,128)} custom-call(bf16[1024,2048]{1,0:T(8,128)(2,1)} %add_convert_fusion.h_ref.ha, bf16[1024,2048]{1,0:T(8,128)(2,1)} %collective-permute-done.4.hb, bf16[3,1024,1024]{2,1,0:T(8,128)(2,1)} %bitcast.63, bf16[3,1024,1024]{2,1,0:T(8,128)(2,1)} %bitcast.70), custom_call_target="tpu_custom_call" | custom-call | flops 25769803776 | bytes 20971520 | tf_op jit(solution)/shard_map/pallas_call | solution.py:238
  366.0 8.1 all-to-all-done.2
  377.9 36.3 %shard_map.159 = bf16[1024,2048]{1,0:T(8,128)(2,1)} custom-call(s32[1]{0:T(128)} %bitcast.g.core_ref.c, bf16[3,1024,1024]{2,1,0:T(8,128)(2,1)} %bitcast.64, bf16[3,1024,1024]{2,1,0:T(8,128)(2,1)} %bitcast.15.oth, bf16[2048,6144]{1,0:T(8,128)(2,1)} %refs_5_.1, bf16[2048,6144]{1,0:T(8,128)(2,1)} %refs_5_.1, bf16[2048,6144]{1,0:T(8,128)(2,1)} %refs_5_.1, ...), custom_call_target="tpu_custom_call" | custom-call | flops 25769803776 | bytes 163577856 | tf_op jit(solution)/shard_map/pallas_call | solution.py:238
  414.3 4.7 fusion.2
  419.7 6.1 fusion.6
  425.8 9.6 convert_reduce_fusion.1
  435.4 11.2 %all-to-all-start.3 = ((bf16[8,128,2048]{2,1,0:T(8,128)(2,1)}), bf16[8,128,2048]{2,1,0:T(8,128)(2,1)}, u32[]{:S(2)}, u32[]{:S(2)}) async-start(bf16[8,128,2048]{2,1,0:T(8,128)(2,1)} %bitcast.62), calls=%async_computation.3 | async-start | bytes 8388608 | tf_op jit(solution)/shard_map/all_to_all | solution.py:629
  446.5 452.7 %grad_sum.1 = (f32[2048,6144]{1,0:T(8,128)}, f32[96,128]{1,0:T(8,128)S(1)}) custom-call(f32[3,2048,1024]{2,1,0:T(8,128)} %shard_map.160.g_all, f32[96,128]{1,0:T(8,128)S(1)} %maximum_bitcast_fusion.small), custom_call_target="tpu_custom_call" | custom-call | flops 299999985664 | bytes 157286400 | tf_op jit(solution)/shard_map/grad_sum/pallas_call | solution.py:554
  899.2 36.3 %place_rows.6 = f32[2048,6144]{1,0:T(8,128)} custom-call(f32[2048,6144]{1,0:T(8,128)} %get-tuple-element.33.refs_0_), custom_call_target="tpu_custom_call" | custom-call | flops 100663296 | bytes 100663296 | tf_op jit(solution)/shard_map/place_rows/pallas_call | solution.py:384
  936.7 11.4 %place_rows.7 = f32[2048,2048]{1,0:T(8,128)} custom-call(f32[2048,2048]{1,0:T(8,128)} %all-reduce.2.cloned.1.call-done.refs_0_), custom_call_target="tpu_custom_call" | custom-call | flops 33554432 | bytes 33554432 | tf_op jit(solution)/shard_map/place_rows/pallas_call | solution.py:384
  (68 shorter events, 21.7 us)
Async XLA Ops:
  7.2 6.6 copy-start.12
  7.2 6.6 copy-start.13
  7.2 6.6 copy-start.11
  7.2 59.1 %all-to-all-start = ((bf16[8,128,2048]{2,1,0:T(8,128)(2,1)}), bf16[8,128,2048]{2,1,0:T(8,128)(2,1)}, u32[]{:S(2)}, u32[]{:S(2)}) async-start(bf16[8,128,2048]{2,1,0:T(8,128)(2,1)} %param.9), calls=%async_computation | async-start | bytes 8388608 | tf_op jit(solution)/shard_map/all_to_all | solution.py:594
  13.8 64.5 %copy-start.3 = (f32[2048]{0:T(1024)}, f32[2048]{0:T(1024)S(1)}, u32[]{:S(2)}) copy-start(f32[2048]{0:T(1024)S(1)} %convert_element_type.28) | copy-start | bytes 24580
  69.1 4.0 copy-start.5
  96.4 8.0 copy-start.16
  96.4 61.7 %collective-permute-start = (bf16[3,1024,1024]{2,1,0:T(8,128)(2,1)}, bf16[3,1024,1024]{2,1,0:T(8,128)(2,1)}, u32[]{:S(2)}, u32[]{:S(2)}) collective-permute-start(bf16[3,1024,1024]{2,1,0:T(8,128)(2,1)} %shard_map.153), channel_id=1, source_target_pairs={{0,1},{1,0},{2,3},{3,2},{4,5},{5,4},{6,7},{7,6},{8,9},{9,8},{10,11... | collective-permute-start | bytes 18874376 | tf_op jit(solution)/shard_map/ppermute | solution.py:592
  96.4 61.7 %all-to-all-start.1 = ((bf16[8,128,2048]{2,1,0:T(8,128)(2,1)}), bf16[8,128,2048]{2,1,0:T(8,128)(2,1)}, u32[]{:S(2)}, u32[]{:S(2)}) async-start(bf16[8,128,2048]{2,1,0:T(8,128)(2,1)} %param.10), calls=%async_computation.1 | async-start | bytes 8388608 | tf_op jit(solution)/shard_map/all_to_all | solution.py:595
  203.5 9.1 copy-start.14
  203.5 18.3 %collective-permute-start.1 = (bf16[8,128,1024]{2,1,0:T(8,128)(2,1)S(1)}, bf16[8,128,1024]{2,1,0:T(8,128)(2,1)S(1)}, u32[]{:S(2)}, u32[]{:S(2)}) collective-permute-start(bf16[8,128,1024]{2,1,0:T(8,128)(2,1)S(1)} %get-tuple-element.23), channel_id=1, source_target_pairs={{0,1},{1,0},{2,3},{3,2},{4,5},{5,4},{6,7},{7,6},{8,9},{9,8},{10,11... | collective-permute-start | bytes 6291464 | tf_op jit(solution)/shard_map/ppermute | solution.py:592
  212.0 25.2 %collective-permute-start.2 = (bf16[1024,1024]{1,0:T(8,128)(2,1)}, bf16[1024,1024]{1,0:T(8,128)(2,1)S(1)}, u32[]{:S(2)}, u32[]{:S(2)}) collective-permute-start(bf16[1024,1024]{1,0:T(8,128)(2,1)} %shard_map.157), channel_id=1, source_target_pairs={{0,1},{1,0},{2,3},{3,2},{4,5},{5,4},{6,7},{7,6},{8,9},{9,8},{10,11... | collective-permute-start | bytes 6291464 | tf_op jit(solution)/shard_map/ppermute | solution.py:592
  213.1 116.1 %collective-permute-start.4 = (bf16[1024,2048]{1,0:T(8,128)(2,1)}, bf16[1024,2048]{1,0:T(8,128)(2,1)}, u32[]{:S(2)}, u32[]{:S(2)}) collective-permute-start(bf16[1024,2048]{1,0:T(8,128)(2,1)} %add_convert_fusion.h_ref.ha), channel_id=1, source_target_pairs={{0,1},{1,0},{2,3},{3,2},{4,5},{5,4},{6,7},{7,6},{8,9},{9,8},{10,11... | collective-permute-start | bytes 12582920 | tf_op jit(solution)/shard_map/ppermute | solution.py:592
  221.8 1.4 copy-start.15
  223.2 14.1 %copy-start.1 = (bf16[1024,1024]{1,0:T(8,128)(2,1)S(1)}, bf16[1024,1024]{1,0:T(8,128)(2,1)}, u32[]{:S(2)}) copy-start(bf16[1024,1024]{1,0:T(8,128)(2,1)} %shard_map.156) | copy-start | bytes 6291460
  306.8 71.2 %collective-permute-start.3 = (bf16[3,8,128,1024]{3,2,1,0:T(8,128)(2,1)}, bf16[3,8,128,1024]{3,2,1,0:T(8,128)(2,1)}, u32[]{:S(2)}, u32[]{:S(2)}) collective-permute-start(bf16[3,8,128,1024]{3,2,1,0:T(8,128)(2,1)} %get-tuple-element.30), channel_id=1, source_target_pairs={{0,1},{1,0},{2,3},{3,2},{4,5},{5,4},{6,7},{7,6},{8,9},{9,8},{10,11... | collective-permute-start | bytes 18874376 | tf_op jit(solution)/shard_map/ppermute | solution.py:592
  306.8 67.4 %all-to-all-start.2 = ((bf16[8,128,2048]{2,1,0:T(8,128)(2,1)}), bf16[8,128,2048]{2,1,0:T(8,128)(2,1)}, u32[]{:S(2)}, u32[]{:S(2)}) async-start(bf16[8,128,2048]{2,1,0:T(8,128)(2,1)} %bitcast.66), calls=%async_computation.2 | async-start | bytes 8388608 | tf_op jit(solution)/shard_map/all_to_all | solution.py:619
  314.2 622.5 %all-reduce.2.cloned.1.call-start = ((), (), s32[]{:S(2)}) async-start(), calls=%async_computation.4 | async-start | bytes 33554432 | tf_op jit(solution)/shard_map/psum | solution.py:618
  377.9 36.3 %copy-start.4 = (f32[2048]{0:T(1024)S(1)}, f32[2048]{0:T(1024)}, u32[]{:S(2)}) copy-start(f32[2048]{0:T(1024)} %copy-done.3) | copy-start | bytes 24580
  377.9 36.3 %copy-start.6 = (f32[1024]{0:T(1024)S(1)}, f32[1024]{0:T(1024)}, u32[]{:S(2)}) copy-start(f32[1024]{0:T(1024)} %copy-done.5) | copy-start | bytes 12292
  414.2 4.8 copy-start.10
  414.2 5.5 copy-start.2
  414.2 5.5 copy-start.8
  435.4 512.8 %all-to-all-start.3 = ((bf16[8,128,2048]{2,1,0:T(8,128)(2,1)}), bf16[8,128,2048]{2,1,0:T(8,128)(2,1)}, u32[]{:S(2)}, u32[]{:S(2)}) async-start(bf16[8,128,2048]{2,1,0:T(8,128)(2,1)} %bitcast.62), calls=%async_computation.3 | async-start | bytes 8388608 | tf_op jit(solution)/shard_map/all_to_all | solution.py:629
  (3 other events, 2.5 us)
Sparse Core Ops, SparseCore 0:
  329.3 323.2 all-reduce.1

commit v5 on v4

--- a/solution.py
+++ b/solution.py
@@ -38,19 +38,19 @@
             dst[c, pl.ds(at_b, half), :] = src_b[c]
 
 
-def block_cases(n_blk, pair, banded, process):
-    for i in range(n_blk // 2):
-        cond = pair == i
-        if i >= 1:
-            cond = cond & jnp.logical_not(banded)
-
-        @pl.when(cond)
+def block_cases(group, banded, process):
+    for i in range(2):
+        @pl.when((group == i) & jnp.logical_not(banded))
         def _():
-            process(list(range(2 * i + 2)), ((0, 2 * i + 1), (0, 2 * i + 2)), False)
-
-    @pl.when(banded & (pair >= 1))
+            process(list(range(4 * i + 4)), [(0, 4 * i + r + 1, False) for r in range(4)])
+
+    @pl.when((group == 0) & banded)
     def _():
-        process([2 * pair - 2 + i for i in range(4)], ((0, 3), (1, 4)), True)
+        process(list(range(4)), [(0, 1, False), (0, 2, False), (0, 3, True), (1, 4, True)])
+
+    @pl.when((group == 1) & banded)
+    def _():
+        process(list(range(2, 8)), [(r, r + 3, True) for r in range(4)])
 
 
 def masked_scores(k, q, factor, last, band_first):
@@ -67,57 +67,57 @@
 
 
 def forward_kernel(n_blk, half, kind_ref, core_ref, qa, ka, va, qb, kb, vb, oa, ob, lse, qs, ks, vs, vt, s_scr, out_scr):
-    pair = pl.program_id(1)
+    group = pl.program_id(1)
     core = core_ref[0]
     factor = LOG2_E / math.sqrt(qs.shape[2])
     at_a = pl.multiple_of(core * half, half)
     at_b = pl.multiple_of((1 - core) * half, half)
 
-    @pl.when(pair == 0)
+    @pl.when(group == 0)
     def _():
         merge_halves(n_blk, half, at_a, at_b, ((qs, qa, qb), (ks, ka, kb), (vs, va, vb)))
         for c in range(n_blk):
             vt[c] = jnp.transpose(vs[c])
 
-    def process(chunks, ranges, banded):
-        tops, sums = [None, None], [None, None]
+    def process(chunks, ranges):
+        tops, sums = [None] * 4, [None] * 4
         for idx, c in enumerate(chunks):
-            for r, (lo, hi) in enumerate(ranges):
+            for r, (lo, hi, edge) in enumerate(ranges):
                 if lo <= idx < hi:
-                    s = masked_scores(ks[c], qs[2 * pair + r], factor, idx == hi - 1, banded and idx == lo)
+                    s = masked_scores(ks[c], qs[4 * group + r], factor, idx == hi - 1, edge and idx == lo)
                     s_scr[r, idx] = s
                     part = fold(s, jnp.max)
                     tops[r] = part if tops[r] is None else jnp.maximum(tops[r], part)
-        for r, (lo, hi) in enumerate(ranges):
+        for r, (lo, hi, edge) in enumerate(ranges):
             tops[r] = jnp.max(tops[r], axis=0, keepdims=True)
             for idx in range(lo, hi):
                 e = jnp.exp2(s_scr[r, idx] - tops[r])
                 s_scr[r, idx] = e
                 sums[r] = plus(sums[r], fold(e, jnp.sum))
-        for r, (lo, hi) in enumerate(ranges):
+        for r, (lo, hi, edge) in enumerate(ranges):
             total = jnp.sum(sums[r], axis=0, keepdims=True)
             inv = 1.0 / total
             o_t = None
             for idx in range(lo, hi):
                 o_t = plus(o_t, dot_nn(vt[chunks[idx]], (s_scr[r, idx] * inv).astype(jnp.bfloat16)))
             out_scr[r] = jnp.transpose(o_t).astype(jnp.bfloat16)
-            lse[2 * pair + r] = jnp.broadcast_to(tops[r] + jnp.log2(total), lse.shape[1:])
-
-    block_cases(n_blk, pair, kind_ref[pl.program_id(0)] == 1, process)
-    for r in range(2):
-        oa[2 * pair + r] = out_scr[r, pl.ds(at_a, half), :]
-        ob[2 * pair + r] = out_scr[r, pl.ds(at_b, half), :]
+            lse[4 * group + r] = jnp.broadcast_to(tops[r] + jnp.log2(total), lse.shape[1:])
+
+    block_cases(group, kind_ref[pl.program_id(0)] == 1, process)
+    for r in range(4):
+        oa[4 * group + r] = out_scr[r, pl.ds(at_a, half), :]
+        ob[4 * group + r] = out_scr[r, pl.ds(at_b, half), :]
 
 
 def backward_kernel(n_blk, half, kind_ref, core_ref, qa, ka, va, ga, qb, kb, vb, gb, lse, da, db, bias,
                     qs, ks, vs, gs, kt, p_scr, dp_scr, dk_scr, dv_scr, out_scr):
-    pair = pl.program_id(1)
+    group = pl.program_id(1)
     core = core_ref[0]
     scale = 1.0 / math.sqrt(qs.shape[2])
     at_a = pl.multiple_of(core * half, half)
     at_b = pl.multiple_of((1 - core) * half, half)
 
-    @pl.when(pair == 0)
+    @pl.when(group == 0)
     def _():
         merge_halves(n_blk, half, at_a, at_b, ((qs, qa, qb), (ks, ka, kb), (vs, va, vb), (gs, ga, gb)))
         for c in range(n_blk):
@@ -126,14 +126,14 @@
         dv_scr[...] = jnp.zeros_like(dv_scr)
         bias[...] = jnp.zeros_like(bias)
 
-    def process(chunks, ranges, banded):
-        deltas, dq_t = [None, None], [None, None]
+    def process(chunks, ranges):
+        deltas, dq_t = [None] * 4, [None] * 4
         for idx, c in enumerate(chunks):
             dv = None
-            for r, (lo, hi) in enumerate(ranges):
+            for r, (lo, hi, edge) in enumerate(ranges):
                 if lo <= idx < hi:
-                    qi = 2 * pair + r
-                    s = masked_scores(ks[c], qs[qi], scale * LOG2_E, idx == hi - 1, banded and idx == lo)
+                    qi = 4 * group + r
+                    s = masked_scores(ks[c], qs[qi], scale * LOG2_E, idx == hi - 1, edge and idx == lo)
                     p = jnp.exp2(s - lse[qi][0:1])
                     p_scr[r, idx] = p
                     dp = dot_nt(vs[c], gs[qi]).astype(jnp.bfloat16)
@@ -144,26 +144,26 @@
         deltas = [jnp.sum(d, axis=0, keepdims=True) for d in deltas]
         for idx, c in enumerate(chunks):
             dk = None
-            for r, (lo, hi) in enumerate(ranges):
+            for r, (lo, hi, edge) in enumerate(ranges):
                 if lo <= idx < hi:
                     ds = (p_scr[r, idx] * (dp_scr[r, idx].astype(jnp.float32) - deltas[r])).astype(jnp.bfloat16)
                     dq_t[r] = plus(dq_t[r], dot_nn(kt[c], ds))
-                    dk = plus(dk, dot_nn(ds, qs[2 * pair + r]))
+                    dk = plus(dk, dot_nn(ds, qs[4 * group + r]))
             dk_scr[c] += dk
-        for r in range(2):
+        for r in range(4):
             out_scr[r] = jnp.transpose(dq_t[r] * scale).astype(jnp.bfloat16)
 
-    block_cases(n_blk, pair, kind_ref[pl.program_id(0)] == 1, process)
+    block_cases(group, kind_ref[pl.program_id(0)] == 1, process)
 
     def give(part, c, slot):
         bias[part] += fold(out_scr[slot].astype(jnp.float32), jnp.sum)
         da[part, c] = out_scr[slot, pl.ds(at_a, half), :]
         db[part, c] = out_scr[slot, pl.ds(at_b, half), :]
 
-    for r in range(2):
-        give(0, 2 * pair + r, r)
-
-    @pl.when(pair == n_blk // 2 - 1)
+    for r in range(4):
+        give(0, 4 * group + r, r)
+
+    @pl.when(group == 1)
     def _():
         for c in range(n_blk):
             out_scr[0] = (dk_scr[c] * scale).astype(jnp.bfloat16)
@@ -188,7 +188,7 @@
     return pl.pallas_call(
         body,
         grid_spec=pltpu.PrefetchScalarGridSpec(
-            num_scalar_prefetch=2, grid=(heads, n_tok[0] // 2), in_specs=in_specs, out_specs=out_specs, scratch_shapes=scratch),
+            num_scalar_prefetch=2, grid=(heads, 2), in_specs=in_specs, out_specs=out_specs, scratch_shapes=scratch),
         out_shape=out_shape,
         compiler_params=pltpu.CompilerParams(
             dimension_semantics=("arbitrary", "arbitrary"), vmem_limit_bytes=48 * 1024 * 1024),
@@ -210,7 +210,7 @@
         [part(0), part(1), part(2)] * 2, [one, one, lse],
         [jax.ShapeDtypeStruct((n_blk, half, wide), bf)] * 2 + [jax.ShapeDtypeStruct((heads, n_blk, 8, blk), jnp.float32)],
         [pltpu.VMEM((n_blk, blk, dim), bf)] * 3 + [pltpu.VMEM((n_blk, dim, blk), bf)]
-        + [pltpu.VMEM((2, n_blk, blk, blk), jnp.float32), pltpu.VMEM((2, blk, dim), bf)],
+        + [pltpu.VMEM((4, n_blk, blk, blk), jnp.float32), pltpu.VMEM((4, blk, dim), bf)],
         (n_blk, blk), 2)
 
 
@@ -227,8 +227,8 @@
         [part(0), part(1), part(2), one] * 2 + [lse], [three, three, sums],
         [jax.ShapeDtypeStruct((3, n_blk, half, wide), bf)] * 2 + [jax.ShapeDtypeStruct((heads, 3, 8, dim), jnp.float32)],
         [pltpu.VMEM((n_blk, blk, dim), bf)] * 4 + [pltpu.VMEM((n_blk, dim, blk), bf)]
-        + [pltpu.VMEM((2, n_blk, blk, blk), jnp.float32), pltpu.VMEM((2, n_blk, blk, blk), bf)]
-        + [pltpu.VMEM((n_blk, blk, dim), jnp.float32)] * 2 + [pltpu.VMEM((2, blk, dim), bf)],
+        + [pltpu.VMEM((4, n_blk, blk, blk), jnp.float32), pltpu.VMEM((4, n_blk, blk, blk), bf)]
+        + [pltpu.VMEM((n_blk, blk, dim), jnp.float32)] * 2 + [pltpu.VMEM((4, blk, dim), bf)],
         (n_blk, blk), 5)
 
 
@@ -608,7 +608,8 @@
         o_own, o_send, lse = attention_forward(my_kinds, core_arr, qkv_own, qkv_oth)
         o_oth = swap(o_send).reshape(n_tok, wide)
         o_own = o_own.reshape(n_tok, wide)
-        do_oth = swap(project_do(g_b, w_out, other_arr)).reshape(blocks[1:])
+        do_send = project_do(g_b, w_out, other_arr)
+        do_oth = swap(do_send).reshape(blocks[1:])
         do_own = project_do(g_b, w_out, core_arr).reshape(blocks[1:])
         h_oth = swap(h_norm)
 

time: 964 us -> 947 us (0.982)
  Pallas kernels: 777 us -> 760 us
    pallas_call x2, Pallas kernels: 114 us -> 96.9 us  [attention_call(): pl.pallas_call(body, grid_spec=pltpu.PrefetchScalarGridSpec(num_scalar_pr...]
  transfers between devices with their start and end apart: 10 -> 10, of which waited for: 3 -> 3; matrix products, arithmetic and copies ran while one was open for 2% -> 2% of each run, Pallas kernels for 74% -> 75%
where the time goes in v5:
time: 947 us; the launch traced here: 942 us
  Pallas kernels  760 us (80%)
  waiting for transfers between devices  95.9 us (10%)
  starting transfers between devices  33.5 us (4%)
  other arithmetic  31.4 us (3%)
  between operations  14.6 us (2%)
    pallas_call x1, Pallas kernels, grad_sum(): pl.pallas_call(functools.partial(grad_sum_kernel, n_chip, rows), in_specs...  453 us
    pallas_call x8, Pallas kernels, matmul_call(): pl.pallas_call(body, grid_spec=pltpu.PrefetchScalarGridSpec(num_scalar_pr...  155 us
    pallas_call x2, Pallas kernels, attention_call(): pl.pallas_call(body, grid_spec=pltpu.PrefetchScalarGridSpec(num_scalar_pr...  96.9 us
    pallas_call x4, Pallas kernels, place(): pl.pallas_call(copy_kernel, grid=(rows // tile,), in_specs=in_specs, out_...  55.2 us
    all_to_all x1, waiting for transfers between devices, local_block(): x_b = lax.all_to_all(x, 'chip', 0, 0, tiled=True).reshape(n_tok, d_model)  51.8 us
    all_to_all x1, waiting for transfers between devices, local_block(): g_b = lax.all_to_all(d_y, 'chip', 0, 0, tiled=True).reshape(n_tok, d_model)  35.6 us
  transfers between devices with their start and end apart: 10, of which 3 were waited for; matrix products, arithmetic and copies ran while one was open for 2% of the time, Pallas kernels for 75%

profile of v5, /device:TPU:0, one launch (start us, length us, event | category | flops | bytes accessed | tf_op | source)
XLA Modules:
  0.0 942.4 jit_solution(12130300396876841858)
XLA Ops:
  7.2 6.6 all-to-all-start
  14.5 51.8 %all-to-all-done = bf16[8,128,2048]{2,1,0:T(8,128)(2,1)} async-done(((bf16[8,128,2048]{2,1,0:T(8,128)(2,1)}), bf16[8,128,2048]{2,1,0:T(8,128)(2,1)}, u32[]{:S(2)}, u32[]{:S(2)}) %all-to-all-start) | async-done | bytes 4194336 | tf_op jit(solution)/shard_map/all_to_all | solution.py:594
  73.7 4.6 add_convert_fusion.h_ref.ha
  78.3 18.0 %shard_map.153 = bf16[3,1024,1024]{2,1,0:T(8,128)(2,1)} custom-call(s32[1]{0:T(128)S(6)} %sub.20.g, bf16[1024,2048]{1,0:T(8,128)(2,1)} %add_convert_fusion.h_ref.ha, bf16[2048,6144]{1,0:T(8,128)(2,1)} %refs_5_.1, bf16[1,6144]{1,0:T(2,128)(2,1)} %reshape.141.b_ref), custom_call_target="tpu_custom_call" | custom-call | flops 12884901888 | bytes 29372416 | tf_op jit(solution)/shard_map/pallas_call | solution.py:238
  96.4 8.0 all-to-all-start.1
  104.4 18.0 %shard_map.152 = bf16[3,1024,1024]{2,1,0:T(8,128)(2,1)} custom-call(s32[1]{0:T(128)} %bitcast.g.core_ref.c, bf16[1024,2048]{1,0:T(8,128)(2,1)} %add_convert_fusion.h_ref.ha, bf16[2048,6144]{1,0:T(8,128)(2,1)} %refs_5_.1, bf16[1,6144]{1,0:T(2,128)(2,1)} %reshape.141.b_ref), custom_call_target="tpu_custom_call" | custom-call | flops 12884901888 | bytes 29372416 | tf_op jit(solution)/shard_map/pallas_call | solution.py:238
  122.4 35.6 %all-to-all-done.1 = bf16[8,128,2048]{2,1,0:T(8,128)(2,1)} async-done(((bf16[8,128,2048]{2,1,0:T(8,128)(2,1)}), bf16[8,128,2048]{2,1,0:T(8,128)(2,1)}, u32[]{:S(2)}, u32[]{:S(2)}) %all-to-all-start.1) | async-done | bytes 4194336 | tf_op jit(solution)/shard_map/all_to_all | solution.py:595
  158.0 35.3 %shard_map.154 = (bf16[8,128,1024]{2,1,0:T(8,128)(2,1)S(1)}, bf16[8,128,1024]{2,1,0:T(8,128)(2,1)S(1)}, f32[8,8,8,256]{3,2,1,0:T(8,128)S(1)}) custom-call(s32[8]{0:T(128)S(1)} %dynamic_slice.3.kind_ref, s32[1]{0:T(128)} %bitcast.g.core_ref.c, bf16[3,8,128,1024]{3,2,1,0:T(8,128)(2,1)} %bitcast.56, bf16[3,8,128,1024]{3,2,1,0:T(8,128)(2,1)} %bitcast.57, ...), custom_call_target="tpu_custom_call" | custom-call | flops 8589934592 | bytes 25165824 | tf_op jit(solution)/shard_map/pallas_call | solution.py:188
  194.7 8.6 shard_map.157
  204.4 8.6 shard_map.156
  214.4 14.1 %shard_map.155 = bf16[1024,2048]{1,0:T(8,128)(2,1)} custom-call(s32[1]{0:T(128)} %bitcast.g.core_ref.c, bf16[1024,2048]{1,0:T(8,128)(2,1)} %bitcast.1.x_ref, bf16[1024,1024]{1,0:T(8,128)(2,1)} %bitcast.52, bf16[1024,1024]{1,0:T(8,128)(2,1)} %bitcast.71, bf16[2048,2048]{1,0:T(8,128)(2,1)} %w_ref.7, bf16[2048,2048]{1,0:T(8,128)(2,1)} %w_ref.7, ...), custom_call_target="tpu_custom_call" | custom-call | flops 8589934592 | bytes 25169920 | tf_op jit(solution)/shard_map/pallas_call | solution.py:238
  228.5 61.6 %shard_map.158 = (bf16[3,8,128,1024]{3,2,1,0:T(8,128)(2,1)}, bf16[3,8,128,1024]{3,2,1,0:T(8,128)(2,1)}, f32[8,3,8,128]{3,2,1,0:T(8,128)S(1)}) custom-call(s32[8]{0:T(128)S(1)} %dynamic_slice.3.kind_ref, s32[1]{0:T(128)} %bitcast.g.core_ref.c, bf16[3,8,128,1024]{3,2,1,0:T(8,128)(2,1)} %bitcast.59, bf16[3,8,128,1024]{3,2,1,0:T(8,128)(2,1)} %bitcast.60, ...), custom_call_target="tpu_custom_call" | custom-call | flops 21474836480 | bytes 25165824 | tf_op jit(solution)/shard_map/pallas_call | solution.py:188
  290.1 7.4 all-to-all-start.2
  297.8 14.5 %shard_map.161 = f32[2048,2048]{1,0:T(8,128)} custom-call(s32[1]{0:T(128)} %bitcast.g.core_ref.c, bf16[1024,1024]{1,0:T(8,128)(2,1)} %bitcast.53, bf16[1024,1024]{1,0:T(8,128)(2,1)} %bitcast.72, bf16[1024,2048]{1,0:T(8,128)(2,1)} %bitcast.2.dy_ref), custom_call_target="tpu_custom_call" | custom-call | flops 8589934592 | bytes 8388608 | tf_op jit(solution)/shard_map/pallas_call | solution.py:238
  312.3 36.8 %shard_map.160.g_all = f32[3,2048,1024]{2,1,0:T(8,128)} custom-call(bf16[1024,2048]{1,0:T(8,128)(2,1)} %add_convert_fusion.h_ref.ha, bf16[1024,2048]{1,0:T(8,128)(2,1)} %collective-permute-done.4.hb, bf16[3,1024,1024]{2,1,0:T(8,128)(2,1)} %bitcast.63, bf16[3,1024,1024]{2,1,0:T(8,128)(2,1)} %bitcast.70), custom_call_target="tpu_custom_call" | custom-call | flops 25769803776 | bytes 20971520 | tf_op jit(solution)/shard_map/pallas_call | solution.py:238
  349.2 8.4 all-to-all-done.2
  361.4 36.3 %shard_map.159 = bf16[1024,2048]{1,0:T(8,128)(2,1)} custom-call(s32[1]{0:T(128)} %bitcast.g.core_ref.c, bf16[3,1024,1024]{2,1,0:T(8,128)(2,1)} %bitcast.64, bf16[3,1024,1024]{2,1,0:T(8,128)(2,1)} %bitcast.15.oth, bf16[2048,6144]{1,0:T(8,128)(2,1)} %refs_5_.1, bf16[2048,6144]{1,0:T(8,128)(2,1)} %refs_5_.1, bf16[2048,6144]{1,0:T(8,128)(2,1)} %refs_5_.1, ...), custom_call_target="tpu_custom_call" | custom-call | flops 25769803776 | bytes 163577856 | tf_op jit(solution)/shard_map/pallas_call | solution.py:238
  397.7 4.7 fusion.2
  403.2 6.1 fusion.6
  409.3 9.6 %convert_reduce_fusion.1 = (f32[2048]{0:T(1024)S(1)}, bf16[1024,2048]{1,0:T(8,128)(2,1)}) fusion(bf16[1024,2048]{1,0:T(8,128)(2,1)} %bitcast.2.dy_ref, f32[1024]{0:T(1024)S(1)} %negate_multiply_fusion, f32[1024]{0:T(1024)S(1)} %fusion.11, f32[1024]{0:T(1024)S(1)} %copy-done.6, bf16[8,128,2048]{2,1,0:T(8,128)(2,1)} %all-to-all-done, f32[1024]{0:T(1024)S(1)} %copy-done.8, ...), kind=kLoop, calls=%fused_computation.4 | loop fusion | flops 27260928 | bytes 16809984 | tf_op jit(solution)/shard_map/reduce_sum | solution.py:633
  418.9 10.9 %all-to-all-start.3 = ((bf16[8,128,2048]{2,1,0:T(8,128)(2,1)}), bf16[8,128,2048]{2,1,0:T(8,128)(2,1)}, u32[]{:S(2)}, u32[]{:S(2)}) async-start(bf16[8,128,2048]{2,1,0:T(8,128)(2,1)} %bitcast.62), calls=%async_computation.3 | async-start | bytes 8388608 | tf_op jit(solution)/shard_map/all_to_all | solution.py:630
  429.8 452.8 %grad_sum.1 = (f32[2048,6144]{1,0:T(8,128)}, f32[96,128]{1,0:T(8,128)S(1)}) custom-call(f32[3,2048,1024]{2,1,0:T(8,128)} %shard_map.160.g_all, f32[96,128]{1,0:T(8,128)S(1)} %maximum_bitcast_fusion.small), custom_call_target="tpu_custom_call" | custom-call | flops 299999985664 | bytes 157286400 | tf_op jit(solution)/shard_map/grad_sum/pallas_call | solution.py:554
  882.6 36.3 %place_rows.6 = f32[2048,6144]{1,0:T(8,128)} custom-call(f32[2048,6144]{1,0:T(8,128)} %get-tuple-element.33.refs_0_), custom_call_target="tpu_custom_call" | custom-call | flops 100663296 | bytes 100663296 | tf_op jit(solution)/shard_map/place_rows/pallas_call | solution.py:384
  920.1 11.4 %place_rows.7 = f32[2048,2048]{1,0:T(8,128)} custom-call(f32[2048,2048]{1,0:T(8,128)} %all-reduce.2.cloned.1.call-done.refs_0_), custom_call_target="tpu_custom_call" | custom-call | flops 33554432 | bytes 33554432 | tf_op jit(solution)/shard_map/place_rows/pallas_call | solution.py:384
  (68 shorter events, 21.7 us)
Async XLA Ops:
  7.2 6.6 copy-start.12
  7.2 6.6 copy-start.13
  7.2 6.6 copy-start.11
  7.2 59.1 %all-to-all-start = ((bf16[8,128,2048]{2,1,0:T(8,128)(2,1)}), bf16[8,128,2048]{2,1,0:T(8,128)(2,1)}, u32[]{:S(2)}, u32[]{:S(2)}) async-start(bf16[8,128,2048]{2,1,0:T(8,128)(2,1)} %param.9), calls=%async_computation | async-start | bytes 8388608 | tf_op jit(solution)/shard_map/all_to_all | solution.py:594
  13.8 64.5 %copy-start.3 = (f32[2048]{0:T(1024)}, f32[2048]{0:T(1024)S(1)}, u32[]{:S(2)}) copy-start(f32[2048]{0:T(1024)S(1)} %convert_element_type.28) | copy-start | bytes 24580
  69.1 4.0 copy-start.5
  96.4 8.0 copy-start.16
  96.4 61.7 %collective-permute-start = (bf16[3,1024,1024]{2,1,0:T(8,128)(2,1)}, bf16[3,1024,1024]{2,1,0:T(8,128)(2,1)}, u32[]{:S(2)}, u32[]{:S(2)}) collective-permute-start(bf16[3,1024,1024]{2,1,0:T(8,128)(2,1)} %shard_map.153), channel_id=1, source_target_pairs={{0,1},{1,0},{2,3},{3,2},{4,5},{5,4},{6,7},{7,6},{8,9},{9,8},{10,11... | collective-permute-start | bytes 18874376 | tf_op jit(solution)/shard_map/ppermute | solution.py:592
  96.4 61.7 %all-to-all-start.1 = ((bf16[8,128,2048]{2,1,0:T(8,128)(2,1)}), bf16[8,128,2048]{2,1,0:T(8,128)(2,1)}, u32[]{:S(2)}, u32[]{:S(2)}) async-start(bf16[8,128,2048]{2,1,0:T(8,128)(2,1)} %param.10), calls=%async_computation.1 | async-start | bytes 8388608 | tf_op jit(solution)/shard_map/all_to_all | solution.py:595
  194.7 9.1 copy-start.14
  194.7 18.3 %collective-permute-start.1 = (bf16[8,128,1024]{2,1,0:T(8,128)(2,1)S(1)}, bf16[8,128,1024]{2,1,0:T(8,128)(2,1)S(1)}, u32[]{:S(2)}, u32[]{:S(2)}) collective-permute-start(bf16[8,128,1024]{2,1,0:T(8,128)(2,1)S(1)} %get-tuple-element.23), channel_id=1, source_target_pairs={{0,1},{1,0},{2,3},{3,2},{4,5},{5,4},{6,7},{7,6},{8,9},{9,8},{10,11... | collective-permute-start | bytes 6291464 | tf_op jit(solution)/shard_map/ppermute | solution.py:592
  203.3 25.2 %collective-permute-start.2 = (bf16[1024,1024]{1,0:T(8,128)(2,1)}, bf16[1024,1024]{1,0:T(8,128)(2,1)S(1)}, u32[]{:S(2)}, u32[]{:S(2)}) collective-permute-start(bf16[1024,1024]{1,0:T(8,128)(2,1)} %shard_map.157), channel_id=1, source_target_pairs={{0,1},{1,0},{2,3},{3,2},{4,5},{5,4},{6,7},{7,6},{8,9},{9,8},{10,11... | collective-permute-start | bytes 6291464 | tf_op jit(solution)/shard_map/ppermute | solution.py:592
  204.4 108.0 %collective-permute-start.4 = (bf16[1024,2048]{1,0:T(8,128)(2,1)}, bf16[1024,2048]{1,0:T(8,128)(2,1)}, u32[]{:S(2)}, u32[]{:S(2)}) collective-permute-start(bf16[1024,2048]{1,0:T(8,128)(2,1)} %add_convert_fusion.h_ref.ha), channel_id=1, source_target_pairs={{0,1},{1,0},{2,3},{3,2},{4,5},{5,4},{6,7},{7,6},{8,9},{9,8},{10,11... | collective-permute-start | bytes 12582920 | tf_op jit(solution)/shard_map/ppermute | solution.py:592
  213.0 1.4 copy-start.15
  214.4 14.1 %copy-start.1 = (bf16[1024,1024]{1,0:T(8,128)(2,1)S(1)}, bf16[1024,1024]{1,0:T(8,128)(2,1)}, u32[]{:S(2)}) copy-start(bf16[1024,1024]{1,0:T(8,128)(2,1)} %shard_map.156) | copy-start | bytes 6291460
  290.1 71.3 %collective-permute-start.3 = (bf16[3,8,128,1024]{3,2,1,0:T(8,128)(2,1)}, bf16[3,8,128,1024]{3,2,1,0:T(8,128)(2,1)}, u32[]{:S(2)}, u32[]{:S(2)}) collective-permute-start(bf16[3,8,128,1024]{3,2,1,0:T(8,128)(2,1)} %get-tuple-element.30), channel_id=1, source_target_pairs={{0,1},{1,0},{2,3},{3,2},{4,5},{5,4},{6,7},{7,6},{8,9},{9,8},{10,11... | collective-permute-start | bytes 18874376 | tf_op jit(solution)/shard_map/ppermute | solution.py:592
  290.1 67.4 %all-to-all-start.2 = ((bf16[8,128,2048]{2,1,0:T(8,128)(2,1)}), bf16[8,128,2048]{2,1,0:T(8,128)(2,1)}, u32[]{:S(2)}, u32[]{:S(2)}) async-start(bf16[8,128,2048]{2,1,0:T(8,128)(2,1)} %bitcast.66), calls=%async_computation.2 | async-start | bytes 8388608 | tf_op jit(solution)/shard_map/all_to_all | solution.py:620
  297.6 622.5 %all-reduce.2.cloned.1.call-start = ((), (), s32[]{:S(2)}) async-start(), calls=%async_computation.4 | async-start | bytes 33554432 | tf_op jit(solution)/shard_map/psum | solution.py:619
  361.3 36.3 %copy-start.4 = (f32[2048]{0:T(1024)S(1)}, f32[2048]{0:T(1024)}, u32[]{:S(2)}) copy-start(f32[2048]{0:T(1024)} %copy-done.3) | copy-start | bytes 24580
  361.3 36.3 %copy-start.6 = (f32[1024]{0:T(1024)S(1)}, f32[1024]{0:T(1024)}, u32[]{:S(2)}) copy-start(f32[1024]{0:T(1024)} %copy-done.5) | copy-start | bytes 12292
  397.7 4.8 copy-start.10
  397.7 5.5 copy-start.2
  397.7 5.5 copy-start.8
  418.9 512.7 %all-to-all-start.3 = ((bf16[8,128,2048]{2,1,0:T(8,128)(2,1)}), bf16[8,128,2048]{2,1,0:T(8,128)(2,1)}, u32[]{:S(2)}, u32[]{:S(2)}) async-start(bf16[8,128,2048]{2,1,0:T(8,128)(2,1)} %bitcast.62), calls=%async_computation.3 | async-start | bytes 8388608 | tf_op jit(solution)/shard_map/all_to_all | solution.py:630
  (3 other events, 2.5 us)
Sparse Core Ops, SparseCore 0:
  312.5 323.4 all-reduce.1
